TPU v7x, 256 devices: a whole 4x4x8 slice. The times are simulated.
256 devices in a mesh: row: 16 (over x, y), col: 16 (over z, core).
Axes of the slice: x: 4, y: 4, z: 8, core: 2. Of those that a mesh axis runs over, the one named last changes fastest.
Arguments:
- points: bfloat16 [40960, 64], P(('row', 'col')), may hold values from -5 to 5
- start_vectors: bfloat16 [40960, 32], P(('row', 'col')), may hold values from -12 to 12
Outputs:
- basis: float32 [40960, 32], P(('row', 'col'))
All inputs are finite; a program needn't handle non-finite values.
Results may differ from a plain program's by a relative error of at most 0.007.
Values may be sent and summed in bfloat16 or wider, within the bound.
No kernel may reach another device: no remote copies, remote signals or barrier semaphores. Data moves between devices by JAX's collectives and lax.ppermute only.
A program may use at most 64 MiB of HBM per device.

v0:
```python
import functools

import jax
import jax.numpy as jnp
from jax import lax
from jax.sharding import Mesh
from jax.sharding import PartitionSpec as P

ITERS = 2
ROW = ("row_0", "row_1")
ROW_COL = ("row_0", "row_1", "col")


KERNEL_SCALE = 5.12


def one_axis_at_a_time(shard, axes):
    return functools.reduce(lax.psum, axes, shard)


def in_order(pieces, dim):
    dims = list(pieces.shape[1:])
    dims[dim] *= pieces.shape[0]
    return jnp.moveaxis(pieces, 0, dim).reshape(dims)


def sent_to_all(shard, axis):
    size = lax.axis_size(axis)
    return lax.all_to_all(
        jnp.broadcast_to(shard[None], (size, *shard.shape)), axis, 0, 0, tiled=True
    )


def gather_directly(shard, axis, dim):
    return in_order(sent_to_all(shard, axis), dim)


def gathered_total(shard, axis):
    pieces = lax.all_gather(shard, axis)
    return pieces.sum(axis=0)


def squared_norms(values):
    return jnp.sum(jnp.square(values.astype(jnp.float32)), axis=1)


def affinity(block_pts, block_sq, col_pts, col_sq):
    features = block_pts.shape[1]
    cross = lax.dot_general(
        block_pts, col_pts, (((1,), (1,)), ((), ())), preferred_element_type=jnp.float32
    )
    dist = block_sq[:, None] + col_sq[None, :] - 2.0 * cross
    return jnp.exp(dist * (-KERNEL_SCALE / features)).astype(jnp.bfloat16)


def sweep(row_pts, row_sq, col_pts, col_sq, panel, with_degree):
    rows, features = row_pts.shape
    height = min(512, rows)
    count = rows // height
    stacked = (row_pts.reshape(count, height, features), row_sq.reshape(count, height))

    def one_block(item):
        weights = affinity(item[0], item[1], col_pts, col_sq)
        results = ()
        if panel is not None:
            results = results + (jnp.dot(weights, panel, preferred_element_type=jnp.float32),)
        if with_degree:
            results = results + (jnp.sum(weights, axis=1, dtype=jnp.float32),)
        return results

    mapped = lax.map(one_block, stacked)
    return [piece.reshape((rows,) + piece.shape[2:]) for piece in mapped]


def orthonormal(product, degree, total, group, offset):
    scaled = product / degree[:, None]
    gram_part = jnp.dot(scaled.T, scaled, preferred_element_type=jnp.float32)
    gram = one_axis_at_a_time(gram_part, ROW)
    mine = lax.dynamic_slice_in_dim(scaled, offset, group, 0)
    lower = jnp.linalg.cholesky(gram / total)
    return lax.linalg.triangular_solve(lower, mine, left_side=False, lower=True, transpose_a=True)


def shards(points, start_vectors):
    group = points.shape[0]
    total = group * lax.axis_size(ROW) * lax.axis_size("col")
    offset = lax.axis_index("col") * group
    row_pts = gather_directly(points, "col", 0)
    col_pts = gather_directly(points, ROW, 0)
    row_sq = squared_norms(row_pts)
    col_sq = squared_norms(col_pts)
    degree_part = sweep(row_pts, row_sq, col_pts, col_sq, None, True)[0]
    vectors = start_vectors
    ortho = jnp.zeros(start_vectors.shape, jnp.float32)
    degree = None
    for step in range(ITERS):
        panel = gather_directly(vectors, ROW, 0)
        if step == 0:
            product_part = sweep(row_pts, row_sq, col_pts, col_sq, panel, False)[0]
            product, degree = (
                gathered_total(product_part, "col"),
                gathered_total(degree_part, "col"),
            )
        else:
            product_part = sweep(row_pts, row_sq, col_pts, col_sq, panel, False)[0]
            product = gathered_total(product_part, "col")
        ortho = orthonormal(product, degree, total, group, offset)
        vectors = ortho.astype(jnp.bfloat16)
    return ortho


def solution(mesh):
    finer = Mesh(mesh.devices.reshape(4, 4, mesh.shape["col"]), ("row_0", "row_1", "col"))
    in_specs = (P(ROW_COL, None), P(ROW_COL, None))
    out_specs = P(ROW_COL, None)
    return jax.shard_map(
        shards, mesh=finer, in_specs=in_specs, out_specs=out_specs, check_vma=False
    )
```

profile of v0, /device:TPU:32, one launch (start us, length us, event | category | flops | bytes accessed | tf_op | source)
XLA Modules:
  0.0 276.3 jit_solution(24421918623637520)
XLA Ops:
  7.3 15.3 %all_to_all.20 = bf16[16,160,32]{1,2,0:T(8,128)(2,1)S(1)} all-to-all(bf16[16,160,32]{1,2,0:T(8,128)(2,1)S(1)} %broadcast_in_dim.21), channel_id=1, replica_groups=mesh['row_0'=4,'row_1'=4,'col'=16] {'row_0','row_1'}, dimensions={0} | all-to-all | bytes 327680 | tf_op jit(solution)/shard_map/all_to_all | solution.py:29
  24.2 14.0 %all_to_all.21 = bf16[16,160,64]{1,2,0:T(8,128)(2,1)S(1)} all-to-all(bf16[16,160,64]{1,2,0:T(8,128)(2,1)} %broadcast_in_dim.20), channel_id=1, replica_groups=mesh['row_0'=4,'row_1'=4,'col'=16] {'row_0','row_1'}, dimensions={0} | all-to-all | bytes 655360 | tf_op jit(solution)/shard_map/all_to_all | solution.py:29
  38.2 8.6 %all-to-all-start = ((bf16[16,160,64]{1,2,0:T(8,128)(2,1)}), bf16[16,160,64]{1,2,0:T(8,128)(2,1)S(1)}, u32[]{:S(2)}, u32[]{:S(2)}) async-start(bf16[16,160,64]{1,2,0:T(8,128)(2,1)} %broadcast_in_dim.20), calls=%async_computation | async-start | bytes 1048576 | tf_op jit(solution)/shard_map/all_to_all | solution.py:29
  47.7 13.3 %all-to-all-done = bf16[16,160,64]{1,2,0:T(8,128)(2,1)S(1)} async-done(((bf16[16,160,64]{1,2,0:T(8,128)(2,1)}), bf16[16,160,64]{1,2,0:T(8,128)(2,1)S(1)}, u32[]{:S(2)}, u32[]{:S(2)}) %all-to-all-start) | async-done | bytes 327712 | tf_op jit(solution)/shard_map/all_to_all | solution.py:29
  61.7 13.0 %while.30 = (s32[]{:T(128)}, f32[5,512,32]{1,0,2:T(8,128)S(1)}, f32[5,512]{1,0:T(8,128)S(1)}, f32[2560]{0:T(1024)S(1)}, bf16[5,512,64]{2,1,0:T(8,128)(2,1)S(1)},...) while((s32[]{:T(128)}, f32[5,512,32]{1,0,2:T(8,128)S(1)}, ...), condition=%wide.region_3.4_spmd, body=%wide.region_2.3_spmd.sunk | while | flops 258211840 | bytes 1788009 | solution.py:71
  69.5 1.9 fusion.60
  75.6 8.0 %while.31 = (s32[]{:T(128)}, f32[5,512]{1,0:T(8,128)S(1)}, f32[5,512]{1,0:T(8,128)S(1)}, f32[2560]{0:T(1024)S(1)}, bf16[5,512,64]{2,1,0:T(8,128)(2,1)S(1)}, /*in...) while((s32[]{:T(128)}, f32[5,512]{1,0:T(8,128)S(1)}, f32[5,512]{1,0:T(8,128)S(1)}, f32[2560]{0:T(1024)S(1)}, ...), condition=%wide.region_7.8_spmd, body=%wide.region_5.7_spmd.sunk | while | flops 176946688 | bytes 811105 | solution.py:71
  83.7 16.9 %all-gather = f32[16,1,2560]{2,1,0:T(1,128)S(1)} all-gather(f32[1,1,2560]{2,1,0:T(1,128)S(1)} %reshape.48), channel_id=1, replica_groups=mesh['row_0'=4,'row_1'=4,'col'=16] {'col'}, dimensions={0}, use_global_device_ids=true | all-gather | bytes 174080 | tf_op jit(solution)/shard_map/all_gather | solution.py:39
  100.7 14.7 %all-gather.4.cloned.1.call-done = f32[16,2560,32]{1,2,0:T(8,128)} async-done(((f32[1,2560,32]{1,2,0:T(8,128)}), f32[16,2560,32]{1,2,0:T(8,128)}) %all-gather.4.cloned.1.call-update) | async-done | bytes 5242896 | tf_op jit(solution)/shard_map/all_gather | solution.py:39
  115.4 2.8 %reduce_sum.59 = f32[2560,32]{0,1:T(8,128)S(1)} reduce(f32[16,2560,32]{1,2,0:T(8,128)} %all-gather.4.cloned.1.call-done, f32[]{:T(128)} %constant.84.clone.1), dimensions={0}, to_apply=%region_4.5 | reduce | flops 1228800 | bytes 5570564 | tf_op jit(solution)/shard_map/reduce_sum | solution.py:40
  118.4 17.0 %psum.28 = f32[32,32]{0,1:T(8,128)S(1)} all-reduce(f32[32,32]{0,1:T(8,128)S(1)} %fusion.36), channel_id=1, replica_groups=mesh['row_0'=4,'row_1'=4,'col'=16] {'row_0'}, use_global_device_ids=true, to_apply=%region_9.10 | all-reduce | flops 1024 | bytes 8192 | tf_op jit(solution)/shard_map/psum | solution.py:18
  135.4 16.7 %psum.29 = f32[32,32]{0,1:T(8,128)S(1)} all-reduce(f32[32,32]{0,1:T(8,128)S(1)} %psum.28), channel_id=1, replica_groups=mesh['row_0'=4,'row_1'=4,'col'=16] {'row_1'}, use_global_device_ids=true, to_apply=%region_10.11 | all-reduce | flops 1024 | bytes 8192 | tf_op jit(solution)/shard_map/psum | solution.py:18
  152.2 2.9 %cholesky.44 = f32[32,32]{1,0:T(8,128)S(1)} custom-call(f32[32,32]{1,0:T(8,128)S(1)} %fusion.31), custom_call_target="Cholesky" | custom-call | tf_op jit(solution)/shard_map/jit(cholesky)/cholesky | solution.py:80
  156.5 2.4 custom-call.6
  159.9 3.5 %all-to-all-start.3 = ((bf16[16,160,32]{1,2,0:T(8,128)(2,1)}), bf16[16,160,32]{1,2,0:T(8,128)(2,1)S(1)}, u32[]{:S(2)}, u32[]{:S(2)}) async-start(bf16[16,160,32]{1,2,0:T(8,128)(2,1)} %broadcast_in_dim.26), calls=%async_computation.3 | async-start | bytes 524288 | tf_op jit(solution)/shard_map/all_to_all | solution.py:29
  163.5 8.4 %all-to-all-done.3 = bf16[16,160,32]{1,2,0:T(8,128)(2,1)S(1)} async-done(((bf16[16,160,32]{1,2,0:T(8,128)(2,1)}), bf16[16,160,32]{1,2,0:T(8,128)(2,1)S(1)}, u32[]{:S(2)}, u32[]{:S(2)}) %all-to-all-start.3) | async-done | bytes 163872 | tf_op jit(solution)/shard_map/all_to_all | solution.py:29
  172.3 13.0 %while.32 = (s32[]{:T(128)}, f32[5,512,32]{1,0,2:T(8,128)S(1)}, f32[5,512]{1,0:T(8,128)S(1)}, f32[2560]{0:T(1024)S(1)}, bf16[5,512,64]{2,1,0:T(8,128)(2,1)S(1)},...) while((s32[]{:T(128)}, f32[5,512,32]{1,0,2:T(8,128)S(1)}, ...), condition=%wide.region_14.17_spmd, body=%wide.region_13.16_spmd.sunk | while | flops 258211840 | bytes 1788009 | solution.py:71
  180.1 1.9 fusion.66
  186.2 38.9 %all-gather.6.cloned.1.call-done = f32[16,2560,32]{1,2,0:T(8,128)} async-done(((f32[1,2560,32]{1,2,0:T(8,128)}), f32[16,2560,32]{1,2,0:T(8,128)}) %all-gather.6.cloned.1.call-update) | async-done | bytes 5242896 | tf_op jit(solution)/shard_map/all_gather | solution.py:39
  225.1 2.8 %reduce_sum.61 = f32[2560,32]{0,1:T(8,128)S(1)} reduce(f32[16,2560,32]{1,2,0:T(8,128)} %all-gather.6.cloned.1.call-done, f32[]{:T(128)} %constant.84.clone.1), dimensions={0}, to_apply=%region_15.18 | reduce | flops 1228800 | bytes 5570564 | tf_op jit(solution)/shard_map/reduce_sum | solution.py:40
  228.0 16.8 %psum.30 = f32[32,32]{0,1:T(8,128)S(1)} all-reduce(f32[32,32]{0,1:T(8,128)S(1)} %fusion.37), channel_id=1, replica_groups=mesh['row_0'=4,'row_1'=4,'col'=16] {'row_0'}, use_global_device_ids=true, to_apply=%region_16.19 | all-reduce | flops 1024 | bytes 8192 | tf_op jit(solution)/shard_map/psum | solution.py:18
  244.9 16.9 %psum.31 = f32[32,32]{0,1:T(8,128)S(1)} all-reduce(f32[32,32]{0,1:T(8,128)S(1)} %psum.30), channel_id=1, replica_groups=mesh['row_0'=4,'row_1'=4,'col'=16] {'row_1'}, use_global_device_ids=true, to_apply=%region_17.20 | all-reduce | flops 1024 | bytes 8192 | tf_op jit(solution)/shard_map/psum | solution.py:18
  261.9 2.9 %cholesky.55 = f32[32,32]{1,0:T(8,128)S(1)} custom-call(f32[32,32]{1,0:T(8,128)S(1)} %fusion.29), custom_call_target="Cholesky" | custom-call | tf_op jit(solution)/shard_map/jit(cholesky)/cholesky | solution.py:80
  266.1 2.4 custom-call.7
  (93 shorter events, 41.1 us)
Async XLA Ops:
  38.2 22.8 %all-to-all-start = ((bf16[16,160,64]{1,2,0:T(8,128)(2,1)}), bf16[16,160,64]{1,2,0:T(8,128)(2,1)S(1)}, u32[]{:S(2)}, u32[]{:S(2)}) async-start(bf16[16,160,64]{1,2,0:T(8,128)(2,1)} %broadcast_in_dim.20), calls=%async_computation | async-start | bytes 1048576 | tf_op jit(solution)/shard_map/all_to_all | solution.py:29
  46.8 68.7 %all-gather.4.cloned.1.call-start = ((), (), s32[]{:S(2)}) async-start(), calls=%async_computation.4 | async-start | bytes 5570560 | tf_op jit(solution)/shard_map/all_gather | solution.py:39
  159.9 12.0 %all-to-all-start.3 = ((bf16[16,160,32]{1,2,0:T(8,128)(2,1)}), bf16[16,160,32]{1,2,0:T(8,128)(2,1)S(1)}, u32[]{:S(2)}, u32[]{:S(2)}) async-start(bf16[16,160,32]{1,2,0:T(8,128)(2,1)} %broadcast_in_dim.26), calls=%async_computation.3 | async-start | bytes 524288 | tf_op jit(solution)/shard_map/all_to_all | solution.py:29
  163.4 61.6 %all-gather.6.cloned.1.call-start = ((), (), s32[]{:S(2)}) async-start(), calls=%async_computation.5 | async-start | bytes 5570560 | tf_op jit(solution)/shard_map/all_gather | solution.py:39
Sparse Core Ops, SparseCore 0:
  75.8 39.6 all-gather.3
  186.3 38.7 all-gather.5
where the time goes:
time: 277 us; the launch traced here: 276 us
  blocking collectives  114 us (41%)
  waiting for transfers between devices  75.3 us (27%)
  matrix products  27.8 us (10%)
  other arithmetic  19.4 us (7%)
  local copies, waits for them, and re-layouts  13.8 us (5%)
  between operations  13.6 us (5%)
  starting transfers between devices  12.2 us (4%)
    psum x4, blocking collectives, one_axis_at_a_time(): return functools.reduce(lax.psum, axes, shard)  67.4 us
    all_gather x2, waiting for transfers between devices, gathered_total(): pieces = lax.all_gather(shard, axis)  53.6 us
    all_to_all x2, blocking collectives, sent_to_all(): lax.all_to_all(jnp.broadcast_to(shard[None], (size, *shard.shape)), axis,...  29.3 us
    all_to_all x2, waiting for transfers between devices, sent_to_all(): lax.all_to_all(jnp.broadcast_to(shard[None], (size, *shard.shape)), axis,...  21.7 us
    dot_general x10, matrix products, one_block(): jnp.dot(weights, panel, preferred_element_type=jnp.float32)  18.8 us
    all_gather x1, blocking collectives, gathered_total(): pieces = lax.all_gather(shard, axis)  16.9 us
    all_to_all x2, starting transfers between devices, sent_to_all(): lax.all_to_all(jnp.broadcast_to(shard[None], (size, *shard.shape)), axis,...  12.1 us
    dot_general x5, matrix products, affinity(): lax.dot_general(block_pts, col_pts, (((1,), (1,)), ((), ())), preferred_e...  7.56 us
  transfers between devices with their start and end apart: 4, of which 4 were waited for; matrix products, arithmetic and copies ran while one was open for 3% of the time, Pallas kernels for 0%

commit v1 on v0

v1 whole, which is shorter than its diff:
```python
import math

import jax
import jax.numpy as jnp
from jax import lax
from jax.experimental import pallas as pl
from jax.experimental.pallas import tpu as pltpu
from jax.sharding import PartitionSpec as P

KERNEL_SCALE = 5.12
F32 = jnp.float32
BF16 = jnp.bfloat16
HIGHEST = lax.Precision.HIGHEST
LANES = 128
SMALL = pltpu.CompilerParams(vmem_limit_bytes=32 * 1024 * 1024)
VEC, ONES, NORM, END = 64, 96, 99, 102


def lane_of(shape):
    return lax.broadcasted_iota(jnp.int32, shape, len(shape) - 1)


def roll(x, shift):
    shift %= LANES
    return pltpu.roll(x, shift, 1) if shift else x


def pieces(x):
    first = x.astype(BF16).astype(F32)
    second = (x - first).astype(BF16).astype(F32)
    return first, second, x - first - second


def widen(x):
    rows, width = x.shape
    return jnp.concatenate([x, jnp.zeros((rows, LANES - width), x.dtype)], axis=1)


def quarters_packed(x):
    n = x.shape[0] // 4
    x = jnp.where(lane_of(x.shape) < 32, x, 0.0)
    parts = [roll(x[q * n : (q + 1) * n], 32 * q) for q in range(4)]
    return (parts[0] + parts[1]) + (parts[2] + parts[3])


def quarters_unpacked(x):
    keep = lane_of(x.shape) < 32
    parts = [jnp.where(keep, roll(x, -32 * q), 0.0) for q in range(4)]
    return jnp.concatenate(parts, axis=0)


def inverse_factor(gram):
    n = gram.shape[0]
    lane = lane_of(gram.shape)
    row = lax.broadcasted_iota(jnp.int32, gram.shape, 0)
    a = jnp.where(lane < n, gram, 0.0) + jnp.where(lane == row + n, 1.0, 0.0)
    for j in range(n):
        pivot = a[j : j + 1, j : j + 1]
        scale = 1.0 / jnp.sqrt(pivot)
        top = a[j : j + 1, :] * scale
        column = jnp.where(row > j, a[:, j : j + 1] * scale, 0.0)
        a = jnp.where(row == j, top, a - column * top)
    return jnp.where(lane < n, roll(a, -n), 0.0)


def pack_body(count, log_scale):
    def body(points_ref, vectors_ref, cols_ref, rows_ref):
        pts = points_ref[...].astype(F32)
        half = pts.shape[0] // 2
        wide = widen(pts)
        norm = jnp.sum(wide * wide, axis=1, keepdims=True) * (-0.5 * log_scale)
        vec = roll(widen(vectors_ref[...].astype(F32)), VEC)
        lane = lane_of(wide.shape)
        out = jnp.where(lane < VEC, wide, vec)
        out = jnp.where((lane >= ONES) & (lane < NORM), 1.0, out)
        for i, piece in enumerate(pieces(norm)):
            out = jnp.where(lane == NORM + i, piece, out)
        out = out.astype(BF16)
        packed = (wide[:half] + roll(wide[half:], VEC)).astype(BF16)
        for i in range(count):
            cols_ref[i] = out
            rows_ref[i] = packed

    return body


def left_operand(packed, log_scale):
    raw = packed.astype(F32)
    lane = lane_of(raw.shape)
    low = lane < VEC
    scaled = raw * log_scale
    first = scaled.astype(BF16).astype(F32)
    second = scaled - first
    squares = raw * raw
    halves = []
    for side in range(2):
        mine = low if side == 0 else jnp.logical_not(low)
        norm = jnp.sum(jnp.where(mine, squares, 0.0), axis=1, keepdims=True) * (-0.5 * log_scale)
        one, two = (first, second) if side == 0 else (roll(first, VEC), roll(second, VEC))
        one = jnp.where(low, one, jnp.where((lane >= NORM) & (lane < END), 1.0, 0.0))
        for i, piece in enumerate(pieces(norm)):
            one = jnp.where(lane == ONES + i, piece, one)
        two = jnp.where(low, two, 0.0)
        halves.append(jnp.concatenate([one.astype(BF16), two.astype(BF16)], axis=1))
    return jnp.concatenate(halves, axis=0)


def first_body(count, group, log_scale):
    total = count * group
    chunk = 512

    def body(rows_ref, cols_ref, aff_ref, send_ref):
        def block(b, carry):
            left = left_operand(rows_ref[b], log_scale)
            acc = jnp.zeros((group, LANES), F32)
            for start in range(0, total, chunk):
                cols = cols_ref[start : start + chunk, :]
                power = lax.dot_general(
                    left,
                    jnp.concatenate([cols, cols], axis=1),
                    (((1,), (1,)), ((), ())),
                    preferred_element_type=F32,
                )
                weights = jnp.exp2(power).astype(BF16)
                aff_ref[b, :, start : start + chunk] = weights
                acc = acc + jnp.dot(weights, cols, preferred_element_type=F32)
            send_ref[b, 0:40, :] = quarters_packed(roll(acc, -VEC))
            lane = lane_of((8, LANES))
            degree = jnp.zeros((8, LANES), F32)
            for k in range(group // 8):
                column = acc[8 * k : 8 * k + 8, ONES : ONES + 1]
                degree = jnp.where(lane == k, column, degree)
            send_ref[b, 40:48, :] = degree
            return carry

        lax.fori_loop(0, count, block, 0)

    return body


def gram_of(x):
    return lax.dot_general(
        x, x, (((0,), (0,)), ((), ())), precision=HIGHEST, preferred_element_type=F32
    )


def scale_body(count):
    def body(recv_ref, spread_ref, degree_ref):
        total = jnp.sum(recv_ref[...], axis=0)
        degree = total[40:48]
        lane = lane_of((8, LANES))
        wide = []
        for j in range(5):
            piece = jnp.broadcast_to(degree[:, j : j + 1], (8, LANES))
            for q in range(1, 4):
                k = 5 * q + j
                piece = jnp.where(lane >= 32 * q, degree[:, k : k + 1], piece)
            wide.append(piece)
        wide = jnp.concatenate(wide, axis=0)
        degree_ref[...] = wide
        scaled = quarters_unpacked(total[0:40] / wide)
        gram = gram_of(scaled)[0:32]
        first = scaled.astype(BF16).astype(F32)
        out = first + roll(scaled - first, 32)
        one, two, three = pieces(jnp.where(lane_of(gram.shape) < 32, gram, 0.0))
        zeros = jnp.zeros((out.shape[0] - 64, LANES), F32)
        extra = jnp.concatenate([roll(one, 64) + roll(two, 96), roll(three, 64), zeros], axis=0)
        out = (out + extra).astype(BF16)
        for i in range(count):
            spread_ref[i] = out

    return body


def second_body(count, group):
    def body(aff_ref, spread_ref, send_ref):
        sums = jnp.zeros((64, LANES), F32)
        for i in range(count):
            sums = sums + spread_ref[i * group : i * group + 64, :].astype(F32)
        gram = roll(sums[0:32], -64) + roll(sums[0:32], -96) + roll(sums[32:64], -64)
        gram = quarters_packed(gram)

        def block(b, carry):
            acc = jnp.dot(aff_ref[b], spread_ref[...], preferred_element_type=F32)
            send_ref[b, 0:40, :] = quarters_packed(acc + roll(acc, -32))
            send_ref[b, 40:48, :] = gram
            return carry

        lax.fori_loop(0, count, block, 0)

    return body


def apply_inverse(x, inverse):
    inverse = jnp.concatenate([inverse, jnp.zeros((LANES - 32, LANES), F32)], axis=0)
    return lax.dot_general(
        x, inverse, (((1,), (1,)), ((), ())), precision=HIGHEST, preferred_element_type=F32
    )


def middle_body(count, points):
    def body(recv_ref, degree_ref, scaled_ref, gram_ref):
        total = jnp.sum(recv_ref[...], axis=0)
        inverse = inverse_factor(quarters_unpacked(total[40:48]) / points)
        product = quarters_unpacked(total[0:40] / degree_ref[...])
        scaled = apply_inverse(product, inverse)
        scaled_ref[...] = scaled
        gram = quarters_packed(gram_of(scaled)[0:32])
        for i in range(count):
            gram_ref[i] = gram

    return body


def again_body(count):
    def body(recv_ref, gram_ref):
        gram = jnp.sum(recv_ref[...], axis=0)
        for i in range(count):
            gram_ref[i] = gram

    return body


def last_body(points):
    def body(recv_ref, scaled_ref, out_ref):
        gram = quarters_unpacked(jnp.sum(recv_ref[...], axis=0)) / points
        out_ref[...] = apply_inverse(scaled_ref[...], inverse_factor(gram))[:, 0:32]

    return body


def shards(points, start_vectors):
    group, features = points.shape
    row, col = lax.axis_size("row"), lax.axis_size("col")
    total = group * row * col
    log_scale = 2.0 * KERNEL_SCALE / features * math.log2(math.e)
    shape = jax.ShapeDtypeStruct

    def exchange(x, axis):
        return lax.all_to_all(x, axis, 0, 0, tiled=True)

    cols, rows = pl.pallas_call(
        pack_body(row, log_scale),
        out_shape=(shape((row, group, LANES), BF16), shape((col, group // 2, LANES), BF16)),
        name="pack",
        compiler_params=SMALL,
    )(points, start_vectors)
    cols = exchange(cols, "row").reshape(row * group, LANES)
    rows = exchange(rows, "col")
    aff, send = pl.pallas_call(
        first_body(col, group, log_scale),
        out_shape=(pltpu.VMEM((col, group, row * group), BF16), shape((col, 48, LANES), F32)),
        name="first",
        compiler_params=SMALL,
    )(rows, cols)
    spread, degree = pl.pallas_call(
        scale_body(row),
        out_shape=(shape((row, group, LANES), BF16), shape((40, LANES), F32)),
        name="scale",
        compiler_params=SMALL,
    )(exchange(send, "col"))
    spread = exchange(spread, "row").reshape(row * group, LANES)
    send = pl.pallas_call(
        second_body(col, group), out_shape=shape((col, 48, LANES), F32), name="second",
        compiler_params=SMALL,
    )(aff, spread)
    scaled, gram = pl.pallas_call(
        middle_body(row, total),
        out_shape=(shape((group, LANES), F32), shape((row, 8, LANES), F32)),
        name="middle",
    )(exchange(send, "col"), degree)
    gram = pl.pallas_call(
        again_body(col), out_shape=shape((col, 8, LANES), F32), name="again"
    )(exchange(gram, "row"))
    return pl.pallas_call(
        last_body(total), out_shape=shape((group, 32), F32), name="last"
    )(exchange(gram, "col"), scaled)


def solution(mesh):
    spec = P(("row", "col"), None)
    return jax.shard_map(
        shards, mesh=mesh, in_specs=(spec, spec), out_specs=spec, check_vma=False
    )
```

time: 277 us -> 164 us (0.59)
  the two profiles are of different devices: /device:TPU:32 before, /device:TPU:1 now
where the time goes in v1:
time: 164 us; the launch traced here: 163 us
  blocking collectives  117 us (71%)
  Pallas kernels  41.9 us (26%)
  local copies, waits for them, and re-layouts  3.88 us (2%)
    all_to_all x7, blocking collectives, exchange(): return lax.all_to_all(x, axis, 0, 0, tiled=True)  117 us
    pallas_call x1, Pallas kernels, shards(): pl.pallas_call(first_body(col, group, log_scale), out_shape=(pltpu.VMEM((...  21.3 us
    pallas_call x1, Pallas kernels, shards(): pl.pallas_call(second_body(col, group), out_shape=shape((col, 48, LANES),...  8.23 us
    pallas_call x1, Pallas kernels, shards(): pl.pallas_call(middle_body(row, total), out_shape=(shape((group, LANES),...  5.37 us
    pallas_call x1, Pallas kernels, shards(): pl.pallas_call(last_body(total), out_shape=shape((group, 32), F32), name=...  4.84 us

profile of v1, /device:TPU:1, one launch (start us, length us, event | category | flops | bytes accessed | tf_op | source)
XLA Modules:
  0.0 162.9 jit_solution(2334923972900315744)
XLA Ops:
  0.0 0.9 copy.3.points_ref
  0.9 0.8 copy.4.vectors_ref
  1.7 0.2 pack.1
  1.9 22.7 %all_to_all.35.rows_ref = bf16[16,80,128]{2,1,0:T(8,128)(2,1)S(1)} all-to-all(bf16[16,80,128]{2,1,0:T(8,128)(2,1)S(1)} %get-tuple-element.13), channel_id=1, replica_groups=mesh['row'=16,'col'=16] {'col'}, dimensions={0} | all-to-all | bytes 655360 | tf_op jit(solution)/shard_map/all_to_all | solution.py:240
  24.6 19.4 %all_to_all.36 = bf16[16,160,128]{2,1,0:T(8,128)(2,1)S(1)} all-to-all(bf16[16,160,128]{2,1,0:T(8,128)(2,1)S(1)} %get-tuple-element.14), channel_id=1, replica_groups=mesh['row'=16,'col'=16] {'row'}, dimensions={0} | all-to-all | bytes 1310720 | tf_op jit(solution)/shard_map/all_to_all | solution.py:240
  44.0 21.3 %first.1 = (bf16[16,160,2560]{2,1,0:T(8,128)(2,1)S(1)}, f32[16,48,128]{2,1,0:T(8,128)S(1)}) custom-call(bf16[16,80,128]{2,1,0:T(8,128)(2,1)S(1)} %all_to_all.35.rows_ref, bf16[2560,128]{1,0:T(8,128)(2,1)S(1)} %bitcast.3), custom_call_target="tpu_custom_call" | custom-call | tf_op jit(solution)/shard_map/first/pallas_call | solution.py:250
  65.3 17.8 %all_to_all.37.recv_ref = f32[16,48,128]{2,1,0:T(8,128)S(1)} all-to-all(f32[16,48,128]{2,1,0:T(8,128)S(1)} %get-tuple-element.16), channel_id=1, replica_groups=mesh['row'=16,'col'=16] {'col'}, dimensions={0} | all-to-all | bytes 786432 | tf_op jit(solution)/shard_map/all_to_all | solution.py:240
  83.1 0.6 scale.1
  83.7 0.0 copy-start
  83.7 0.6 copy-done
  84.3 16.2 %all_to_all.38 = bf16[16,160,128]{2,1,0:T(8,128)(2,1)S(1)} all-to-all(bf16[16,160,128]{2,1,0:T(8,128)(2,1)S(1)} %get-tuple-element.17), channel_id=1, replica_groups=mesh['row'=16,'col'=16] {'row'}, dimensions={0} | all-to-all | bytes 1310720 | tf_op jit(solution)/shard_map/all_to_all | solution.py:240
  100.5 8.2 %second.1 = f32[16,48,128]{2,1,0:T(8,128)S(1)} custom-call(bf16[16,160,2560]{2,1,0:T(8,128)(2,1)S(1)} %get-tuple-element.15.aff_ref, bf16[2560,128]{1,0:T(8,128)(2,1)S(1)} %bitcast.2), custom_call_target="tpu_custom_call" | custom-call | tf_op jit(solution)/shard_map/second/pallas_call | solution.py:263
  108.8 18.1 %all_to_all.39.recv_ref = f32[16,48,128]{2,1,0:T(8,128)} all-to-all(f32[16,48,128]{2,1,0:T(8,128)S(1)} %second.1), channel_id=1, replica_groups=mesh['row'=16,'col'=16] {'col'}, dimensions={0} | all-to-all | bytes 786432 | tf_op jit(solution)/shard_map/all_to_all | solution.py:240
  126.8 5.4 %middle.1 = (f32[160,128]{1,0:T(8,128)}, f32[16,8,128]{2,1,0:T(8,128)}) custom-call(f32[16,48,128]{2,1,0:T(8,128)} %all_to_all.39.recv_ref, f32[40,128]{1,0:T(8,128)} %copy-done), custom_call_target="tpu_custom_call" | custom-call | tf_op jit(solution)/shard_map/middle/pallas_call | solution.py:267
  132.2 10.7 %all_to_all.40.recv_ref = f32[16,8,128]{2,1,0:T(8,128)} all-to-all(f32[16,8,128]{2,1,0:T(8,128)} %get-tuple-element.19), channel_id=1, replica_groups=mesh['row'=16,'col'=16] {'row'}, dimensions={0} | all-to-all | bytes 131072 | tf_op jit(solution)/shard_map/all_to_all | solution.py:240
  142.9 1.5 again.1
  144.4 12.1 %all_to_all.41.recv_ref = f32[16,8,128]{2,1,0:T(8,128)} all-to-all(f32[16,8,128]{2,1,0:T(8,128)} %again.1), channel_id=1, replica_groups=mesh['row'=16,'col'=16] {'col'}, dimensions={0} | all-to-all | bytes 131072 | tf_op jit(solution)/shard_map/all_to_all | solution.py:240
  156.5 4.8 %last.1 = f32[160,32]{1,0:T(8,128)} custom-call(f32[16,8,128]{2,1,0:T(8,128)} %all_to_all.41.recv_ref, f32[160,128]{1,0:T(8,128)} %get-tuple-element.20.scaled_ref), custom_call_target="tpu_custom_call" | custom-call | tf_op jit(solution)/shard_map/last/pallas_call | solution.py:275
  161.3 1.6 copy.5
Async XLA Ops:
  83.7 0.6 copy-start

commit v2 on v0

v2 whole, which is shorter than its diff:
```python
import math

import jax
import jax.numpy as jnp
from jax import lax
from jax.experimental import pallas as pl
from jax.experimental.pallas import tpu as pltpu
from jax.sharding import PartitionSpec as P

KERNEL_SCALE = 5.12
F32 = jnp.float32
BF16 = jnp.bfloat16
LANES = 128
PARAMS = pltpu.CompilerParams(vmem_limit_bytes=32 * 1024 * 1024)
REST = 32
WIDTH = 512
NORM, ONES, END = 64, 67, 70


def lane_of(shape):
    return lax.broadcasted_iota(jnp.int32, shape, len(shape) - 1)


def row_of(shape):
    return lax.broadcasted_iota(jnp.int32, shape, len(shape) - 2)


def roll(x, shift):
    shift %= LANES
    return pltpu.roll(x, shift, 1) if shift else x


def fold(x, place=0):
    h = x.shape[0] // 4
    group = lane_of((h, LANES)) // REST
    out = jnp.zeros((h, LANES), F32)
    for g in range(4):
        out = jnp.where(group == g, roll(x[g * h : (g + 1) * h], REST * (g - place)), out)
    return out


def unfold(pieces):
    h = pieces[0].shape[0]
    group = lane_of((h, LANES)) // REST
    rows = []
    for g in range(4):
        out = jnp.zeros((h, LANES), F32)
        for q, piece in enumerate(pieces):
            out = jnp.where(group == q, roll(piece, REST * (q - g)), out)
        rows.append(out)
    return jnp.concatenate(rows, axis=0)


def split(x):
    first = x.astype(BF16).astype(F32)
    second = (x - first).astype(BF16).astype(F32)
    return first, second, x - first - second


def widen(x):
    return jnp.concatenate([x, jnp.zeros((x.shape[0], LANES - x.shape[1]), x.dtype)], axis=1)


def main_and_rest(x):
    return x[:, 0:LANES], fold(widen(x[:, LANES : LANES + REST]))


def copies(ref, value):
    for i in range(ref.shape[0]):
        ref[i] = value


def pack_body(points_ref, vectors_ref, cols_ref, rows_ref):
    pts = points_ref[...].astype(F32)
    main, rest = main_and_rest(pts)
    copies(rows_ref, jnp.concatenate([main, rest], axis=0).astype(BF16))
    features, group = pts.shape
    half = group // 2
    flat = jnp.concatenate([main, widen(pts[:, LANES:])], axis=1)
    flat = jnp.concatenate([flat, jnp.zeros_like(flat)], axis=0).T
    by_point = flat[0:half] + roll(flat[half:group], features)
    main, rest = main_and_rest(vectors_ref[...].astype(F32))
    parts = [by_point, main, rest, jnp.zeros((8, LANES), F32)]
    copies(cols_ref, jnp.concatenate(parts, axis=0).astype(BF16))


def first_body(log_scale):
    def body(rows_ref, cols_ref, aff_ref, send_ref, left_ref, right_ref, vec_ref):
        count = rows_ref.shape[0]
        total = left_ref.shape[0]

        def put_right(tile, raw):
            n, at = divmod(tile * LANES, WIDTH)
            scaled = raw * log_scale
            first = scaled.astype(BF16)
            norm = jnp.sum(raw * raw, axis=0, keepdims=True) * (-0.5 * log_scale)
            row = row_of((16, LANES))
            extra = jnp.where(row < ONES - NORM, 1.0, 0.0)
            for i, piece in enumerate(split(norm)):
                extra = jnp.where(row == ONES - NORM + i, piece, extra)
            right_ref[n, 0:64, at : at + LANES] = first
            right_ref[n, 64:80, at : at + LANES] = extra.astype(BF16)
            right_ref[n, 80:128, at : at + LANES] = jnp.zeros((48, LANES), BF16)
            right_ref[n, 128:192, at : at + LANES] = (scaled - first.astype(F32)).astype(BF16)
            right_ref[n, 192:256, at : at + LANES] = jnp.zeros((64, LANES), BF16)

        for i in range(count):
            put_right(i, rows_ref[i, 0:64].astype(F32))
        for m in range(count // 4):
            rests = [rows_ref[4 * m + q, 64:80].astype(F32) for q in range(4)]
            put_right(count + m, unfold(rests))

        lane = lane_of((80, LANES))
        low = lane < NORM
        for i in range(count):
            raw = cols_ref[i, 0:80].astype(F32)
            squares = raw * raw
            blocks = []
            for side in range(2):
                mine = low if side == 0 else jnp.logical_not(low)
                norm = jnp.sum(jnp.where(mine, squares, 0.0), axis=1, keepdims=True)
                norm = norm * (-0.5 * log_scale)
                block = jnp.where(low, raw if side == 0 else roll(raw, NORM), 0.0)
                for k, piece in enumerate(split(norm)):
                    block = jnp.where(lane == NORM + k, piece, block)
                block = jnp.where((lane >= ONES) & (lane < END), 1.0, block)
                blocks.append(block.astype(BF16))
            at = i * LANES
            left_ref[at : at + 80, :] = blocks[0]
            left_ref[at + 80 : at + LANES, :] = blocks[1][0:48]
            at = count * LANES + i * REST
            left_ref[at : at + REST, :] = blocks[1][48:80]

        vec_ref[32:48, :] = jnp.where(row_of((16, total)) == 0, 1.0, 0.0).astype(BF16)
        for i in range(count):
            vec_ref[0:32, i * LANES : (i + 1) * LANES] = cols_ref[i, 80:112]
        for m in range(count // 4):
            rests = [cols_ref[4 * m + q, 112:128].astype(F32)[0:8] for q in range(4)]
            at = (count + m) * LANES
            vec_ref[0:32, at : at + LANES] = unfold(rests).astype(BF16)

        chunk = 512

        def product(n):
            right = right_ref[n]
            for at in range(0, total, chunk):
                left = left_ref[at : at + chunk, :]
                power = jnp.dot(
                    jnp.concatenate([left, left], axis=1), right, preferred_element_type=F32
                )
                aff_ref[n, at : at + chunk, :] = jnp.exp2(power).astype(BF16)
            return jnp.dot(vec_ref[...], aff_ref[n], preferred_element_type=F32)

        def block(n, carry):
            out = product(n)
            for k in range(WIDTH // LANES):
                tile = out[:, k * LANES : (k + 1) * LANES]
                send_ref[n * (WIDTH // LANES) + k, 0:32, :] = tile[0:32]
                send_ref[n * (WIDTH // LANES) + k, 40:48, :] = tile[32:40]
            return carry

        lax.fori_loop(0, count * LANES // WIDTH, block, 0)
        out = product(count * LANES // WIDTH)
        for m in range(count // 4):
            tile = out[:, m * LANES : (m + 1) * LANES]
            for q in range(4):
                send_ref[4 * m + q, 32:40, :] = fold(tile[0:32], q)
                send_ref[4 * m + q, 41:42, :] = roll(tile[32:40], -REST * q)[0:1]

    return body


def gram_of(x):
    return lax.dot_general(
        x,
        x,
        (((1,), (1,)), ((), ())),
        precision=lax.Precision.HIGHEST,
        preferred_element_type=F32,
    )


def whole(main, rest):
    return jnp.concatenate([main, unfold([rest])], axis=1)


def scale_body(recv_ref, spread_ref, degree_ref):
    total = jnp.sum(recv_ref[...], axis=0)
    rest = jnp.where(lane_of((1, LANES)) < REST, total[41:42], 0.0)
    rest = jnp.broadcast_to(rest, (8, LANES))
    rest = (rest + roll(rest, REST)) + (roll(rest, 2 * REST) + roll(rest, 3 * REST))
    degree_ref[0:8, :] = jnp.broadcast_to(total[40:41], (8, LANES))
    degree_ref[8:16, :] = rest
    main, rest = total[0:32] / total[40:41], total[32:40] / rest
    gram = fold(widen(gram_of(whole(main, rest))))
    copies(spread_ref, jnp.concatenate([main, rest, gram], axis=0))


def second_body(aff_ref, spread_ref, send_ref, vec_ref):
    count = spread_ref.shape[0]
    gram = jnp.sum(spread_ref[:, 40:48, :], axis=0)

    def put(tile, value):
        first = value.astype(BF16)
        at = tile * LANES
        vec_ref[0:32, at : at + LANES] = first
        vec_ref[32:64, at : at + LANES] = (value - first.astype(F32)).astype(BF16)

    for i in range(count):
        put(i, spread_ref[i, 0:32, :])
    for m in range(count // 4):
        put(count + m, unfold([spread_ref[4 * m + q, 32:40, :] for q in range(4)]))

    def product(n):
        out = jnp.dot(vec_ref[...], aff_ref[n], preferred_element_type=F32)
        return out[0:32] + out[32:64]

    def block(n, carry):
        out = product(n)
        for k in range(WIDTH // LANES):
            send_ref[n * (WIDTH // LANES) + k, 0:32, :] = out[:, k * LANES : (k + 1) * LANES]
            send_ref[n * (WIDTH // LANES) + k, 40:48, :] = gram
        return carry

    lax.fori_loop(0, count * LANES // WIDTH, block, 0)
    out = product(count * LANES // WIDTH)
    for m in range(count // 4):
        for q in range(4):
            send_ref[4 * m + q, 32:40, :] = fold(out[:, m * LANES : (m + 1) * LANES], q)


def solved(gram, right):
    size = gram.shape[0]
    wide = right.shape[1] // LANES
    columns = [
        jnp.broadcast_to(gram[8 * (k // 8) :, k : k + 1], (size - 8 * (k // 8), LANES))
        for k in range(size)
    ]
    rows = [right[8 * g : 8 * g + 8] for g in range(size // 8)]
    for j in range(size):
        base, at = j // 8, j % 8
        pivot = columns[j][at : at + 1]
        scale = lax.rsqrt(pivot)
        scale = scale * (1.5 - 0.5 * pivot * scale * scale)
        factor = columns[j] * scale
        for k in range(j + 1, size):
            skip = 8 * (k // 8 - base)
            mine = factor[k - 8 * base : k - 8 * base + 1]
            columns[k] = columns[k] - factor[skip:] * mine
        top = rows[base][at : at + 1] * jnp.concatenate([scale] * wide, axis=1)
        for g in range(base, size // 8):
            part = factor[8 * (g - base) : 8 * (g - base) + 8]
            if g == base:
                row = row_of((8, LANES))
                part = jnp.where(row > at, part, 0.0)
            new = rows[g] - jnp.concatenate([part] * wide, axis=1) * top
            if g == base:
                new = jnp.where(row_of(new.shape) == at, top, new)
            rows[g] = new
    return jnp.concatenate(rows, axis=0)


def middle_body(points):
    def body(recv_ref, degree_ref, scaled_ref, gram_ref):
        total = jnp.sum(recv_ref[...], axis=0)
        main = total[0:32] / degree_ref[0:1, :]
        rest = total[32:40] / degree_ref[8:16, :]
        scaled = solved(unfold([total[40:48]]) / points, whole(main, rest))
        scaled_ref[...] = scaled
        copies(gram_ref, fold(widen(gram_of(scaled))))

    return body


def again_body(recv_ref, gram_ref):
    copies(gram_ref, jnp.sum(recv_ref[...], axis=0))


def last_body(points):
    def body(recv_ref, scaled_ref, out_ref):
        gram = unfold([jnp.sum(recv_ref[...], axis=0)]) / points
        out_ref[...] = solved(gram, scaled_ref[...])[:, 0 : out_ref.shape[1]]

    return body


def shards(points, start_vectors):
    group, features = points.shape
    row, col = lax.axis_size("row"), lax.axis_size("col")
    total = group * row * col
    log_scale = 2.0 * KERNEL_SCALE / features * math.log2(math.e)
    blocks = col * group // WIDTH
    shape = jax.ShapeDtypeStruct

    def exchange(x, axis):
        return lax.all_to_all(x, axis, 0, 0, tiled=True)

    def call(body, name, out_shape, *args, scratch=()):
        return pl.pallas_call(
            body, out_shape=out_shape, scratch_shapes=scratch, name=name, compiler_params=PARAMS
        )(*args)

    cols, rows = call(
        pack_body,
        "pack",
        (shape((row, 128, LANES), BF16), shape((col, 80, LANES), BF16)),
        points.T,
        start_vectors.T,
    )
    rows = exchange(rows, "col")
    cols = exchange(cols, "row")
    aff, send = call(
        first_body(log_scale),
        "first",
        (pltpu.VMEM((blocks, row * group, WIDTH), BF16), shape((col, 48, LANES), F32)),
        rows,
        cols,
        scratch=(
            pltpu.VMEM((row * group, LANES), BF16),
            pltpu.VMEM((blocks, 256, WIDTH), BF16),
            pltpu.VMEM((48, row * group), BF16),
        ),
    )
    spread, degree = call(
        scale_body,
        "scale",
        (shape((row, 48, LANES), F32), shape((16, LANES), F32)),
        exchange(send, "col"),
    )
    send = call(
        second_body,
        "second",
        shape((col, 48, LANES), F32),
        aff,
        exchange(spread, "row"),
        scratch=(pltpu.VMEM((64, row * group), BF16),),
    )
    scaled, gram = call(
        middle_body(total),
        "middle",
        (shape((32, 2 * LANES), F32), shape((row, 8, LANES), F32)),
        exchange(send, "col"),
        degree,
    )
    gram = call(again_body, "again", shape((col, 8, LANES), F32), exchange(gram, "row"))
    out = call(
        last_body(total), "last", shape((32, group), F32), exchange(gram, "col"), scaled
    )
    return out.T


def solution(mesh):
    spec = P(("row", "col"), None)
    return jax.shard_map(
        shards, mesh=mesh, in_specs=(spec, spec), out_specs=spec, check_vma=False
    )
```

time: 277 us -> 126 us (0.45)
  the two profiles are of different devices: /device:TPU:32 before, /device:TPU:1 now
where the time goes in v2:
time: 126 us
  blocking collectives  111 us (88%)
  Pallas kernels  13.6 us (11%)
  local copies, waits for them, and re-layouts  1.47 us (1%)
    all_to_all x7, blocking collectives, exchange(): return lax.all_to_all(x, axis, 0, 0, tiled=True)  111 us
    pallas_call x7, Pallas kernels, call(): pl.pallas_call(body, out_shape=out_shape, scratch_shapes=scratch, name=na...  13.6 us

profile of v2, /device:TPU:1, one launch (start us, length us, event | category | flops | bytes accessed | tf_op | source)
XLA Modules:
  0.0 125.9 jit_solution(4955327858492046851)
XLA Ops:
  0.0 0.0 copy-start
  0.0 0.8 copy-done
  0.8 0.0 copy-start.1
  0.8 0.7 copy-done.1
  1.5 0.2 pack.1
  1.7 17.7 %all_to_all.35.cols_ref = bf16[16,128,128]{2,1,0:T(8,128)(2,1)S(1)} all-to-all(bf16[16,128,128]{2,1,0:T(8,128)(2,1)S(1)} %get-tuple-element.14), channel_id=1, replica_groups=mesh['row'=16,'col'=16] {'row'}, dimensions={0} | all-to-all | bytes 1048576 | tf_op jit(solution)/shard_map/all_to_all | solution.py:296
  19.4 23.3 %all_to_all.36.rows_ref = bf16[16,80,128]{2,1,0:T(8,128)(2,1)S(1)} all-to-all(bf16[16,80,128]{2,1,0:T(8,128)(2,1)S(1)} %get-tuple-element.13), channel_id=1, replica_groups=mesh['row'=16,'col'=16] {'col'}, dimensions={0} | all-to-all | bytes 655360 | tf_op jit(solution)/shard_map/all_to_all | solution.py:296
  42.7 7.5 %first.1 = (bf16[5,2560,512]{2,1,0:T(8,128)(2,1)S(1)}, f32[16,48,128]{2,1,0:T(8,128)S(1)}) custom-call(bf16[16,80,128]{2,1,0:T(8,128)(2,1)S(1)} %all_to_all.36.rows_ref, bf16[16,128,128]{2,1,0:T(8,128)(2,1)S(1)} %all_to_all.35.cols_ref), custom_call_target="tpu_custom_call" | custom-call | tf_op jit(solution)/shard_map/first/pallas_call | solution.py:299
  50.3 17.3 %all_to_all.37.recv_ref = f32[16,48,128]{2,1,0:T(8,128)S(1)} all-to-all(f32[16,48,128]{2,1,0:T(8,128)S(1)} %get-tuple-element.16), channel_id=1, replica_groups=mesh['row'=16,'col'=16] {'col'}, dimensions={0} | all-to-all | bytes 786432 | tf_op jit(solution)/shard_map/all_to_all | solution.py:296
  67.5 0.4 scale.1
  67.9 13.6 %all_to_all.38.spread_ref = f32[16,48,128]{2,1,0:T(8,128)S(1)} all-to-all(f32[16,48,128]{2,1,0:T(8,128)S(1)} %get-tuple-element.17), channel_id=1, replica_groups=mesh['row'=16,'col'=16] {'row'}, dimensions={0} | all-to-all | bytes 786432 | tf_op jit(solution)/shard_map/all_to_all | solution.py:296
  81.6 3.1 %second.1 = f32[16,48,128]{2,1,0:T(8,128)S(1)} custom-call(bf16[5,2560,512]{2,1,0:T(8,128)(2,1)S(1)} %get-tuple-element.15.aff_ref, f32[16,48,128]{2,1,0:T(8,128)S(1)} %all_to_all.38.spread_ref), custom_call_target="tpu_custom_call" | custom-call | tf_op jit(solution)/shard_map/second/pallas_call | solution.py:299
  84.6 17.3 %all_to_all.39.recv_ref = f32[16,48,128]{2,1,0:T(8,128)S(1)} all-to-all(f32[16,48,128]{2,1,0:T(8,128)S(1)} %second.1), channel_id=1, replica_groups=mesh['row'=16,'col'=16] {'col'}, dimensions={0} | all-to-all | bytes 786432 | tf_op jit(solution)/shard_map/all_to_all | solution.py:296
  102.0 1.0 middle.1
  103.0 9.9 %all_to_all.40.recv_ref = f32[16,8,128]{2,1,0:T(8,128)S(1)} all-to-all(f32[16,8,128]{2,1,0:T(8,128)S(1)} %get-tuple-element.19), channel_id=1, replica_groups=mesh['row'=16,'col'=16] {'row'}, dimensions={0} | all-to-all | bytes 131072 | tf_op jit(solution)/shard_map/all_to_all | solution.py:296
  112.9 11.6 %all_to_all.41.recv_ref = f32[16,8,128]{2,1,0:T(8,128)S(1)} all-to-all(f32[16,8,128]{2,1,0:T(8,128)S(1)} %again.1), channel_id=1, replica_groups=mesh['row'=16,'col'=16] {'col'}, dimensions={0} | all-to-all | bytes 131072 | tf_op jit(solution)/shard_map/all_to_all | solution.py:296
  124.5 1.4 %last.1 = f32[32,160]{1,0:T(8,128)} custom-call(f32[16,8,128]{2,1,0:T(8,128)S(1)} %all_to_all.41.recv_ref, f32[32,256]{1,0:T(8,128)S(1)} %get-tuple-element.20.scaled_ref), custom_call_target="tpu_custom_call" | custom-call | tf_op jit(solution)/shard_map/last/pallas_call | solution.py:299
  (1 shorter events, 0.0 us)
Async XLA Ops:
  0.0 0.8 copy-start
  0.8 0.7 copy-start.1

commit v3 on v2

v3 whole, which is shorter than its diff:
```python
import math

import jax
import jax.numpy as jnp
from jax import lax
from jax.experimental import pallas as pl
from jax.experimental.pallas import tpu as pltpu
from jax.sharding import Mesh
from jax.sharding import PartitionSpec as P

KERNEL_SCALE = 5.12
F32 = jnp.float32
BF16 = jnp.bfloat16
LANES = 128
PARAMS = pltpu.CompilerParams(vmem_limit_bytes=32 * 1024 * 1024)
REST = 32
WIDTH = 512
NORM, ONES, END = 64, 67, 70


def lane_of(shape):
    return lax.broadcasted_iota(jnp.int32, shape, len(shape) - 1)


def row_of(shape):
    return lax.broadcasted_iota(jnp.int32, shape, len(shape) - 2)


def roll(x, shift):
    shift %= LANES
    return pltpu.roll(x, shift, 1) if shift else x


def fold(x, place=0):
    h = x.shape[0] // 4
    group = lane_of((h, LANES)) // REST
    out = jnp.zeros((h, LANES), F32)
    for g in range(4):
        out = jnp.where(group == g, roll(x[g * h : (g + 1) * h], REST * (g - place)), out)
    return out


def unfold(pieces):
    h = pieces[0].shape[0]
    group = lane_of((h, LANES)) // REST
    rows = []
    for g in range(4):
        out = jnp.zeros((h, LANES), F32)
        for q, piece in enumerate(pieces):
            out = jnp.where(group == q, roll(piece, REST * (q - g)), out)
        rows.append(out)
    return jnp.concatenate(rows, axis=0)


def split(x):
    first = x.astype(BF16).astype(F32)
    second = (x - first).astype(BF16).astype(F32)
    return first, second, x - first - second


def widen(x):
    return jnp.concatenate([x, jnp.zeros((x.shape[0], LANES - x.shape[1]), x.dtype)], axis=1)


def main_and_rest(x):
    return x[:, 0:LANES], fold(widen(x[:, LANES : LANES + REST]))


def copies(ref, value):
    for i in range(ref.shape[0]):
        ref[i] = value


def pack_body(points_hbm, vectors_hbm, cols_ref, rows_ref, points_ref, vectors_ref, sems):
    loads = (
        pltpu.make_async_copy(points_hbm, points_ref, sems.at[0]),
        pltpu.make_async_copy(vectors_hbm, vectors_ref, sems.at[1]),
    )
    for load in loads:
        load.start()
    for load in loads:
        load.wait()
    pts = points_ref[...].astype(F32)
    main, rest = main_and_rest(pts)
    copies(rows_ref, jnp.concatenate([main, rest], axis=0).astype(BF16))
    features, group = pts.shape
    half = group // 2
    flat = jnp.concatenate([main, widen(pts[:, LANES:])], axis=1)
    flat = jnp.concatenate([flat, jnp.zeros_like(flat)], axis=0).T
    by_point = flat[0:half] + roll(flat[half:group], features)
    main, rest = main_and_rest(vectors_ref[...].astype(F32))
    parts = [by_point, main, rest, jnp.zeros((8, LANES), F32)]
    copies(cols_ref, jnp.concatenate(parts, axis=0).astype(BF16))


def blocks_of(count):
    lanes = count * LANES
    main = [(at, WIDTH) for at in range(0, lanes, WIDTH)]
    return main, (lanes, lanes // 4)


def put_columns(log_scale, cols_ref, left_ref, vec_ref):
    count = cols_ref.shape[0]
    total = left_ref.shape[0]
    lane = lane_of((80, LANES))
    low = lane < NORM
    for i in range(count):
        raw = cols_ref[i, 0:80].astype(F32)
        squares = raw * raw
        blocks = []
        for side in range(2):
            mine = low if side == 0 else jnp.logical_not(low)
            norm = jnp.sum(jnp.where(mine, squares, 0.0), axis=1, keepdims=True)
            norm = norm * (-0.5 * log_scale)
            block = jnp.where(low, raw if side == 0 else roll(raw, NORM), 0.0)
            for k, piece in enumerate(split(norm)):
                block = jnp.where(lane == NORM + k, piece, block)
            block = jnp.where((lane >= ONES) & (lane < END), 1.0, block)
            blocks.append(block.astype(BF16))
        at = i * LANES
        left_ref[at : at + 80, :] = blocks[0]
        left_ref[at + 80 : at + LANES, :] = blocks[1][0:48]
        at = count * LANES + i * REST
        left_ref[at : at + REST, :] = blocks[1][48:80]
    vec_ref[32:48, :] = jnp.where(row_of((16, total)) == 0, 1.0, 0.0).astype(BF16)
    for i in range(count):
        vec_ref[0:32, i * LANES : (i + 1) * LANES] = cols_ref[i, 80:112]
    for m in range(count // 4):
        rests = [cols_ref[4 * m + q, 112:128].astype(F32)[0:8] for q in range(4)]
        at = (count + m) * LANES
        vec_ref[0:32, at : at + LANES] = unfold(rests).astype(BF16)


def put_rows(log_scale, rows_ref, right_ref):
    count = rows_ref.shape[0]

    def put(tile, raw):
        at = tile * LANES
        scaled = raw * log_scale
        first = scaled.astype(BF16)
        norm = jnp.sum(raw * raw, axis=0, keepdims=True) * (-0.5 * log_scale)
        row = row_of((16, LANES))
        extra = jnp.where(row < ONES - NORM, 1.0, 0.0)
        for i, piece in enumerate(split(norm)):
            extra = jnp.where(row == ONES - NORM + i, piece, extra)
        right_ref[0:64, at : at + LANES] = first
        right_ref[64:80, at : at + LANES] = extra.astype(BF16)
        right_ref[80:128, at : at + LANES] = jnp.zeros((48, LANES), BF16)
        right_ref[128:192, at : at + LANES] = (scaled - first.astype(F32)).astype(BF16)
        right_ref[192:256, at : at + LANES] = jnp.zeros((64, LANES), BF16)

    for i in range(count):
        put(i, rows_ref[i, 0:64].astype(F32))
    for m in range(count // 4):
        put(count + m, unfold([rows_ref[4 * m + q, 64:80].astype(F32) for q in range(4)]))


def affinity_product(left_ref, right_ref, vec_ref, aff_ref, send_ref):
    total = left_ref.shape[0]
    main, rest = blocks_of(send_ref.shape[0])
    chunk = 512

    def product(at, width):
        right = right_ref[:, at : at + width]
        for start in range(0, total, chunk):
            left = left_ref[start : start + chunk, :]
            power = jnp.dot(
                jnp.concatenate([left, left], axis=1), right, preferred_element_type=F32
            )
            aff_ref[start : start + chunk, at : at + width] = jnp.exp2(power).astype(BF16)
        return jnp.dot(
            vec_ref[...], aff_ref[:, at : at + width], preferred_element_type=F32
        )

    for at, width in main:
        out = product(at, width)
        for k in range(width // LANES):
            tile = out[:, k * LANES : (k + 1) * LANES]
            send_ref[at // LANES + k, 0:32, :] = tile[0:32]
            send_ref[at // LANES + k, 40:48, :] = tile[32:40]
    out = product(*rest)
    for m in range(rest[1] // LANES):
        tile = out[:, m * LANES : (m + 1) * LANES]
        for q in range(4):
            send_ref[4 * m + q, 32:40, :] = fold(tile[0:32], q)
            send_ref[4 * m + q, 41:42, :] = roll(tile[32:40], -REST * q)[0:1]


def away_body(log_scale):
    def body(rows_ref, cols_ref, aff_ref, send_ref, left_ref, vec_ref, right_ref):
        put_columns(log_scale, cols_ref, left_ref, vec_ref)
        put_rows(log_scale, rows_ref, right_ref)
        affinity_product(left_ref, right_ref, vec_ref, aff_ref, send_ref)

    return body


def home_body(log_scale):
    def body(rows_ref, left_ref, vec_ref, aff_ref, send_ref, right_ref):
        put_rows(log_scale, rows_ref, right_ref)
        affinity_product(left_ref, right_ref, vec_ref, aff_ref, send_ref)

    return body


def join_body(mine_ref, other_ref, out_ref):
    out_ref[...] = mine_ref[...] + other_ref[...]


def gram_of(x):
    return lax.dot_general(
        x,
        x,
        (((1,), (1,)), ((), ())),
        precision=lax.Precision.HIGHEST,
        preferred_element_type=F32,
    )


def whole(main, rest):
    return jnp.concatenate([main, unfold([rest])], axis=1)


def scale_body(recv_ref, spread_ref, degree_ref):
    total = jnp.sum(recv_ref[...], axis=0)
    rest = jnp.where(lane_of((1, LANES)) < REST, total[41:42], 0.0)
    rest = jnp.broadcast_to(rest, (8, LANES))
    rest = (rest + roll(rest, REST)) + (roll(rest, 2 * REST) + roll(rest, 3 * REST))
    degree_ref[0:8, :] = jnp.broadcast_to(total[40:41], (8, LANES))
    degree_ref[8:16, :] = rest
    main, rest = total[0:32] / total[40:41], total[32:40] / rest
    gram = fold(widen(gram_of(whole(main, rest))))
    copies(spread_ref, jnp.concatenate([main, rest, gram], axis=0))


def put_vectors(spread_ref, vec_ref):
    count = spread_ref.shape[0]

    def put(tile, value):
        first = value.astype(BF16)
        at = tile * LANES
        vec_ref[0:32, at : at + LANES] = first
        vec_ref[32:64, at : at + LANES] = (value - first.astype(F32)).astype(BF16)

    for i in range(count):
        put(i, spread_ref[i, 0:32, :])
    for m in range(count // 4):
        put(count + m, unfold([spread_ref[4 * m + q, 32:40, :] for q in range(4)]))


def second_product(aff_ref, vec_ref, gram, send_ref):
    main, rest = blocks_of(send_ref.shape[0])

    def product(at, width):
        out = jnp.dot(vec_ref[...], aff_ref[:, at : at + width], preferred_element_type=F32)
        return out[0:32] + out[32:64]

    for at, width in main:
        out = product(at, width)
        for k in range(width // LANES):
            send_ref[at // LANES + k, 0:32, :] = out[:, k * LANES : (k + 1) * LANES]
            send_ref[at // LANES + k, 40:48, :] = gram
    out = product(*rest)
    for m in range(rest[1] // LANES):
        for q in range(4):
            send_ref[4 * m + q, 32:40, :] = fold(out[:, m * LANES : (m + 1) * LANES], q)


def away_again_body(aff_ref, spread_ref, send_ref, vec_ref, gram_ref):
    gram = jnp.sum(spread_ref[:, 40:48, :], axis=0)
    gram_ref[...] = gram
    put_vectors(spread_ref, vec_ref)
    second_product(aff_ref, vec_ref, gram, send_ref)


def home_again_body(aff_ref, vec_ref, gram_ref, send_ref):
    second_product(aff_ref, vec_ref, gram_ref[...], send_ref)


def solved(gram, right):
    size = gram.shape[0]
    wide = right.shape[1] // LANES
    columns = [
        jnp.broadcast_to(gram[8 * (k // 8) :, k : k + 1], (size - 8 * (k // 8), LANES))
        for k in range(size)
    ]
    rows = [right[8 * g : 8 * g + 8] for g in range(size // 8)]
    for j in range(size):
        base, at = j // 8, j % 8
        pivot = columns[j][at : at + 1]
        scale = lax.rsqrt(pivot)
        scale = scale * (1.5 - 0.5 * pivot * scale * scale)
        factor = columns[j] * scale
        for k in range(j + 1, size):
            skip = 8 * (k // 8 - base)
            mine = factor[k - 8 * base : k - 8 * base + 1]
            columns[k] = columns[k] - factor[skip:] * mine
        top = rows[base][at : at + 1] * jnp.concatenate([scale] * wide, axis=1)
        for g in range(base, size // 8):
            part = factor[8 * (g - base) : 8 * (g - base) + 8]
            if g == base:
                row = row_of((8, LANES))
                part = jnp.where(row > at, part, 0.0)
            new = rows[g] - jnp.concatenate([part] * wide, axis=1) * top
            if g == base:
                new = jnp.where(row_of(new.shape) == at, top, new)
            rows[g] = new
    return jnp.concatenate(rows, axis=0)


def middle_body(points):
    def body(recv_ref, degree_ref, scaled_ref, gram_ref):
        total = jnp.sum(recv_ref[...], axis=0)
        main = total[0:32] / degree_ref[0:1, :]
        rest = total[32:40] / degree_ref[8:16, :]
        scaled = solved(unfold([total[40:48]]) / points, whole(main, rest))
        scaled_ref[...] = scaled
        copies(gram_ref, fold(widen(gram_of(scaled))))

    return body


def again_body(recv_ref, gram_ref):
    copies(gram_ref, jnp.sum(recv_ref[...], axis=0))


def last_body(points):
    def body(recv_ref, scaled_ref, out_ref):
        gram = unfold([jnp.sum(recv_ref[...], axis=0)]) / points
        out_ref[...] = solved(gram, scaled_ref[...])[:, 0 : out_ref.shape[1]]

    return body


def shards(points, start_vectors):
    group, features = points.shape
    row, half, cores = lax.axis_size("row"), lax.axis_size("z"), lax.axis_size("core")
    col = half * cores
    total = group * row * col
    log_scale = 2.0 * KERNEL_SCALE / features * math.log2(math.e)
    lanes = half * group
    shape = jax.ShapeDtypeStruct

    def exchange(x, axis):
        return lax.all_to_all(x, axis, 0, 0, tiled=True)

    def swap(x):
        return lax.ppermute(x, "core", [(0, 1), (1, 0)])

    def call(body, name, out_shape, *args, scratch=(), **kwargs):
        return pl.pallas_call(
            body,
            out_shape=out_shape,
            scratch_shapes=scratch,
            name=name,
            compiler_params=PARAMS,
            **kwargs,
        )(*args)

    hbm_space = pl.BlockSpec(memory_space=pltpu.HBM)
    cols, rows = call(
        pack_body,
        "pack",
        (shape((row, 128, LANES), BF16), shape((half, 80, LANES), BF16)),
        points.T,
        start_vectors.T,
        scratch=(
            pltpu.VMEM((features, group), BF16),
            pltpu.VMEM((start_vectors.shape[1], group), BF16),
            pltpu.SemaphoreType.DMA((2,)),
        ),
        in_specs=[hbm_space, hbm_space],
    )
    home_rows = exchange(rows, "z")
    away_rows = swap(home_rows)
    cols = exchange(cols, "row")
    aff_shape = pltpu.VMEM((row * group, lanes), BF16)
    send_shape = shape((half, 48, LANES), F32)
    right_shape = pltpu.VMEM((256, lanes), BF16)
    away_aff, away_send, left, vec = call(
        away_body(log_scale),
        "away",
        (
            aff_shape,
            send_shape,
            pltpu.VMEM((row * group, LANES), BF16),
            pltpu.VMEM((48, row * group), BF16),
        ),
        away_rows,
        cols,
        scratch=(right_shape,),
    )
    other = swap(away_send)
    home_aff, home_send = call(
        home_body(log_scale),
        "home",
        (aff_shape, send_shape),
        home_rows,
        left,
        vec,
        scratch=(right_shape,),
    )
    send = call(join_body, "join", send_shape, home_send, other)
    spread, degree = call(
        scale_body,
        "scale",
        (shape((row, 48, LANES), F32), shape((16, LANES), F32)),
        exchange(send, "z"),
    )
    away_send, vec, gram = call(
        away_again_body,
        "away_again",
        (send_shape, pltpu.VMEM((64, row * group), BF16), pltpu.VMEM((8, LANES), F32)),
        away_aff,
        exchange(spread, "row"),
    )
    other = swap(away_send)
    home_send = call(home_again_body, "home_again", send_shape, home_aff, vec, gram)
    send = call(join_body, "join_again", send_shape, home_send, other)
    scaled, gram = call(
        middle_body(total),
        "middle",
        (shape((32, 2 * LANES), F32), shape((row, 8, LANES), F32)),
        exchange(send, "z"),
        degree,
    )
    gram = call(again_body, "again", shape((col, 8, LANES), F32), exchange(gram, "row"))
    out = call(
        last_body(total),
        "last",
        shape((32, group), F32),
        exchange(gram, ("z", "core")),
        scaled,
    )
    return out.T


def solution(mesh):
    rows, cols = mesh.devices.shape
    finer = Mesh(mesh.devices.reshape(rows, cols // 2, 2), ("row", "z", "core"))
    spec = P(("row", "z", "core"), None)
    return jax.shard_map(
        shards, mesh=finer, in_specs=(spec, spec), out_specs=spec, check_vma=False
    )
```

time: 126 us -> 115 us (0.913)
  blocking collectives: 111 us -> 77.8 us
  starting transfers between devices: 0 us -> 15.2 us
  waiting for transfers between devices: 0 us -> 6.16 us
    all_to_all x7 -> x6, blocking collectives: 111 us -> 77.8 us  [exchange(): return lax.all_to_all(x, axis, 0, 0, tiled=True)]
    ppermute x0 -> x3, starting transfers between devices: none -> 8.44 us  [swap(): return lax.ppermute(x, 'core', [(0, 1), (1, 0)])]
    all_to_all x0 -> x1, starting transfers between devices: none -> 6.76 us  [exchange(): return lax.all_to_all(x, axis, 0, 0, tiled=True)]
    all_to_all x0 -> x1, waiting for transfers between devices: none -> 5.13 us  [exchange(): return lax.all_to_all(x, axis, 0, 0, tiled=True)]
    pallas_call x7 -> x11, Pallas kernels: 13.6 us -> 14 us  [call(): pl.pallas_call(body, out_shape=out_shape, scratch_shapes=scratch, name=na...]
  transfers between devices with their start and end apart: 0 -> 4, of which waited for: 0 -> 2; matrix products, arithmetic and copies ran while one was open for 0% -> 0% of each run, Pallas kernels for 0% -> 4%
where the time goes in v3:
time: 115 us
  blocking collectives  77.8 us (68%)
  starting transfers between devices  15.2 us (13%)
  Pallas kernels  14 us (12%)
  waiting for transfers between devices  6.16 us (5%)
  local copies, waits for them, and re-layouts  1.47 us (1%)
    all_to_all x6, blocking collectives, exchange(): return lax.all_to_all(x, axis, 0, 0, tiled=True)  77.8 us
    pallas_call x11, Pallas kernels, call(): pl.pallas_call(body, out_shape=out_shape, scratch_shapes=scratch, name=na...  14 us
    ppermute x3, starting transfers between devices, swap(): return lax.ppermute(x, 'core', [(0, 1), (1, 0)])  8.44 us
    all_to_all x1, starting transfers between devices, exchange(): return lax.all_to_all(x, axis, 0, 0, tiled=True)  6.76 us
    all_to_all x1, waiting for transfers between devices, exchange(): return lax.all_to_all(x, axis, 0, 0, tiled=True)  5.13 us
  transfers between devices with their start and end apart: 4, of which 2 were waited for; matrix products, arithmetic and copies ran while one was open for 0% of the time, Pallas kernels for 4%

profile of v3, /device:TPU:1, one launch (start us, length us, event | category | flops | bytes accessed | tf_op | source)
XLA Modules:
  0.0 114.8 jit_solution(11441294111877111022)
XLA Ops:
  0.0 0.8 copy-done
  0.8 0.7 copy-done.1
  1.5 1.0 pack.1
  2.5 17.0 %all_to_all.35.rows_ref = bf16[8,80,128]{2,1,0:T(8,128)(2,1)S(1)} all-to-all(bf16[8,80,128]{2,1,0:T(8,128)(2,1)S(1)} %get-tuple-element.20), channel_id=1, replica_groups=mesh['row'=16,'z'=8,'core'=2] {'z'}, dimensions={0} | all-to-all | bytes 327680 | tf_op jit(solution)/shard_map/all_to_all | solution.py:345
  19.6 6.8 %all-to-all-start.1 = ((bf16[16,128,128]{2,1,0:T(8,128)(2,1)}), bf16[16,128,128]{2,1,0:T(8,128)(2,1)S(1)}, u32[]{:S(2)}, u32[]{:S(2)}) async-start(bf16[16,128,128]{2,1,0:T(8,128)(2,1)} %get-tuple-element.21), calls=%async_computation.1 | async-start | bytes 1048576 | tf_op jit(solution)/shard_map/all_to_all | solution.py:345
  26.3 2.9 %collective-permute-start = (bf16[8,80,128]{2,1,0:T(8,128)(2,1)S(1)}, bf16[8,80,128]{2,1,0:T(8,128)(2,1)S(1)}, u32[]{:S(2)}, u32[]{:S(2)}) collective-permute-start(bf16[8,80,128]{2,1,0:T(8,128)(2,1)S(1)} %all_to_all.35.rows_ref), channel_id=1, source_target_pairs={{0,1},{1,0},{2,3},{3,2},{4,5},{5,4},{6,7},{7,6},{8,9},{9,8},{10,11... | collective-permute-start | bytes 491528 | tf_op jit(solution)/shard_map/ppermute | solution.py:348
  29.2 1.0 collective-permute-done.rows_ref
  30.2 5.1 %all-to-all-done.1.cols_ref = bf16[16,128,128]{2,1,0:T(8,128)(2,1)S(1)} async-done(((bf16[16,128,128]{2,1,0:T(8,128)(2,1)}), bf16[16,128,128]{2,1,0:T(8,128)(2,1)S(1)}, u32[]{:S(2)}, u32[]{:S(2)}) %all-to-all-start.1) | async-done | bytes 524320 | tf_op jit(solution)/shard_map/all_to_all | solution.py:345
  35.3 4.2 %away.1 = (bf16[2560,1280]{1,0:T(8,128)(2,1)S(1)}, f32[8,48,128]{2,1,0:T(8,128)S(1)}, bf16[2560,128]{1,0:T(8,128)(2,1)S(1)}, bf16[48,2560]{1,0:T(8,128)(2,1)S(1)}) custom-call(bf16[8,80,128]{2,1,0:T(8,128)(2,1)S(1)} %collective-permute-done.rows_ref, bf16[16,128,128]{2,1,0:T(8,128)(2,1)S(1)} %all-to-all-done.1.cols_ref), custom_call_target="tpu_custom_call" | custom-call | tf_op jit(solution)/shard_map/away/pallas_call | solution.py:351
  39.6 3.9 %collective-permute-start.1 = (f32[8,48,128]{2,1,0:T(8,128)S(1)}, f32[8,48,128]{2,1,0:T(8,128)S(1)}, u32[]{:S(2)}, u32[]{:S(2)}) collective-permute-start(f32[8,48,128]{2,1,0:T(8,128)S(1)} %get-tuple-element.27), channel_id=1, source_target_pairs={{0,1},{1,0},{2,3},{3,2},{4,5},{5,4},{6,7},{7,6},{8,9},{9,8},{10,11... | collective-permute-start | bytes 589832 | tf_op jit(solution)/shard_map/ppermute | solution.py:348
  43.5 3.2 %home.1 = (bf16[2560,1280]{1,0:T(8,128)(2,1)S(1)}, f32[8,48,128]{2,1,0:T(8,128)S(1)}) custom-call(bf16[8,80,128]{2,1,0:T(8,128)(2,1)S(1)} %all_to_all.35.rows_ref, bf16[2560,128]{1,0:T(8,128)(2,1)S(1)} %get-tuple-element.22.left_ref, bf16[48,2560]{1,0:T(8,128)(2,1)S(1)} %get-tuple-element.23.vec_ref), custom_call_target="tpu_custom_call" | custom-call | tf_op jit(solution)/shard_map/home/pallas_call | solution.py:351
  46.7 0.0 collective-permute-done.1.other_ref
  46.8 13.4 %all_to_all.36.recv_ref = f32[8,48,128]{2,1,0:T(8,128)S(1)} all-to-all(f32[8,48,128]{2,1,0:T(8,128)S(1)} %join.1), channel_id=1, replica_groups=mesh['row'=16,'z'=8,'core'=2] {'z'}, dimensions={0} | all-to-all | bytes 393216 | tf_op jit(solution)/shard_map/all_to_all | solution.py:345
  60.2 0.4 scale.1
  60.5 12.2 %all_to_all.37.spread_ref = f32[16,48,128]{2,1,0:T(8,128)S(1)} all-to-all(f32[16,48,128]{2,1,0:T(8,128)S(1)} %get-tuple-element.28), channel_id=1, replica_groups=mesh['row'=16,'z'=8,'core'=2] {'row'}, dimensions={0} | all-to-all | bytes 786432 | tf_op jit(solution)/shard_map/all_to_all | solution.py:345
  72.7 1.3 %away_again.1 = (f32[8,48,128]{2,1,0:T(8,128)S(1)}, bf16[64,2560]{1,0:T(8,128)(2,1)S(1)}, f32[8,128]{1,0:T(8,128)S(1)}) custom-call(bf16[2560,1280]{1,0:T(8,128)(2,1)S(1)} %get-tuple-element.25.aff_ref, f32[16,48,128]{2,1,0:T(8,128)S(1)} %all_to_all.37.spread_ref), custom_call_target="tpu_custom_call" | custom-call | tf_op jit(solution)/shard_map/away_again/pallas_call | solution.py:351
  74.1 1.6 %collective-permute-start.2 = (f32[8,48,128]{2,1,0:T(8,128)S(1)}, f32[8,48,128]{2,1,0:T(8,128)S(1)}, u32[]{:S(2)}, u32[]{:S(2)}) collective-permute-start(f32[8,48,128]{2,1,0:T(8,128)S(1)} %get-tuple-element.31), channel_id=1, source_target_pairs={{0,1},{1,0},{2,3},{3,2},{4,5},{5,4},{6,7},{7,6},{8,9},{9,8},{10,11... | collective-permute-start | bytes 589832 | tf_op jit(solution)/shard_map/ppermute | solution.py:348
  75.7 1.3 %home_again.1.mine_ref = f32[8,48,128]{2,1,0:T(8,128)S(1)} custom-call(bf16[2560,1280]{1,0:T(8,128)(2,1)S(1)} %get-tuple-element.24.aff_ref, bf16[64,2560]{1,0:T(8,128)(2,1)S(1)} %get-tuple-element.29.vec_ref, f32[8,128]{1,0:T(8,128)S(1)} %get-tuple-element.30.gram_ref), custom_call_target="tpu_custom_call" | custom-call | tf_op jit(solution)/shard_map/home_again/pallas_call | solution.py:351
  77.1 0.0 collective-permute-done.2.other_ref
  77.1 13.4 %all_to_all.38.recv_ref = f32[8,48,128]{2,1,0:T(8,128)S(1)} all-to-all(f32[8,48,128]{2,1,0:T(8,128)S(1)} %join_again.1), channel_id=1, replica_groups=mesh['row'=16,'z'=8,'core'=2] {'z'}, dimensions={0} | all-to-all | bytes 393216 | tf_op jit(solution)/shard_map/all_to_all | solution.py:345
  90.5 1.0 middle.1
  91.5 9.8 %all_to_all.39.recv_ref = f32[16,8,128]{2,1,0:T(8,128)S(1)} all-to-all(f32[16,8,128]{2,1,0:T(8,128)S(1)} %get-tuple-element.33), channel_id=1, replica_groups=mesh['row'=16,'z'=8,'core'=2] {'row'}, dimensions={0} | all-to-all | bytes 131072 | tf_op jit(solution)/shard_map/all_to_all | solution.py:345
  101.3 12.1 %all_to_all.40.recv_ref = f32[16,8,128]{2,1,0:T(8,128)S(1)} all-to-all(f32[16,8,128]{2,1,0:T(8,128)S(1)} %again.1), channel_id=1, replica_groups=mesh['row'=16,'z'=8,'core'=2] {'z','core'}, dimensions={0} | all-to-all | bytes 131072 | tf_op jit(solution)/shard_map/all_to_all | solution.py:345
  113.4 1.4 %last.1 = f32[32,160]{1,0:T(8,128)} custom-call(f32[16,8,128]{2,1,0:T(8,128)S(1)} %all_to_all.40.recv_ref, f32[32,256]{1,0:T(8,128)S(1)} %get-tuple-element.34.scaled_ref), custom_call_target="tpu_custom_call" | custom-call | tf_op jit(solution)/shard_map/last/pallas_call | solution.py:351
  (5 shorter events, 0.1 us)
Async XLA Ops:
  0.0 0.8 copy-start
  0.8 0.7 copy-start.1
  19.6 15.8 %all-to-all-start.1 = ((bf16[16,128,128]{2,1,0:T(8,128)(2,1)}), bf16[16,128,128]{2,1,0:T(8,128)(2,1)S(1)}, u32[]{:S(2)}, u32[]{:S(2)}) async-start(bf16[16,128,128]{2,1,0:T(8,128)(2,1)} %get-tuple-element.21), calls=%async_computation.1 | async-start | bytes 1048576 | tf_op jit(solution)/shard_map/all_to_all | solution.py:345
  26.3 3.9 %collective-permute-start = (bf16[8,80,128]{2,1,0:T(8,128)(2,1)S(1)}, bf16[8,80,128]{2,1,0:T(8,128)(2,1)S(1)}, u32[]{:S(2)}, u32[]{:S(2)}) collective-permute-start(bf16[8,80,128]{2,1,0:T(8,128)(2,1)S(1)} %all_to_all.35.rows_ref), channel_id=1, source_target_pairs={{0,1},{1,0},{2,3},{3,2},{4,5},{5,4},{6,7},{7,6},{8,9},{9,8},{10,11... | collective-permute-start | bytes 491528 | tf_op jit(solution)/shard_map/ppermute | solution.py:348
  39.6 7.1 %collective-permute-start.1 = (f32[8,48,128]{2,1,0:T(8,128)S(1)}, f32[8,48,128]{2,1,0:T(8,128)S(1)}, u32[]{:S(2)}, u32[]{:S(2)}) collective-permute-start(f32[8,48,128]{2,1,0:T(8,128)S(1)} %get-tuple-element.27), channel_id=1, source_target_pairs={{0,1},{1,0},{2,3},{3,2},{4,5},{5,4},{6,7},{7,6},{8,9},{9,8},{10,11... | collective-permute-start | bytes 589832 | tf_op jit(solution)/shard_map/ppermute | solution.py:348
  74.1 3.0 %collective-permute-start.2 = (f32[8,48,128]{2,1,0:T(8,128)S(1)}, f32[8,48,128]{2,1,0:T(8,128)S(1)}, u32[]{:S(2)}, u32[]{:S(2)}) collective-permute-start(f32[8,48,128]{2,1,0:T(8,128)S(1)} %get-tuple-element.31), channel_id=1, source_target_pairs={{0,1},{1,0},{2,3},{3,2},{4,5},{5,4},{6,7},{7,6},{8,9},{9,8},{10,11... | collective-permute-start | bytes 589832 | tf_op jit(solution)/shard_map/ppermute | solution.py:348

commit v4 on v3

--- a/solution.py
+++ b/solution.py
@@ -89,8 +89,7 @@
     flat = jnp.concatenate([flat, jnp.zeros_like(flat)], axis=0).T
     by_point = flat[0:half] + roll(flat[half:group], features)
     main, rest = main_and_rest(vectors_ref[...].astype(F32))
-    parts = [by_point, main, rest, jnp.zeros((8, LANES), F32)]
-    copies(cols_ref, jnp.concatenate(parts, axis=0).astype(BF16))
+    copies(cols_ref, jnp.concatenate([by_point, main, rest], axis=0).astype(BF16))
 
 
 def blocks_of(count):
@@ -126,7 +125,7 @@
     for i in range(count):
         vec_ref[0:32, i * LANES : (i + 1) * LANES] = cols_ref[i, 80:112]
     for m in range(count // 4):
-        rests = [cols_ref[4 * m + q, 112:128].astype(F32)[0:8] for q in range(4)]
+        rests = [cols_ref[4 * m + q, 112:120].astype(F32) for q in range(4)]
         at = (count + m) * LANES
         vec_ref[0:32, at : at + LANES] = unfold(rests).astype(BF16)
 
@@ -187,18 +186,17 @@
 
 
 def away_body(log_scale):
-    def body(rows_ref, cols_ref, aff_ref, send_ref, left_ref, vec_ref, right_ref):
+    def body(right_ref, cols_ref, aff_ref, send_ref, left_ref, vec_ref):
         put_columns(log_scale, cols_ref, left_ref, vec_ref)
-        put_rows(log_scale, rows_ref, right_ref)
         affinity_product(left_ref, right_ref, vec_ref, aff_ref, send_ref)
 
     return body
 
 
-def home_body(log_scale):
-    def body(rows_ref, left_ref, vec_ref, aff_ref, send_ref, right_ref):
-        put_rows(log_scale, rows_ref, right_ref)
-        affinity_product(left_ref, right_ref, vec_ref, aff_ref, send_ref)
+def rows_body(log_scale):
+    def body(away_ref, home_ref, away_right_ref, home_right_ref):
+        put_rows(log_scale, away_ref, away_right_ref)
+        put_rows(log_scale, home_ref, home_right_ref)
 
     return body
 
@@ -339,6 +337,7 @@
     total = group * row * col
     log_scale = 2.0 * KERNEL_SCALE / features * math.log2(math.e)
     lanes = half * group
+    right_shape = pltpu.VMEM((256, lanes), BF16)
     shape = jax.ShapeDtypeStruct
 
     def exchange(x, axis):
@@ -361,9 +360,9 @@
     cols, rows = call(
         pack_body,
         "pack",
-        (shape((row, 128, LANES), BF16), shape((half, 80, LANES), BF16)),
-        points.T,
-        start_vectors.T,
+        (pltpu.VMEM((row, 120, LANES), BF16), pltpu.VMEM((half, 80, LANES), BF16)),
+        pltpu.with_memory_space_constraint(points.T, pltpu.HBM),
+        pltpu.with_memory_space_constraint(start_vectors.T, pltpu.HBM),
         scratch=(
             pltpu.VMEM((features, group), BF16),
             pltpu.VMEM((start_vectors.shape[1], group), BF16),
@@ -374,9 +373,11 @@
     home_rows = exchange(rows, "z")
     away_rows = swap(home_rows)
     cols = exchange(cols, "row")
+    away_right, home_right = call(
+        rows_body(log_scale), "rows", (right_shape, right_shape), away_rows, home_rows
+    )
     aff_shape = pltpu.VMEM((row * group, lanes), BF16)
     send_shape = shape((half, 48, LANES), F32)
-    right_shape = pltpu.VMEM((256, lanes), BF16)
     away_aff, away_send, left, vec = call(
         away_body(log_scale),
         "away",
@@ -386,19 +387,17 @@
             pltpu.VMEM((row * group, LANES), BF16),
             pltpu.VMEM((48, row * group), BF16),
         ),
-        away_rows,
+        away_right,
         cols,
-        scratch=(right_shape,),
     )
     other = swap(away_send)
     home_aff, home_send = call(
-        home_body(log_scale),
+        affinity_product,
         "home",
         (aff_shape, send_shape),
-        home_rows,
         left,
+        home_right,
         vec,
-        scratch=(right_shape,),
     )
     send = call(join_body, "join", send_shape, home_send, other)
     spread, degree = call(

time: 115 us -> 114 us (level)
  local copies, waits for them, and re-layouts: 1.47 us -> 0 us
    unnamed x4 -> x0, local copies, waits for them, and re-layouts: 1.47 us -> none
    pallas_call x11 -> x12, Pallas kernels: 14 us -> 14.9 us  [call(): pl.pallas_call(body, out_shape=out_shape, scratch_shapes=scratch, name=na...]
where the time goes in v4:
time: 114 us
  blocking collectives  77.8 us (68%)
  starting transfers between devices  15.3 us (13%)
  Pallas kernels  14.9 us (13%)
  waiting for transfers between devices  5.56 us (5%)
    all_to_all x6, blocking collectives, exchange(): return lax.all_to_all(x, axis, 0, 0, tiled=True)  77.8 us
    pallas_call x12, Pallas kernels, call(): pl.pallas_call(body, out_shape=out_shape, scratch_shapes=scratch, name=na...  14.9 us
    ppermute x3, starting transfers between devices, swap(): return lax.ppermute(x, 'core', [(0, 1), (1, 0)])  8.52 us
    all_to_all x1, starting transfers between devices, exchange(): return lax.all_to_all(x, axis, 0, 0, tiled=True)  6.76 us
    all_to_all x1, waiting for transfers between devices, exchange(): return lax.all_to_all(x, axis, 0, 0, tiled=True)  4.53 us
  transfers between devices with their start and end apart: 4, of which 2 were waited for; matrix products, arithmetic and copies ran while one was open for 0% of the time, Pallas kernels for 4%

profile of v4, /device:TPU:1, one launch (start us, length us, event | category | flops | bytes accessed | tf_op | source)
XLA Modules:
  0.0 113.7 jit_solution(6249090835904613203)
XLA Ops:
  0.0 1.7 %pack.1 = (bf16[16,120,128]{2,1,0:T(8,128)(2,1)}, bf16[8,80,128]{2,1,0:T(8,128)(2,1)S(1)}) custom-call(bf16[64,160]{1,0:T(8,128)(2,1)} %bitcast.3, bf16[32,160]{1,0:T(8,128)(2,1)} %bitcast.4), custom_call_target="tpu_custom_call" | custom-call | tf_op jit(solution)/shard_map/pack/pallas_call | solution.py:350
  1.8 17.0 %all_to_all.35.home_ref = bf16[8,80,128]{2,1,0:T(8,128)(2,1)S(1)} all-to-all(bf16[8,80,128]{2,1,0:T(8,128)(2,1)S(1)} %get-tuple-element.22), channel_id=1, replica_groups=mesh['row'=16,'z'=8,'core'=2] {'z'}, dimensions={0} | all-to-all | bytes 327680 | tf_op jit(solution)/shard_map/all_to_all | solution.py:344
  18.8 6.8 %all-to-all-start.1 = ((bf16[16,120,128]{2,1,0:T(8,128)(2,1)}), bf16[16,120,128]{2,1,0:T(8,128)(2,1)S(1)}, u32[]{:S(2)}, u32[]{:S(2)}) async-start(bf16[16,120,128]{2,1,0:T(8,128)(2,1)} %get-tuple-element.24), calls=%async_computation.1 | async-start | bytes 983040 | tf_op jit(solution)/shard_map/all_to_all | solution.py:344
  25.5 2.9 %collective-permute-start = (bf16[8,80,128]{2,1,0:T(8,128)(2,1)S(1)}, bf16[8,80,128]{2,1,0:T(8,128)(2,1)S(1)}, u32[]{:S(2)}, u32[]{:S(2)}) collective-permute-start(bf16[8,80,128]{2,1,0:T(8,128)(2,1)S(1)} %all_to_all.35.home_ref), channel_id=1, source_target_pairs={{0,1},{1,0},{2,3},{3,2},{4,5},{5,4},{6,7},{7,6},{8,9},{9,8},{10,11... | collective-permute-start | bytes 491528 | tf_op jit(solution)/shard_map/ppermute | solution.py:347
  28.4 1.0 collective-permute-done.away_ref
  29.4 0.3 rows.1
  29.8 4.5 %all-to-all-done.1.cols_ref = bf16[16,120,128]{2,1,0:T(8,128)(2,1)S(1)} async-done(((bf16[16,120,128]{2,1,0:T(8,128)(2,1)}), bf16[16,120,128]{2,1,0:T(8,128)(2,1)S(1)}, u32[]{:S(2)}, u32[]{:S(2)}) %all-to-all-start.1) | async-done | bytes 491552 | tf_op jit(solution)/shard_map/all_to_all | solution.py:344
  34.3 4.2 %away.1 = (bf16[2560,1280]{1,0:T(8,128)(2,1)S(1)}, f32[8,48,128]{2,1,0:T(8,128)S(1)}, bf16[2560,128]{1,0:T(8,128)(2,1)S(1)}, bf16[48,2560]{1,0:T(8,128)(2,1)S(1)}) custom-call(bf16[256,1280]{1,0:T(8,128)(2,1)S(1)} %get-tuple-element.23.right_ref, bf16[16,120,128]{2,1,0:T(8,128)(2,1)S(1)} %all-to-all-done.1.cols_ref), custom_call_target="tpu_custom_call" | custom-call | tf_op jit(solution)/shard_map/away/pallas_call | solution.py:350
  38.5 4.0 %collective-permute-start.1 = (f32[8,48,128]{2,1,0:T(8,128)S(1)}, f32[8,48,128]{2,1,0:T(8,128)S(1)}, u32[]{:S(2)}, u32[]{:S(2)}) collective-permute-start(f32[8,48,128]{2,1,0:T(8,128)S(1)} %get-tuple-element.31), channel_id=1, source_target_pairs={{0,1},{1,0},{2,3},{3,2},{4,5},{5,4},{6,7},{7,6},{8,9},{9,8},{10,11... | collective-permute-start | bytes 589832 | tf_op jit(solution)/shard_map/ppermute | solution.py:347
  42.5 3.1 %home.1 = (bf16[2560,1280]{1,0:T(8,128)(2,1)S(1)}, f32[8,48,128]{2,1,0:T(8,128)S(1)}) custom-call(bf16[2560,128]{1,0:T(8,128)(2,1)S(1)} %get-tuple-element.25.left_ref, bf16[256,1280]{1,0:T(8,128)(2,1)S(1)} %get-tuple-element.26.right_ref, bf16[48,2560]{1,0:T(8,128)(2,1)S(1)} %get-tuple-element.27.vec_ref), custom_call_target="tpu_custom_call" | custom-call | tf_op jit(solution)/shard_map/home/pallas_call | solution.py:350
  45.6 0.0 collective-permute-done.1.other_ref
  45.7 13.4 %all_to_all.36.recv_ref = f32[8,48,128]{2,1,0:T(8,128)S(1)} all-to-all(f32[8,48,128]{2,1,0:T(8,128)S(1)} %join.1), channel_id=1, replica_groups=mesh['row'=16,'z'=8,'core'=2] {'z'}, dimensions={0} | all-to-all | bytes 393216 | tf_op jit(solution)/shard_map/all_to_all | solution.py:344
  59.1 0.4 scale.1
  59.4 12.2 %all_to_all.37.spread_ref = f32[16,48,128]{2,1,0:T(8,128)S(1)} all-to-all(f32[16,48,128]{2,1,0:T(8,128)S(1)} %get-tuple-element.32), channel_id=1, replica_groups=mesh['row'=16,'z'=8,'core'=2] {'row'}, dimensions={0} | all-to-all | bytes 786432 | tf_op jit(solution)/shard_map/all_to_all | solution.py:344
  71.6 1.3 %away_again.1 = (f32[8,48,128]{2,1,0:T(8,128)S(1)}, bf16[64,2560]{1,0:T(8,128)(2,1)S(1)}, f32[8,128]{1,0:T(8,128)S(1)}) custom-call(bf16[2560,1280]{1,0:T(8,128)(2,1)S(1)} %get-tuple-element.29.aff_ref, f32[16,48,128]{2,1,0:T(8,128)S(1)} %all_to_all.37.spread_ref), custom_call_target="tpu_custom_call" | custom-call | tf_op jit(solution)/shard_map/away_again/pallas_call | solution.py:350
  73.0 1.6 %collective-permute-start.2 = (f32[8,48,128]{2,1,0:T(8,128)S(1)}, f32[8,48,128]{2,1,0:T(8,128)S(1)}, u32[]{:S(2)}, u32[]{:S(2)}) collective-permute-start(f32[8,48,128]{2,1,0:T(8,128)S(1)} %get-tuple-element.35), channel_id=1, source_target_pairs={{0,1},{1,0},{2,3},{3,2},{4,5},{5,4},{6,7},{7,6},{8,9},{9,8},{10,11... | collective-permute-start | bytes 589832 | tf_op jit(solution)/shard_map/ppermute | solution.py:347
  74.6 1.3 %home_again.1.mine_ref = f32[8,48,128]{2,1,0:T(8,128)S(1)} custom-call(bf16[2560,1280]{1,0:T(8,128)(2,1)S(1)} %get-tuple-element.28.aff_ref, bf16[64,2560]{1,0:T(8,128)(2,1)S(1)} %get-tuple-element.33.vec_ref, f32[8,128]{1,0:T(8,128)S(1)} %get-tuple-element.34.gram_ref), custom_call_target="tpu_custom_call" | custom-call | tf_op jit(solution)/shard_map/home_again/pallas_call | solution.py:350
  75.9 0.0 collective-permute-done.2.other_ref
  76.0 13.4 %all_to_all.38.recv_ref = f32[8,48,128]{2,1,0:T(8,128)S(1)} all-to-all(f32[8,48,128]{2,1,0:T(8,128)S(1)} %join_again.1), channel_id=1, replica_groups=mesh['row'=16,'z'=8,'core'=2] {'z'}, dimensions={0} | all-to-all | bytes 393216 | tf_op jit(solution)/shard_map/all_to_all | solution.py:344
  89.4 1.0 middle.1
  90.4 9.8 %all_to_all.39.recv_ref = f32[16,8,128]{2,1,0:T(8,128)S(1)} all-to-all(f32[16,8,128]{2,1,0:T(8,128)S(1)} %get-tuple-element.37), channel_id=1, replica_groups=mesh['row'=16,'z'=8,'core'=2] {'row'}, dimensions={0} | all-to-all | bytes 131072 | tf_op jit(solution)/shard_map/all_to_all | solution.py:344
  100.2 12.1 %all_to_all.40.recv_ref = f32[16,8,128]{2,1,0:T(8,128)S(1)} all-to-all(f32[16,8,128]{2,1,0:T(8,128)S(1)} %again.1), channel_id=1, replica_groups=mesh['row'=16,'z'=8,'core'=2] {'z','core'}, dimensions={0} | all-to-all | bytes 131072 | tf_op jit(solution)/shard_map/all_to_all | solution.py:344
  112.3 1.4 %last.1 = f32[32,160]{1,0:T(8,128)} custom-call(f32[16,8,128]{2,1,0:T(8,128)S(1)} %all_to_all.40.recv_ref, f32[32,256]{1,0:T(8,128)S(1)} %get-tuple-element.38.scaled_ref), custom_call_target="tpu_custom_call" | custom-call | tf_op jit(solution)/shard_map/last/pallas_call | solution.py:350
  (3 shorter events, 0.1 us)
Async XLA Ops:
  18.8 15.5 %all-to-all-start.1 = ((bf16[16,120,128]{2,1,0:T(8,128)(2,1)}), bf16[16,120,128]{2,1,0:T(8,128)(2,1)S(1)}, u32[]{:S(2)}, u32[]{:S(2)}) async-start(bf16[16,120,128]{2,1,0:T(8,128)(2,1)} %get-tuple-element.24), calls=%async_computation.1 | async-start | bytes 983040 | tf_op jit(solution)/shard_map/all_to_all | solution.py:344
  25.5 3.9 %collective-permute-start = (bf16[8,80,128]{2,1,0:T(8,128)(2,1)S(1)}, bf16[8,80,128]{2,1,0:T(8,128)(2,1)S(1)}, u32[]{:S(2)}, u32[]{:S(2)}) collective-permute-start(bf16[8,80,128]{2,1,0:T(8,128)(2,1)S(1)} %all_to_all.35.home_ref), channel_id=1, source_target_pairs={{0,1},{1,0},{2,3},{3,2},{4,5},{5,4},{6,7},{7,6},{8,9},{9,8},{10,11... | collective-permute-start | bytes 491528 | tf_op jit(solution)/shard_map/ppermute | solution.py:347
  38.5 7.1 %collective-permute-start.1 = (f32[8,48,128]{2,1,0:T(8,128)S(1)}, f32[8,48,128]{2,1,0:T(8,128)S(1)}, u32[]{:S(2)}, u32[]{:S(2)}) collective-permute-start(f32[8,48,128]{2,1,0:T(8,128)S(1)} %get-tuple-element.31), channel_id=1, source_target_pairs={{0,1},{1,0},{2,3},{3,2},{4,5},{5,4},{6,7},{7,6},{8,9},{9,8},{10,11... | collective-permute-start | bytes 589832 | tf_op jit(solution)/shard_map/ppermute | solution.py:347
  73.0 3.0 %collective-permute-start.2 = (f32[8,48,128]{2,1,0:T(8,128)S(1)}, f32[8,48,128]{2,1,0:T(8,128)S(1)}, u32[]{:S(2)}, u32[]{:S(2)}) collective-permute-start(f32[8,48,128]{2,1,0:T(8,128)S(1)} %get-tuple-element.35), channel_id=1, source_target_pairs={{0,1},{1,0},{2,3},{3,2},{4,5},{5,4},{6,7},{7,6},{8,9},{9,8},{10,11... | collective-permute-start | bytes 589832 | tf_op jit(solution)/shard_map/ppermute | solution.py:347

commit v5 on v4

--- a/solution.py
+++ b/solution.py
@@ -82,7 +82,7 @@
         load.wait()
     pts = points_ref[...].astype(F32)
     main, rest = main_and_rest(pts)
-    copies(rows_ref, jnp.concatenate([main, rest], axis=0).astype(BF16))
+    rows_ref[...] = jnp.concatenate([main, rest], axis=0).astype(BF16)
     features, group = pts.shape
     half = group // 2
     flat = jnp.concatenate([main, widen(pts[:, LANES:])], axis=1)
@@ -201,6 +201,14 @@
     return body
 
 
+def order_body(*refs):
+    out_ref = refs[-1]
+    count = len(refs) - 1
+    here = lax.axis_index("z")
+    for t in range(count):
+        out_ref[lax.rem(here + count - t, count)] = refs[t][...]
+
+
 def join_body(mine_ref, other_ref, out_ref):
     out_ref[...] = mine_ref[...] + other_ref[...]
 
@@ -346,21 +354,15 @@
     def swap(x):
         return lax.ppermute(x, "core", [(0, 1), (1, 0)])
 
-    def call(body, name, out_shape, *args, scratch=(), **kwargs):
+    def call(body, out_shape, *args, scratch=(), **kwargs):
         return pl.pallas_call(
-            body,
-            out_shape=out_shape,
-            scratch_shapes=scratch,
-            name=name,
-            compiler_params=PARAMS,
-            **kwargs,
+            body, out_shape=out_shape, scratch_shapes=scratch, compiler_params=PARAMS, **kwargs
         )(*args)
 
     hbm_space = pl.BlockSpec(memory_space=pltpu.HBM)
     cols, rows = call(
         pack_body,
-        "pack",
-        (pltpu.VMEM((row, 120, LANES), BF16), pltpu.VMEM((half, 80, LANES), BF16)),
+        (pltpu.VMEM((row, 120, LANES), BF16), pltpu.VMEM((80, LANES), BF16)),
         pltpu.with_memory_space_constraint(points.T, pltpu.HBM),
         pltpu.with_memory_space_constraint(start_vectors.T, pltpu.HBM),
         scratch=(
@@ -370,17 +372,23 @@
         ),
         in_specs=[hbm_space, hbm_space],
     )
-    home_rows = exchange(rows, "z")
+    forth = [(i, (i + 1) % half) for i in range(half)]
+    back = [(i, (i - 1) % half) for i in range(half)]
+    cols = exchange(cols, "row")
+    ahead, behind = [rows], [rows]
+    for _ in range(half // 2):
+        behind.append(lax.ppermute(behind[-1], "z", forth))
+        if len(behind) + len(ahead) - 1 < half:
+            ahead.append(lax.ppermute(ahead[-1], "z", back))
+    home_rows = call(order_body, pltpu.VMEM((half, 80, LANES), BF16), *behind, *ahead[:0:-1])
     away_rows = swap(home_rows)
-    cols = exchange(cols, "row")
     away_right, home_right = call(
-        rows_body(log_scale), "rows", (right_shape, right_shape), away_rows, home_rows
+        rows_body(log_scale), (right_shape, right_shape), away_rows, home_rows
     )
     aff_shape = pltpu.VMEM((row * group, lanes), BF16)
     send_shape = shape((half, 48, LANES), F32)
     away_aff, away_send, left, vec = call(
         away_body(log_scale),
-        "away",
         (
             aff_shape,
             send_shape,
@@ -391,46 +399,28 @@
         cols,
     )
     other = swap(away_send)
-    home_aff, home_send = call(
-        affinity_product,
-        "home",
-        (aff_shape, send_shape),
-        left,
-        home_right,
-        vec,
-    )
-    send = call(join_body, "join", send_shape, home_send, other)
+    home_aff, home_send = call(affinity_product, (aff_shape, send_shape), left, home_right, vec)
+    send = call(join_body, send_shape, home_send, other)
     spread, degree = call(
-        scale_body,
-        "scale",
-        (shape((row, 48, LANES), F32), shape((16, LANES), F32)),
-        exchange(send, "z"),
+        scale_body, (shape((row, 48, LANES), F32), shape((16, LANES), F32)), exchange(send, "z")
     )
     away_send, vec, gram = call(
         away_again_body,
-        "away_again",
         (send_shape, pltpu.VMEM((64, row * group), BF16), pltpu.VMEM((8, LANES), F32)),
         away_aff,
         exchange(spread, "row"),
     )
     other = swap(away_send)
-    home_send = call(home_again_body, "home_again", send_shape, home_aff, vec, gram)
-    send = call(join_body, "join_again", send_shape, home_send, other)
+    home_send = call(home_again_body, send_shape, home_aff, vec, gram)
+    send = call(join_body, send_shape, home_send, other)
     scaled, gram = call(
         middle_body(total),
-        "middle",
         (shape((32, 2 * LANES), F32), shape((row, 8, LANES), F32)),
         exchange(send, "z"),
         degree,
     )
-    gram = call(again_body, "again", shape((col, 8, LANES), F32), exchange(gram, "row"))
-    out = call(
-        last_body(total),
-        "last",
-        shape((32, group), F32),
-        exchange(gram, ("z", "core")),
-        scaled,
-    )
+    gram = call(again_body, shape((col, 8, LANES), F32), exchange(gram, "row"))
+    out = call(last_body(total), shape((32, group), F32), exchange(gram, ("z", "core")), scaled)
     return out.T
 
 

time: 114 us -> 117 us (1.026)
  blocking collectives: 77.8 us -> 65.1 us
  starting transfers between devices: 15.3 us -> 27.2 us
  waiting for transfers between devices: 5.56 us -> 8.88 us
    all_to_all x6 -> x5, blocking collectives: 77.8 us -> 65.1 us  [exchange(): return lax.all_to_all(x, axis, 0, 0, tiled=True)]
    ppermute x0 -> x7, starting transfers between devices: none -> 11.1 us  [the longest x3 9.38 us: shards(): ahead.append(lax.ppermute(ahead[-1], 'z', back))]
    ppermute x0 -> x7, waiting for transfers between devices: none -> 7.84 us  [the longest x4 7.83 us: shards(): behind.append(lax.ppermute(behind[-1], 'z', forth))]
    all_to_all x1, waiting for transfers between devices: 4.53 us -> 0.01 us  [exchange(): return lax.all_to_all(x, axis, 0, 0, tiled=True)]
    pallas_call x12 -> x13, Pallas kernels: 14.9 us -> 15 us  [call(): pl.pallas_call(body, out_shape=out_shape, scratch_shapes=scratch, compile...]
  transfers between devices with their start and end apart: 4 -> 11, of which waited for: 2 -> 5; matrix products, arithmetic and copies ran while one was open for 0% -> 0% of each run, Pallas kernels for 4% -> 4%
where the time goes in v5:
time: 117 us; the launch traced here: 116 us
  blocking collectives  65.1 us (56%)
  starting transfers between devices  27.2 us (23%)
  Pallas kernels  15 us (13%)
  waiting for transfers between devices  8.88 us (8%)
    all_to_all x5, blocking collectives, exchange(): return lax.all_to_all(x, axis, 0, 0, tiled=True)  65.1 us
    pallas_call x13, Pallas kernels, call(): pl.pallas_call(body, out_shape=out_shape, scratch_shapes=scratch, compile...  15 us
    ppermute x3, starting transfers between devices, shards(): ahead.append(lax.ppermute(ahead[-1], 'z', back))  9.38 us
    ppermute x3, starting transfers between devices, swap(): return lax.ppermute(x, 'core', [(0, 1), (1, 0)])  8.52 us
    ppermute x4, waiting for transfers between devices, shards(): behind.append(lax.ppermute(behind[-1], 'z', forth))  7.83 us
    all_to_all x1, starting transfers between devices, exchange(): return lax.all_to_all(x, axis, 0, 0, tiled=True)  7.58 us
  transfers between devices with their start and end apart: 11, of which 5 were waited for; matrix products, arithmetic and copies ran while one was open for 0% of the time, Pallas kernels for 4%

profile of v5, /device:TPU:1, one launch (start us, length us, event | category | flops | bytes accessed | tf_op | source)
XLA Modules:
  0.0 116.2 jit_solution(12338035306430305968)
XLA Ops:
  0.0 1.7 %shard_map.28 = (bf16[16,120,128]{2,1,0:T(8,128)(2,1)}, bf16[80,128]{1,0:T(8,128)(2,1)S(1)}) custom-call(bf16[64,160]{1,0:T(8,128)(2,1)} %bitcast.3, bf16[32,160]{1,0:T(8,128)(2,1)} %bitcast.4), custom_call_target="tpu_custom_call" | custom-call | tf_op jit(solution)/shard_map/pallas_call | solution.py:358
  1.7 7.6 %all-to-all-start = ((bf16[16,120,128]{2,1,0:T(8,128)(2,1)}), bf16[16,120,128]{2,1,0:T(8,128)(2,1)S(1)}, u32[]{:S(2)}, u32[]{:S(2)}) async-start(bf16[16,120,128]{2,1,0:T(8,128)(2,1)} %get-tuple-element.24), calls=%async_computation | async-start | bytes 983040 | tf_op jit(solution)/shard_map/all_to_all | solution.py:352
  9.3 1.7 %collective-permute-start = (bf16[80,128]{1,0:T(8,128)(2,1)S(1)}, bf16[80,128]{1,0:T(8,128)(2,1)S(1)}, u32[]{:S(2)}, u32[]{:S(2)}) collective-permute-start(bf16[80,128]{1,0:T(8,128)(2,1)S(1)} %get-tuple-element.22.refs_0_), channel_id=1, source_target_pairs={{0,2},{2,4},{4,6},{6,8},{8,10},{10,12},{12,14},{14,0},{1,3},{3,5},... | collective-permute-start | bytes 61448 | tf_op jit(solution)/shard_map/ppermute | solution.py:380
  11.1 4.0 %collective-permute-start.4 = (bf16[80,128]{1,0:T(8,128)(2,1)S(1)}, bf16[80,128]{1,0:T(8,128)(2,1)S(1)}, u32[]{:S(2)}, u32[]{:S(2)}) collective-permute-start(bf16[80,128]{1,0:T(8,128)(2,1)S(1)} %get-tuple-element.22.refs_0_), channel_id=1, source_target_pairs={{0,14},{2,0},{4,2},{6,4},{8,6},{10,8},{12,10},{14,12},{1,15},{3,1}... | collective-permute-start | bytes 61448 | tf_op jit(solution)/shard_map/ppermute | solution.py:382
  15.1 1.4 %collective-permute-done.refs_1_ = bf16[80,128]{1,0:T(8,128)(2,1)S(1)} collective-permute-done((bf16[80,128]{1,0:T(8,128)(2,1)S(1)}, bf16[80,128]{1,0:T(8,128)(2,1)S(1)}, u32[]{:S(2)}, u32[]{:S(2)}) %collective-permute-start) | collective-permute-done | bytes 20512 | tf_op jit(solution)/shard_map/ppermute | solution.py:380
  16.5 2.7 %collective-permute-start.5 = (bf16[80,128]{1,0:T(8,128)(2,1)S(1)}, bf16[80,128]{1,0:T(8,128)(2,1)S(1)}, u32[]{:S(2)}, u32[]{:S(2)}) collective-permute-start(bf16[80,128]{1,0:T(8,128)(2,1)S(1)} %collective-permute-done.4.refs_7_), channel_id=1, source_target_pairs={{0,14},{2,0},{4,2},{6,4},{8,6},{10,8},{12,10},{14,12},{1,15},{3,1}... | collective-permute-start | bytes 61448 | tf_op jit(solution)/shard_map/ppermute | solution.py:382
  19.1 1.5 %collective-permute-done.1.refs_2_ = bf16[80,128]{1,0:T(8,128)(2,1)S(1)} collective-permute-done((bf16[80,128]{1,0:T(8,128)(2,1)S(1)}, bf16[80,128]{1,0:T(8,128)(2,1)S(1)}, u32[]{:S(2)}, u32[]{:S(2)}) %collective-permute-start.1) | collective-permute-done | bytes 20512 | tf_op jit(solution)/shard_map/ppermute | solution.py:380
  20.6 2.7 %collective-permute-start.6 = (bf16[80,128]{1,0:T(8,128)(2,1)S(1)}, bf16[80,128]{1,0:T(8,128)(2,1)S(1)}, u32[]{:S(2)}, u32[]{:S(2)}) collective-permute-start(bf16[80,128]{1,0:T(8,128)(2,1)S(1)} %collective-permute-done.5.refs_6_), channel_id=1, source_target_pairs={{0,14},{2,0},{4,2},{6,4},{8,6},{10,8},{12,10},{14,12},{1,15},{3,1}... | collective-permute-start | bytes 61448 | tf_op jit(solution)/shard_map/ppermute | solution.py:382
  23.3 1.2 %collective-permute-done.2.refs_3_ = bf16[80,128]{1,0:T(8,128)(2,1)S(1)} collective-permute-done((bf16[80,128]{1,0:T(8,128)(2,1)S(1)}, bf16[80,128]{1,0:T(8,128)(2,1)S(1)}, u32[]{:S(2)}, u32[]{:S(2)}) %collective-permute-start.2) | collective-permute-done | bytes 20512 | tf_op jit(solution)/shard_map/ppermute | solution.py:380
  24.5 3.8 %collective-permute-done.3.refs_4_ = bf16[80,128]{1,0:T(8,128)(2,1)S(1)} collective-permute-done((bf16[80,128]{1,0:T(8,128)(2,1)S(1)}, bf16[80,128]{1,0:T(8,128)(2,1)S(1)}, u32[]{:S(2)}, u32[]{:S(2)}) %collective-permute-start.3) | collective-permute-done | bytes 20512 | tf_op jit(solution)/shard_map/ppermute | solution.py:380
  28.3 4.8 %collective-permute-start.7 = (bf16[8,80,128]{2,1,0:T(8,128)(2,1)S(1)}, bf16[8,80,128]{2,1,0:T(8,128)(2,1)S(1)}, u32[]{:S(2)}, u32[]{:S(2)}) collective-permute-start(bf16[8,80,128]{2,1,0:T(8,128)(2,1)S(1)} %shard_map.29.home_ref), channel_id=1, source_target_pairs={{0,1},{1,0},{2,3},{3,2},{4,5},{5,4},{6,7},{7,6},{8,9},{9,8},{10,11... | collective-permute-start | bytes 491528 | tf_op jit(solution)/shard_map/ppermute | solution.py:355
  33.1 1.0 collective-permute-done.7.away_ref
  34.5 4.2 %shard_map.31 = (bf16[2560,1280]{1,0:T(8,128)(2,1)S(1)}, f32[8,48,128]{2,1,0:T(8,128)S(1)}, bf16[2560,128]{1,0:T(8,128)(2,1)S(1)}, bf16[48,2560]{1,0:T(8,128)(2,1)S(1)}) custom-call(bf16[256,1280]{1,0:T(8,128)(2,1)S(1)} %get-tuple-element.23.right_ref, bf16[16,120,128]{2,1,0:T(8,128)(2,1)S(1)} %all-to-all-done.cols_ref), custom_call_target="tpu_custom_call" | custom-call | tf_op jit(solution)/shard_map/pallas_call | solution.py:358
  39.3 3.1 %shard_map.32 = (bf16[2560,1280]{1,0:T(8,128)(2,1)S(1)}, f32[8,48,128]{2,1,0:T(8,128)S(1)}) custom-call(bf16[2560,128]{1,0:T(8,128)(2,1)S(1)} %get-tuple-element.25.left_ref, bf16[256,1280]{1,0:T(8,128)(2,1)S(1)} %get-tuple-element.26.right_ref, bf16[48,2560]{1,0:T(8,128)(2,1)S(1)} %get-tuple-element.27.vec_ref), custom_call_target="tpu_custom_call" | custom-call | tf_op jit(solution)/shard_map/pallas_call | solution.py:358
  42.5 15.2 %all_to_all.30.recv_ref = f32[8,48,128]{2,1,0:T(8,128)S(1)} all-to-all(f32[8,48,128]{2,1,0:T(8,128)S(1)} %shard_map.33), channel_id=1, replica_groups=mesh['row'=16,'z'=8,'core'=2] {'z'}, dimensions={0} | all-to-all | bytes 393216 | tf_op jit(solution)/shard_map/all_to_all | solution.py:352
  58.0 14.7 %all_to_all.31.spread_ref = f32[16,48,128]{2,1,0:T(8,128)S(1)} all-to-all(f32[16,48,128]{2,1,0:T(8,128)S(1)} %get-tuple-element.32), channel_id=1, replica_groups=mesh['row'=16,'z'=8,'core'=2] {'row'}, dimensions={0} | all-to-all | bytes 786432 | tf_op jit(solution)/shard_map/all_to_all | solution.py:352
  72.7 1.3 %shard_map.35 = (f32[8,48,128]{2,1,0:T(8,128)S(1)}, bf16[64,2560]{1,0:T(8,128)(2,1)S(1)}, f32[8,128]{1,0:T(8,128)S(1)}) custom-call(bf16[2560,1280]{1,0:T(8,128)(2,1)S(1)} %get-tuple-element.29.aff_ref, f32[16,48,128]{2,1,0:T(8,128)S(1)} %all_to_all.31.spread_ref), custom_call_target="tpu_custom_call" | custom-call | tf_op jit(solution)/shard_map/pallas_call | solution.py:358
  74.0 3.1 %collective-permute-start.9 = (f32[8,48,128]{2,1,0:T(8,128)S(1)}, f32[8,48,128]{2,1,0:T(8,128)S(1)}, u32[]{:S(2)}, u32[]{:S(2)}) collective-permute-start(f32[8,48,128]{2,1,0:T(8,128)S(1)} %get-tuple-element.35), channel_id=1, source_target_pairs={{0,1},{1,0},{2,3},{3,2},{4,5},{5,4},{6,7},{7,6},{8,9},{9,8},{10,11... | collective-permute-start | bytes 589832 | tf_op jit(solution)/shard_map/ppermute | solution.py:355
  77.1 1.3 %shard_map.36.mine_ref = f32[8,48,128]{2,1,0:T(8,128)S(1)} custom-call(bf16[2560,1280]{1,0:T(8,128)(2,1)S(1)} %get-tuple-element.28.aff_ref, bf16[64,2560]{1,0:T(8,128)(2,1)S(1)} %get-tuple-element.33.vec_ref, f32[8,128]{1,0:T(8,128)S(1)} %get-tuple-element.34.gram_ref), custom_call_target="tpu_custom_call" | custom-call | tf_op jit(solution)/shard_map/pallas_call | solution.py:358
  78.5 13.4 %all_to_all.32.recv_ref = f32[8,48,128]{2,1,0:T(8,128)S(1)} all-to-all(f32[8,48,128]{2,1,0:T(8,128)S(1)} %shard_map.37), channel_id=1, replica_groups=mesh['row'=16,'z'=8,'core'=2] {'z'}, dimensions={0} | all-to-all | bytes 393216 | tf_op jit(solution)/shard_map/all_to_all | solution.py:352
  91.9 1.0 shard_map.38
  92.9 9.8 %all_to_all.33.recv_ref = f32[16,8,128]{2,1,0:T(8,128)S(1)} all-to-all(f32[16,8,128]{2,1,0:T(8,128)S(1)} %get-tuple-element.37), channel_id=1, replica_groups=mesh['row'=16,'z'=8,'core'=2] {'row'}, dimensions={0} | all-to-all | bytes 131072 | tf_op jit(solution)/shard_map/all_to_all | solution.py:352
  102.7 12.1 %all_to_all.34.recv_ref = f32[16,8,128]{2,1,0:T(8,128)S(1)} all-to-all(f32[16,8,128]{2,1,0:T(8,128)S(1)} %shard_map.39), channel_id=1, replica_groups=mesh['row'=16,'z'=8,'core'=2] {'z','core'}, dimensions={0} | all-to-all | bytes 131072 | tf_op jit(solution)/shard_map/all_to_all | solution.py:352
  114.8 1.4 %shard_map.40 = f32[32,160]{1,0:T(8,128)} custom-call(f32[16,8,128]{2,1,0:T(8,128)S(1)} %all_to_all.34.recv_ref, f32[32,256]{1,0:T(8,128)S(1)} %get-tuple-element.38.scaled_ref), custom_call_target="tpu_custom_call" | custom-call | tf_op jit(solution)/shard_map/pallas_call | solution.py:358
  (16 shorter events, 1.5 us)
Async XLA Ops:
  1.7 32.7 %all-to-all-start = ((bf16[16,120,128]{2,1,0:T(8,128)(2,1)}), bf16[16,120,128]{2,1,0:T(8,128)(2,1)S(1)}, u32[]{:S(2)}, u32[]{:S(2)}) async-start(bf16[16,120,128]{2,1,0:T(8,128)(2,1)} %get-tuple-element.24), calls=%async_computation | async-start | bytes 983040 | tf_op jit(solution)/shard_map/all_to_all | solution.py:352
  9.3 7.1 %collective-permute-start = (bf16[80,128]{1,0:T(8,128)(2,1)S(1)}, bf16[80,128]{1,0:T(8,128)(2,1)S(1)}, u32[]{:S(2)}, u32[]{:S(2)}) collective-permute-start(bf16[80,128]{1,0:T(8,128)(2,1)S(1)} %get-tuple-element.22.refs_0_), channel_id=1, source_target_pairs={{0,2},{2,4},{4,6},{6,8},{8,10},{10,12},{12,14},{14,0},{1,3},{3,5},... | collective-permute-start | bytes 61448 | tf_op jit(solution)/shard_map/ppermute | solution.py:380
  11.1 5.4 %collective-permute-start.4 = (bf16[80,128]{1,0:T(8,128)(2,1)S(1)}, bf16[80,128]{1,0:T(8,128)(2,1)S(1)}, u32[]{:S(2)}, u32[]{:S(2)}) collective-permute-start(bf16[80,128]{1,0:T(8,128)(2,1)S(1)} %get-tuple-element.22.refs_0_), channel_id=1, source_target_pairs={{0,14},{2,0},{4,2},{6,4},{8,6},{10,8},{12,10},{14,12},{1,15},{3,1}... | collective-permute-start | bytes 61448 | tf_op jit(solution)/shard_map/ppermute | solution.py:382
  16.5 4.1 %collective-permute-start.1 = (bf16[80,128]{1,0:T(8,128)(2,1)S(1)}, bf16[80,128]{1,0:T(8,128)(2,1)S(1)}, u32[]{:S(2)}, u32[]{:S(2)}) collective-permute-start(bf16[80,128]{1,0:T(8,128)(2,1)S(1)} %collective-permute-done.refs_1_), channel_id=1, source_target_pairs={{0,2},{2,4},{4,6},{6,8},{8,10},{10,12},{12,14},{14,0},{1,3},{3,5},... | collective-permute-start | bytes 61448 | tf_op jit(solution)/shard_map/ppermute | solution.py:380
  16.5 4.1 %collective-permute-start.5 = (bf16[80,128]{1,0:T(8,128)(2,1)S(1)}, bf16[80,128]{1,0:T(8,128)(2,1)S(1)}, u32[]{:S(2)}, u32[]{:S(2)}) collective-permute-start(bf16[80,128]{1,0:T(8,128)(2,1)S(1)} %collective-permute-done.4.refs_7_), channel_id=1, source_target_pairs={{0,14},{2,0},{4,2},{6,4},{8,6},{10,8},{12,10},{14,12},{1,15},{3,1}... | collective-permute-start | bytes 61448 | tf_op jit(solution)/shard_map/ppermute | solution.py:382
  20.6 3.8 %collective-permute-start.2 = (bf16[80,128]{1,0:T(8,128)(2,1)S(1)}, bf16[80,128]{1,0:T(8,128)(2,1)S(1)}, u32[]{:S(2)}, u32[]{:S(2)}) collective-permute-start(bf16[80,128]{1,0:T(8,128)(2,1)S(1)} %collective-permute-done.1.refs_2_), channel_id=1, source_target_pairs={{0,2},{2,4},{4,6},{6,8},{8,10},{10,12},{12,14},{14,0},{1,3},{3,5},... | collective-permute-start | bytes 61448 | tf_op jit(solution)/shard_map/ppermute | solution.py:380
  20.6 3.8 %collective-permute-start.6 = (bf16[80,128]{1,0:T(8,128)(2,1)S(1)}, bf16[80,128]{1,0:T(8,128)(2,1)S(1)}, u32[]{:S(2)}, u32[]{:S(2)}) collective-permute-start(bf16[80,128]{1,0:T(8,128)(2,1)S(1)} %collective-permute-done.5.refs_6_), channel_id=1, source_target_pairs={{0,14},{2,0},{4,2},{6,4},{8,6},{10,8},{12,10},{14,12},{1,15},{3,1}... | collective-permute-start | bytes 61448 | tf_op jit(solution)/shard_map/ppermute | solution.py:382
  24.4 3.8 %collective-permute-start.3 = (bf16[80,128]{1,0:T(8,128)(2,1)S(1)}, bf16[80,128]{1,0:T(8,128)(2,1)S(1)}, u32[]{:S(2)}, u32[]{:S(2)}) collective-permute-start(bf16[80,128]{1,0:T(8,128)(2,1)S(1)} %collective-permute-done.2.refs_3_), channel_id=1, source_target_pairs={{0,2},{2,4},{4,6},{6,8},{8,10},{10,12},{12,14},{14,0},{1,3},{3,5},... | collective-permute-start | bytes 61448 | tf_op jit(solution)/shard_map/ppermute | solution.py:380
  28.3 5.8 %collective-permute-start.7 = (bf16[8,80,128]{2,1,0:T(8,128)(2,1)S(1)}, bf16[8,80,128]{2,1,0:T(8,128)(2,1)S(1)}, u32[]{:S(2)}, u32[]{:S(2)}) collective-permute-start(bf16[8,80,128]{2,1,0:T(8,128)(2,1)S(1)} %shard_map.29.home_ref), channel_id=1, source_target_pairs={{0,1},{1,0},{2,3},{3,2},{4,5},{5,4},{6,7},{7,6},{8,9},{9,8},{10,11... | collective-permute-start | bytes 491528 | tf_op jit(solution)/shard_map/ppermute | solution.py:355
  38.7 3.7 %collective-permute-start.8 = (f32[8,48,128]{2,1,0:T(8,128)S(1)}, f32[8,48,128]{2,1,0:T(8,128)S(1)}, u32[]{:S(2)}, u32[]{:S(2)}) collective-permute-start(f32[8,48,128]{2,1,0:T(8,128)S(1)} %get-tuple-element.31), channel_id=1, source_target_pairs={{0,1},{1,0},{2,3},{3,2},{4,5},{5,4},{6,7},{7,6},{8,9},{9,8},{10,11... | collective-permute-start | bytes 589832 | tf_op jit(solution)/shard_map/ppermute | solution.py:355
  74.0 4.5 %collective-permute-start.9 = (f32[8,48,128]{2,1,0:T(8,128)S(1)}, f32[8,48,128]{2,1,0:T(8,128)S(1)}, u32[]{:S(2)}, u32[]{:S(2)}) collective-permute-start(f32[8,48,128]{2,1,0:T(8,128)S(1)} %get-tuple-element.35), channel_id=1, source_target_pairs={{0,1},{1,0},{2,3},{3,2},{4,5},{5,4},{6,7},{7,6},{8,9},{9,8},{10,11... | collective-permute-start | bytes 589832 | tf_op jit(solution)/shard_map/ppermute | solution.py:355

commit v6 on v5

--- a/solution.py
+++ b/solution.py
@@ -130,8 +130,8 @@
         vec_ref[0:32, at : at + LANES] = unfold(rests).astype(BF16)
 
 
-def put_rows(log_scale, rows_ref, right_ref):
-    count = rows_ref.shape[0]
+def put_rows(log_scale, rows_ref, core, right_ref):
+    count = rows_ref.shape[0] // 2
 
     def put(tile, raw):
         at = tile * LANES
@@ -149,9 +149,10 @@
         right_ref[192:256, at : at + LANES] = jnp.zeros((64, LANES), BF16)
 
     for i in range(count):
-        put(i, rows_ref[i, 0:64].astype(F32))
+        put(i, rows_ref[2 * i + core, 0:64].astype(F32))
     for m in range(count // 4):
-        put(count + m, unfold([rows_ref[4 * m + q, 64:80].astype(F32) for q in range(4)]))
+        rests = [rows_ref[2 * (4 * m + q) + core, 64:80].astype(F32) for q in range(4)]
+        put(count + m, unfold(rests))
 
 
 def affinity_product(left_ref, right_ref, vec_ref, aff_ref, send_ref):
@@ -194,19 +195,12 @@
 
 
 def rows_body(log_scale):
-    def body(away_ref, home_ref, away_right_ref, home_right_ref):
-        put_rows(log_scale, away_ref, away_right_ref)
-        put_rows(log_scale, home_ref, home_right_ref)
+    def body(rows_ref, away_right_ref, home_right_ref):
+        core = lax.axis_index("core")
+        put_rows(log_scale, rows_ref, 1 - core, away_right_ref)
+        put_rows(log_scale, rows_ref, core, home_right_ref)
 
     return body
-
-
-def order_body(*refs):
-    out_ref = refs[-1]
-    count = len(refs) - 1
-    here = lax.axis_index("z")
-    for t in range(count):
-        out_ref[lax.rem(here + count - t, count)] = refs[t][...]
 
 
 def join_body(mine_ref, other_ref, out_ref):
@@ -372,19 +366,9 @@
         ),
         in_specs=[hbm_space, hbm_space],
     )
-    forth = [(i, (i + 1) % half) for i in range(half)]
-    back = [(i, (i - 1) % half) for i in range(half)]
     cols = exchange(cols, "row")
-    ahead, behind = [rows], [rows]
-    for _ in range(half // 2):
-        behind.append(lax.ppermute(behind[-1], "z", forth))
-        if len(behind) + len(ahead) - 1 < half:
-            ahead.append(lax.ppermute(ahead[-1], "z", back))
-    home_rows = call(order_body, pltpu.VMEM((half, 80, LANES), BF16), *behind, *ahead[:0:-1])
-    away_rows = swap(home_rows)
-    away_right, home_right = call(
-        rows_body(log_scale), (right_shape, right_shape), away_rows, home_rows
-    )
+    rows = lax.all_gather(rows, ("z", "core"))
+    away_right, home_right = call(rows_body(log_scale), (right_shape, right_shape), rows)
     aff_shape = pltpu.VMEM((row * group, lanes), BF16)
     send_shape = shape((half, 48, LANES), F32)
     away_aff, away_send, left, vec = call(

time: 117 us -> 111 us (0.949)
  blocking collectives: 65.1 us -> 84.2 us
  starting transfers between devices: 27.2 us -> 11.3 us
  waiting for transfers between devices: 8.88 us -> 0.01 us
    all_gather x0 -> x1, blocking collectives: none -> 21.7 us  [shards(): rows = lax.all_gather(rows, ('z', 'core'))]
    ppermute x7 -> x0, starting transfers between devices: 11.1 us -> none  [the longest x3 9.38 us: shards(): ahead.append(lax.ppermute(ahead[-1], 'z', back))]
    ppermute x7 -> x0, waiting for transfers between devices: 7.84 us -> none  [the longest x4 7.83 us: shards(): behind.append(lax.ppermute(behind[-1], 'z', forth))]
    ppermute x3 -> x2, starting transfers between devices: 8.52 us -> 3.71 us  [swap(): return lax.ppermute(x, 'core', [(0, 1), (1, 0)])]
    all_to_all x5, blocking collectives: 65.1 us -> 62.6 us  [exchange(): return lax.all_to_all(x, axis, 0, 0, tiled=True)]
    pallas_call x13 -> x12, Pallas kernels: 15 us -> 14.9 us  [call(): pl.pallas_call(body, out_shape=out_shape, scratch_shapes=scratch, compile...]
  transfers between devices with their start and end apart: 11 -> 3, of which waited for: 5 -> 0; matrix products, arithmetic and copies ran while one was open for 0% -> 0% of each run, Pallas kernels for 4% -> 4%
where the time goes in v6:
time: 111 us
  blocking collectives  84.2 us (76%)
  Pallas kernels  14.9 us (13%)
  starting transfers between devices  11.3 us (10%)
    all_to_all x5, blocking collectives, exchange(): return lax.all_to_all(x, axis, 0, 0, tiled=True)  62.6 us
    all_gather x1, blocking collectives, shards(): rows = lax.all_gather(rows, ('z', 'core'))  21.7 us
    pallas_call x12, Pallas kernels, call(): pl.pallas_call(body, out_shape=out_shape, scratch_shapes=scratch, compile...  14.9 us
    all_to_all x1, starting transfers between devices, exchange(): return lax.all_to_all(x, axis, 0, 0, tiled=True)  7.58 us
    ppermute x2, starting transfers between devices, swap(): return lax.ppermute(x, 'core', [(0, 1), (1, 0)])  3.71 us
  transfers between devices with their start and end apart: 3, of which 0 were waited for; matrix products, arithmetic and copies ran while one was open for 0% of the time, Pallas kernels for 4%

profile of v6, /device:TPU:1, one launch (start us, length us, event | category | flops | bytes accessed | tf_op | source)
XLA Modules:
  0.0 110.5 jit_solution(10617067160716204272)
XLA Ops:
  0.0 1.7 %shard_map.28 = (bf16[16,120,128]{2,1,0:T(8,128)(2,1)}, bf16[80,128]{1,0:T(8,128)(2,1)S(1)}) custom-call(bf16[64,160]{1,0:T(8,128)(2,1)} %bitcast.5, bf16[32,160]{1,0:T(8,128)(2,1)} %bitcast.6), custom_call_target="tpu_custom_call" | custom-call | tf_op jit(solution)/shard_map/pallas_call | solution.py:352
  1.8 7.6 %all-to-all-start = ((bf16[16,120,128]{2,1,0:T(8,128)(2,1)}), bf16[16,120,128]{2,1,0:T(8,128)(2,1)S(1)}, u32[]{:S(2)}, u32[]{:S(2)}) async-start(bf16[16,120,128]{2,1,0:T(8,128)(2,1)} %get-tuple-element.24), calls=%async_computation | async-start | bytes 983040 | tf_op jit(solution)/shard_map/all_to_all | solution.py:346
  9.3 21.7 %all-gather = bf16[1280,128]{1,0:T(8,128)(2,1)S(1)} all-gather(bf16[80,128]{1,0:T(8,128)(2,1)S(1)} %get-tuple-element.22), channel_id=2, replica_groups=mesh['row'=16,'z'=8,'core'=2] {'z','core'}, dimensions={0}, use_global_device_ids=true | all-gather | bytes 348160 | tf_op jit(solution)/shard_map/all_gather | solution.py:370
  31.0 0.3 shard_map.29
  31.4 0.0 all-to-all-done.cols_ref
  31.4 4.2 %shard_map.30 = (bf16[2560,1280]{1,0:T(8,128)(2,1)S(1)}, f32[8,48,128]{2,1,0:T(8,128)S(1)}, bf16[2560,128]{1,0:T(8,128)(2,1)S(1)}, bf16[48,2560]{1,0:T(8,128)(2,1)S(1)}) custom-call(bf16[256,1280]{1,0:T(8,128)(2,1)S(1)} %get-tuple-element.23.right_ref, bf16[16,120,128]{2,1,0:T(8,128)(2,1)S(1)} %all-to-all-done.cols_ref), custom_call_target="tpu_custom_call" | custom-call | tf_op jit(solution)/shard_map/pallas_call | solution.py:352
  35.6 0.3 collective-permute-start
  35.8 3.1 %shard_map.31 = (bf16[2560,1280]{1,0:T(8,128)(2,1)S(1)}, f32[8,48,128]{2,1,0:T(8,128)S(1)}) custom-call(bf16[2560,128]{1,0:T(8,128)(2,1)S(1)} %get-tuple-element.25.left_ref, bf16[256,1280]{1,0:T(8,128)(2,1)S(1)} %get-tuple-element.26.right_ref, bf16[48,2560]{1,0:T(8,128)(2,1)S(1)} %get-tuple-element.27.vec_ref), custom_call_target="tpu_custom_call" | custom-call | tf_op jit(solution)/shard_map/pallas_call | solution.py:352
  38.9 0.0 collective-permute-done.other_ref
  39.0 12.6 %all_to_all.30.recv_ref = f32[8,48,128]{2,1,0:T(8,128)S(1)} all-to-all(f32[8,48,128]{2,1,0:T(8,128)S(1)} %shard_map.32), channel_id=1, replica_groups=mesh['row'=16,'z'=8,'core'=2] {'z'}, dimensions={0} | all-to-all | bytes 393216 | tf_op jit(solution)/shard_map/all_to_all | solution.py:346
  51.6 0.4 shard_map.33
  51.9 14.7 %all_to_all.31.spread_ref = f32[16,48,128]{2,1,0:T(8,128)S(1)} all-to-all(f32[16,48,128]{2,1,0:T(8,128)S(1)} %get-tuple-element.32), channel_id=1, replica_groups=mesh['row'=16,'z'=8,'core'=2] {'row'}, dimensions={0} | all-to-all | bytes 786432 | tf_op jit(solution)/shard_map/all_to_all | solution.py:346
  66.7 1.3 %shard_map.34 = (f32[8,48,128]{2,1,0:T(8,128)S(1)}, bf16[64,2560]{1,0:T(8,128)(2,1)S(1)}, f32[8,128]{1,0:T(8,128)S(1)}) custom-call(bf16[2560,1280]{1,0:T(8,128)(2,1)S(1)} %get-tuple-element.29.aff_ref, f32[16,48,128]{2,1,0:T(8,128)S(1)} %all_to_all.31.spread_ref), custom_call_target="tpu_custom_call" | custom-call | tf_op jit(solution)/shard_map/pallas_call | solution.py:352
  68.0 3.5 %collective-permute-start.1 = (f32[8,48,128]{2,1,0:T(8,128)S(1)}, f32[8,48,128]{2,1,0:T(8,128)S(1)}, u32[]{:S(2)}, u32[]{:S(2)}) collective-permute-start(f32[8,48,128]{2,1,0:T(8,128)S(1)} %get-tuple-element.35), channel_id=1, source_target_pairs={{0,1},{1,0},{2,3},{3,2},{4,5},{5,4},{6,7},{7,6},{8,9},{9,8},{10,11... | collective-permute-start | bytes 589832 | tf_op jit(solution)/shard_map/ppermute | solution.py:349
  71.5 1.3 %shard_map.35.mine_ref = f32[8,48,128]{2,1,0:T(8,128)S(1)} custom-call(bf16[2560,1280]{1,0:T(8,128)(2,1)S(1)} %get-tuple-element.28.aff_ref, bf16[64,2560]{1,0:T(8,128)(2,1)S(1)} %get-tuple-element.33.vec_ref, f32[8,128]{1,0:T(8,128)S(1)} %get-tuple-element.34.gram_ref), custom_call_target="tpu_custom_call" | custom-call | tf_op jit(solution)/shard_map/pallas_call | solution.py:352
  72.8 0.0 collective-permute-done.1.other_ref
  72.8 13.4 %all_to_all.32.recv_ref = f32[8,48,128]{2,1,0:T(8,128)S(1)} all-to-all(f32[8,48,128]{2,1,0:T(8,128)S(1)} %shard_map.36), channel_id=1, replica_groups=mesh['row'=16,'z'=8,'core'=2] {'z'}, dimensions={0} | all-to-all | bytes 393216 | tf_op jit(solution)/shard_map/all_to_all | solution.py:346
  86.2 1.0 shard_map.37
  87.2 9.8 %all_to_all.33.recv_ref = f32[16,8,128]{2,1,0:T(8,128)S(1)} all-to-all(f32[16,8,128]{2,1,0:T(8,128)S(1)} %get-tuple-element.37), channel_id=1, replica_groups=mesh['row'=16,'z'=8,'core'=2] {'row'}, dimensions={0} | all-to-all | bytes 131072 | tf_op jit(solution)/shard_map/all_to_all | solution.py:346
  97.0 12.1 %all_to_all.34.recv_ref = f32[16,8,128]{2,1,0:T(8,128)S(1)} all-to-all(f32[16,8,128]{2,1,0:T(8,128)S(1)} %shard_map.38), channel_id=1, replica_groups=mesh['row'=16,'z'=8,'core'=2] {'z','core'}, dimensions={0} | all-to-all | bytes 131072 | tf_op jit(solution)/shard_map/all_to_all | solution.py:346
  109.1 1.4 %shard_map.39 = f32[32,160]{1,0:T(8,128)} custom-call(f32[16,8,128]{2,1,0:T(8,128)S(1)} %all_to_all.34.recv_ref, f32[32,256]{1,0:T(8,128)S(1)} %get-tuple-element.38.scaled_ref), custom_call_target="tpu_custom_call" | custom-call | tf_op jit(solution)/shard_map/pallas_call | solution.py:352
  (3 shorter events, 0.1 us)
Async XLA Ops:
  1.8 29.6 %all-to-all-start = ((bf16[16,120,128]{2,1,0:T(8,128)(2,1)}), bf16[16,120,128]{2,1,0:T(8,128)(2,1)S(1)}, u32[]{:S(2)}, u32[]{:S(2)}) async-start(bf16[16,120,128]{2,1,0:T(8,128)(2,1)} %get-tuple-element.24), calls=%async_computation | async-start | bytes 983040 | tf_op jit(solution)/shard_map/all_to_all | solution.py:346
  35.6 3.4 %collective-permute-start = (f32[8,48,128]{2,1,0:T(8,128)S(1)}, f32[8,48,128]{2,1,0:T(8,128)S(1)}, u32[]{:S(2)}, u32[]{:S(2)}) collective-permute-start(f32[8,48,128]{2,1,0:T(8,128)S(1)} %get-tuple-element.31), channel_id=1, source_target_pairs={{0,1},{1,0},{2,3},{3,2},{4,5},{5,4},{6,7},{7,6},{8,9},{9,8},{10,11... | collective-permute-start | bytes 589832 | tf_op jit(solution)/shard_map/ppermute | solution.py:349
  68.0 4.8 %collective-permute-start.1 = (f32[8,48,128]{2,1,0:T(8,128)S(1)}, f32[8,48,128]{2,1,0:T(8,128)S(1)}, u32[]{:S(2)}, u32[]{:S(2)}) collective-permute-start(f32[8,48,128]{2,1,0:T(8,128)S(1)} %get-tuple-element.35), channel_id=1, source_target_pairs={{0,1},{1,0},{2,3},{3,2},{4,5},{5,4},{6,7},{7,6},{8,9},{9,8},{10,11... | collective-permute-start | bytes 589832 | tf_op jit(solution)/shard_map/ppermute | solution.py:349

commit v7 on v6

--- a/solution.py
+++ b/solution.py
@@ -71,25 +71,39 @@
         ref[i] = value
 
 
-def pack_body(points_hbm, vectors_hbm, cols_ref, rows_ref, points_ref, vectors_ref, sems):
-    loads = (
-        pltpu.make_async_copy(points_hbm, points_ref, sems.at[0]),
-        pltpu.make_async_copy(vectors_hbm, vectors_ref, sems.at[1]),
-    )
-    for load in loads:
-        load.start()
-    for load in loads:
-        load.wait()
-    pts = points_ref[...].astype(F32)
-    main, rest = main_and_rest(pts)
-    rows_ref[...] = jnp.concatenate([main, rest], axis=0).astype(BF16)
-    features, group = pts.shape
-    half = group // 2
-    flat = jnp.concatenate([main, widen(pts[:, LANES:])], axis=1)
-    flat = jnp.concatenate([flat, jnp.zeros_like(flat)], axis=0).T
-    by_point = flat[0:half] + roll(flat[half:group], features)
-    main, rest = main_and_rest(vectors_ref[...].astype(F32))
-    copies(cols_ref, jnp.concatenate([by_point, main, rest], axis=0).astype(BF16))
+def pack_body(log_scale):
+    def body(points_hbm, vectors_hbm, cols_hbm, rows_ref, points_ref, vectors_ref, block_ref, sems):
+        loads = (
+            pltpu.make_async_copy(points_hbm, points_ref, sems.at[0]),
+            pltpu.make_async_copy(vectors_hbm, vectors_ref, sems.at[1]),
+        )
+        for load in loads:
+            load.start()
+        loads[0].wait()
+        pts = points_ref[...].astype(F32)
+        group = pts.shape[1]
+        main, rest = main_and_rest(pts)
+        rows_ref[...] = jnp.concatenate([main, rest], axis=0).astype(BF16)
+        flat = jnp.concatenate([main, widen(pts[:, LANES:])], axis=1)
+        flat = jnp.concatenate([flat, jnp.zeros_like(flat)], axis=0).T[0:group]
+        norm = jnp.sum(flat * flat, axis=1, keepdims=True) * (-0.5 * log_scale)
+        lane = lane_of(flat.shape)
+        for k, piece in enumerate(split(norm)):
+            flat = jnp.where(lane == NORM + k, piece, flat)
+        flat = jnp.where((lane >= ONES) & (lane < END), 1.0, flat)
+        loads[1].wait()
+        main, rest = main_and_rest(vectors_ref[...].astype(F32))
+        block_ref[...] = jnp.concatenate([flat, main, rest], axis=0).astype(BF16)
+        count = cols_hbm.shape[0]
+        sends = [
+            pltpu.make_async_copy(block_ref, cols_hbm.at[i], sems.at[2 + i]) for i in range(count)
+        ]
+        for send in sends:
+            send.start()
+        for send in sends:
+            send.wait()
+
+    return body
 
 
 def blocks_of(count):
@@ -98,34 +112,18 @@
     return main, (lanes, lanes // 4)
 
 
-def put_columns(log_scale, cols_ref, left_ref, vec_ref):
+def put_columns(cols_ref, left_ref, vec_ref):
     count = cols_ref.shape[0]
     total = left_ref.shape[0]
-    lane = lane_of((80, LANES))
-    low = lane < NORM
     for i in range(count):
-        raw = cols_ref[i, 0:80].astype(F32)
-        squares = raw * raw
-        blocks = []
-        for side in range(2):
-            mine = low if side == 0 else jnp.logical_not(low)
-            norm = jnp.sum(jnp.where(mine, squares, 0.0), axis=1, keepdims=True)
-            norm = norm * (-0.5 * log_scale)
-            block = jnp.where(low, raw if side == 0 else roll(raw, NORM), 0.0)
-            for k, piece in enumerate(split(norm)):
-                block = jnp.where(lane == NORM + k, piece, block)
-            block = jnp.where((lane >= ONES) & (lane < END), 1.0, block)
-            blocks.append(block.astype(BF16))
-        at = i * LANES
-        left_ref[at : at + 80, :] = blocks[0]
-        left_ref[at + 80 : at + LANES, :] = blocks[1][0:48]
+        left_ref[i * LANES : (i + 1) * LANES, :] = cols_ref[i, 0:128]
         at = count * LANES + i * REST
-        left_ref[at : at + REST, :] = blocks[1][48:80]
+        left_ref[at : at + REST, :] = cols_ref[i, 128:160]
     vec_ref[32:48, :] = jnp.where(row_of((16, total)) == 0, 1.0, 0.0).astype(BF16)
     for i in range(count):
-        vec_ref[0:32, i * LANES : (i + 1) * LANES] = cols_ref[i, 80:112]
+        vec_ref[0:32, i * LANES : (i + 1) * LANES] = cols_ref[i, 160:192]
     for m in range(count // 4):
-        rests = [cols_ref[4 * m + q, 112:120].astype(F32) for q in range(4)]
+        rests = [cols_ref[4 * m + q, 192:200].astype(F32) for q in range(4)]
         at = (count + m) * LANES
         vec_ref[0:32, at : at + LANES] = unfold(rests).astype(BF16)
 
@@ -186,12 +184,9 @@
             send_ref[4 * m + q, 41:42, :] = roll(tile[32:40], -REST * q)[0:1]
 
 
-def away_body(log_scale):
-    def body(right_ref, cols_ref, aff_ref, send_ref, left_ref, vec_ref):
-        put_columns(log_scale, cols_ref, left_ref, vec_ref)
-        affinity_product(left_ref, right_ref, vec_ref, aff_ref, send_ref)
-
-    return body
+def away_body(right_ref, cols_ref, aff_ref, send_ref, left_ref, vec_ref):
+    put_columns(cols_ref, left_ref, vec_ref)
+    affinity_product(left_ref, right_ref, vec_ref, aff_ref, send_ref)
 
 
 def rows_body(log_scale):
@@ -355,16 +350,18 @@
 
     hbm_space = pl.BlockSpec(memory_space=pltpu.HBM)
     cols, rows = call(
-        pack_body,
-        (pltpu.VMEM((row, 120, LANES), BF16), pltpu.VMEM((80, LANES), BF16)),
+        pack_body(log_scale),
+        (shape((row, group + 40, LANES), BF16), pltpu.VMEM((80, LANES), BF16)),
         pltpu.with_memory_space_constraint(points.T, pltpu.HBM),
         pltpu.with_memory_space_constraint(start_vectors.T, pltpu.HBM),
         scratch=(
             pltpu.VMEM((features, group), BF16),
             pltpu.VMEM((start_vectors.shape[1], group), BF16),
-            pltpu.SemaphoreType.DMA((2,)),
+            pltpu.VMEM((group + 40, LANES), BF16),
+            pltpu.SemaphoreType.DMA((2 + row,)),
         ),
         in_specs=[hbm_space, hbm_space],
+        out_specs=(hbm_space, pl.BlockSpec(memory_space=pltpu.VMEM)),
     )
     cols = exchange(cols, "row")
     rows = lax.all_gather(rows, ("z", "core"))
@@ -372,7 +369,7 @@
     aff_shape = pltpu.VMEM((row * group, lanes), BF16)
     send_shape = shape((half, 48, LANES), F32)
     away_aff, away_send, left, vec = call(
-        away_body(log_scale),
+        away_body,
         (
             aff_shape,
             send_shape,

time: 111 us -> 110 us (level)
  no operation moved by 1% of the time
where the time goes in v7:
time: 110 us
  blocking collectives  84.2 us (77%)
  Pallas kernels  14.2 us (13%)
  starting transfers between devices  11.3 us (10%)
    all_to_all x5, blocking collectives, exchange(): return lax.all_to_all(x, axis, 0, 0, tiled=True)  62.6 us
    all_gather x1, blocking collectives, shards(): rows = lax.all_gather(rows, ('z', 'core'))  21.7 us
    pallas_call x12, Pallas kernels, call(): pl.pallas_call(body, out_shape=out_shape, scratch_shapes=scratch, compile...  14.2 us
    all_to_all x1, starting transfers between devices, exchange(): return lax.all_to_all(x, axis, 0, 0, tiled=True)  7.58 us
    ppermute x2, starting transfers between devices, swap(): return lax.ppermute(x, 'core', [(0, 1), (1, 0)])  3.7 us
  transfers between devices with their start and end apart: 3, of which 0 were waited for; matrix products, arithmetic and copies ran while one was open for 0% of the time, Pallas kernels for 4%

profile of v7, /device:TPU:1, one launch (start us, length us, event | category | flops | bytes accessed | tf_op | source)
XLA Modules:
  0.0 109.8 jit_solution(2730603497805543770)
XLA Ops:
  0.0 2.1 %shard_map.28 = (bf16[16,200,128]{2,1,0:T(8,128)(2,1)}, bf16[80,128]{1,0:T(8,128)(2,1)S(1)}) custom-call(bf16[64,160]{1,0:T(8,128)(2,1)} %bitcast.5, bf16[32,160]{1,0:T(8,128)(2,1)} %bitcast.6), custom_call_target="tpu_custom_call" | custom-call | tf_op jit(solution)/shard_map/pallas_call | solution.py:347
  2.1 7.6 %all-to-all-start = ((bf16[16,200,128]{2,1,0:T(8,128)(2,1)}), bf16[16,200,128]{2,1,0:T(8,128)(2,1)S(1)}, u32[]{:S(2)}, u32[]{:S(2)}) async-start(bf16[16,200,128]{2,1,0:T(8,128)(2,1)} %get-tuple-element.24), calls=%async_computation | async-start | bytes 1638400 | tf_op jit(solution)/shard_map/all_to_all | solution.py:341
  9.7 21.7 %all-gather = bf16[1280,128]{1,0:T(8,128)(2,1)S(1)} all-gather(bf16[80,128]{1,0:T(8,128)(2,1)S(1)} %get-tuple-element.22), channel_id=2, replica_groups=mesh['row'=16,'z'=8,'core'=2] {'z','core'}, dimensions={0}, use_global_device_ids=true | all-gather | bytes 348160 | tf_op jit(solution)/shard_map/all_gather | solution.py:367
  31.4 0.3 shard_map.29
  31.7 0.0 all-to-all-done.cols_ref
  31.7 3.1 %shard_map.30 = (bf16[2560,1280]{1,0:T(8,128)(2,1)S(1)}, f32[8,48,128]{2,1,0:T(8,128)S(1)}, bf16[2560,128]{1,0:T(8,128)(2,1)S(1)}, bf16[48,2560]{1,0:T(8,128)(2,1)S(1)}) custom-call(bf16[256,1280]{1,0:T(8,128)(2,1)S(1)} %get-tuple-element.23.right_ref, bf16[16,200,128]{2,1,0:T(8,128)(2,1)S(1)} %all-to-all-done.cols_ref), custom_call_target="tpu_custom_call" | custom-call | tf_op jit(solution)/shard_map/pallas_call | solution.py:347
  34.8 0.2 collective-permute-start
  35.1 3.1 %shard_map.31 = (bf16[2560,1280]{1,0:T(8,128)(2,1)S(1)}, f32[8,48,128]{2,1,0:T(8,128)S(1)}) custom-call(bf16[2560,128]{1,0:T(8,128)(2,1)S(1)} %get-tuple-element.25.left_ref, bf16[256,1280]{1,0:T(8,128)(2,1)S(1)} %get-tuple-element.26.right_ref, bf16[48,2560]{1,0:T(8,128)(2,1)S(1)} %get-tuple-element.27.vec_ref), custom_call_target="tpu_custom_call" | custom-call | tf_op jit(solution)/shard_map/pallas_call | solution.py:347
  38.2 0.0 collective-permute-done.other_ref
  38.2 12.6 %all_to_all.30.recv_ref = f32[8,48,128]{2,1,0:T(8,128)S(1)} all-to-all(f32[8,48,128]{2,1,0:T(8,128)S(1)} %shard_map.32), channel_id=1, replica_groups=mesh['row'=16,'z'=8,'core'=2] {'z'}, dimensions={0} | all-to-all | bytes 393216 | tf_op jit(solution)/shard_map/all_to_all | solution.py:341
  50.8 0.4 shard_map.33
  51.2 14.7 %all_to_all.31.spread_ref = f32[16,48,128]{2,1,0:T(8,128)S(1)} all-to-all(f32[16,48,128]{2,1,0:T(8,128)S(1)} %get-tuple-element.32), channel_id=1, replica_groups=mesh['row'=16,'z'=8,'core'=2] {'row'}, dimensions={0} | all-to-all | bytes 786432 | tf_op jit(solution)/shard_map/all_to_all | solution.py:341
  65.9 1.3 %shard_map.34 = (f32[8,48,128]{2,1,0:T(8,128)S(1)}, bf16[64,2560]{1,0:T(8,128)(2,1)S(1)}, f32[8,128]{1,0:T(8,128)S(1)}) custom-call(bf16[2560,1280]{1,0:T(8,128)(2,1)S(1)} %get-tuple-element.29.aff_ref, f32[16,48,128]{2,1,0:T(8,128)S(1)} %all_to_all.31.spread_ref), custom_call_target="tpu_custom_call" | custom-call | tf_op jit(solution)/shard_map/pallas_call | solution.py:347
  67.3 3.5 %collective-permute-start.1 = (f32[8,48,128]{2,1,0:T(8,128)S(1)}, f32[8,48,128]{2,1,0:T(8,128)S(1)}, u32[]{:S(2)}, u32[]{:S(2)}) collective-permute-start(f32[8,48,128]{2,1,0:T(8,128)S(1)} %get-tuple-element.35), channel_id=1, source_target_pairs={{0,1},{1,0},{2,3},{3,2},{4,5},{5,4},{6,7},{7,6},{8,9},{9,8},{10,11... | collective-permute-start | bytes 589832 | tf_op jit(solution)/shard_map/ppermute | solution.py:344
  70.7 1.3 %shard_map.35.mine_ref = f32[8,48,128]{2,1,0:T(8,128)S(1)} custom-call(bf16[2560,1280]{1,0:T(8,128)(2,1)S(1)} %get-tuple-element.28.aff_ref, bf16[64,2560]{1,0:T(8,128)(2,1)S(1)} %get-tuple-element.33.vec_ref, f32[8,128]{1,0:T(8,128)S(1)} %get-tuple-element.34.gram_ref), custom_call_target="tpu_custom_call" | custom-call | tf_op jit(solution)/shard_map/pallas_call | solution.py:347
  72.1 0.0 collective-permute-done.1.other_ref
  72.1 13.4 %all_to_all.32.recv_ref = f32[8,48,128]{2,1,0:T(8,128)S(1)} all-to-all(f32[8,48,128]{2,1,0:T(8,128)S(1)} %shard_map.36), channel_id=1, replica_groups=mesh['row'=16,'z'=8,'core'=2] {'z'}, dimensions={0} | all-to-all | bytes 393216 | tf_op jit(solution)/shard_map/all_to_all | solution.py:341
  85.5 1.0 shard_map.37
  86.5 9.8 %all_to_all.33.recv_ref = f32[16,8,128]{2,1,0:T(8,128)S(1)} all-to-all(f32[16,8,128]{2,1,0:T(8,128)S(1)} %get-tuple-element.37), channel_id=1, replica_groups=mesh['row'=16,'z'=8,'core'=2] {'row'}, dimensions={0} | all-to-all | bytes 131072 | tf_op jit(solution)/shard_map/all_to_all | solution.py:341
  96.3 12.1 %all_to_all.34.recv_ref = f32[16,8,128]{2,1,0:T(8,128)S(1)} all-to-all(f32[16,8,128]{2,1,0:T(8,128)S(1)} %shard_map.38), channel_id=1, replica_groups=mesh['row'=16,'z'=8,'core'=2] {'z','core'}, dimensions={0} | all-to-all | bytes 131072 | tf_op jit(solution)/shard_map/all_to_all | solution.py:341
  108.4 1.4 %shard_map.39 = f32[32,160]{1,0:T(8,128)} custom-call(f32[16,8,128]{2,1,0:T(8,128)S(1)} %all_to_all.34.recv_ref, f32[32,256]{1,0:T(8,128)S(1)} %get-tuple-element.38.scaled_ref), custom_call_target="tpu_custom_call" | custom-call | tf_op jit(solution)/shard_map/pallas_call | solution.py:347
  (3 shorter events, 0.1 us)
Async XLA Ops:
  2.1 29.6 %all-to-all-start = ((bf16[16,200,128]{2,1,0:T(8,128)(2,1)}), bf16[16,200,128]{2,1,0:T(8,128)(2,1)S(1)}, u32[]{:S(2)}, u32[]{:S(2)}) async-start(bf16[16,200,128]{2,1,0:T(8,128)(2,1)} %get-tuple-element.24), calls=%async_computation | async-start | bytes 1638400 | tf_op jit(solution)/shard_map/all_to_all | solution.py:341
  34.8 3.4 %collective-permute-start = (f32[8,48,128]{2,1,0:T(8,128)S(1)}, f32[8,48,128]{2,1,0:T(8,128)S(1)}, u32[]{:S(2)}, u32[]{:S(2)}) collective-permute-start(f32[8,48,128]{2,1,0:T(8,128)S(1)} %get-tuple-element.31), channel_id=1, source_target_pairs={{0,1},{1,0},{2,3},{3,2},{4,5},{5,4},{6,7},{7,6},{8,9},{9,8},{10,11... | collective-permute-start | bytes 589832 | tf_op jit(solution)/shard_map/ppermute | solution.py:344
  67.3 4.8 %collective-permute-start.1 = (f32[8,48,128]{2,1,0:T(8,128)S(1)}, f32[8,48,128]{2,1,0:T(8,128)S(1)}, u32[]{:S(2)}, u32[]{:S(2)}) collective-permute-start(f32[8,48,128]{2,1,0:T(8,128)S(1)} %get-tuple-element.35), channel_id=1, source_target_pairs={{0,1},{1,0},{2,3},{3,2},{4,5},{5,4},{6,7},{7,6},{8,9},{9,8},{10,11... | collective-permute-start | bytes 589832 | tf_op jit(solution)/shard_map/ppermute | solution.py:344

commit v8 on v7

--- a/solution.py
+++ b/solution.py
@@ -84,13 +84,14 @@
         group = pts.shape[1]
         main, rest = main_and_rest(pts)
         rows_ref[...] = jnp.concatenate([main, rest], axis=0).astype(BF16)
-        flat = jnp.concatenate([main, widen(pts[:, LANES:])], axis=1)
-        flat = jnp.concatenate([flat, jnp.zeros_like(flat)], axis=0).T[0:group]
-        norm = jnp.sum(flat * flat, axis=1, keepdims=True) * (-0.5 * log_scale)
-        lane = lane_of(flat.shape)
+        flat = jnp.concatenate([pts[:, 0:LANES], widen(pts[:, LANES:])], axis=1)
+        norm = jnp.sum(flat * flat, axis=0, keepdims=True) * (-0.5 * log_scale)
+        row = row_of((8, flat.shape[1]))
+        extra = jnp.where((row >= ONES - NORM) & (row < END - NORM), 1.0, 0.0)
         for k, piece in enumerate(split(norm)):
-            flat = jnp.where(lane == NORM + k, piece, flat)
-        flat = jnp.where((lane >= ONES) & (lane < END), 1.0, flat)
+            extra = jnp.where(row == k, piece, extra)
+        rest = jnp.zeros((LANES - NORM - 8, flat.shape[1]), F32)
+        flat = jnp.concatenate([flat, extra, rest], axis=0).T[0:group]
         loads[1].wait()
         main, rest = main_and_rest(vectors_ref[...].astype(F32))
         block_ref[...] = jnp.concatenate([flat, main, rest], axis=0).astype(BF16)
@@ -190,12 +191,29 @@
 
 
 def rows_body(log_scale):
-    def body(rows_ref, away_right_ref, home_right_ref):
+    def body(pair_ref, *refs):
+        *moved, away_right_ref, home_right_ref, rows_ref = refs
         core = lax.axis_index("core")
+        here = lax.axis_index("z")
+        count = rows_ref.shape[0] // 2
+        steps = len(moved) // 2
+        rows_ref[pl.ds(2 * here, 2)] = pair_ref[...]
+        for t in range(1, steps + 1):
+            mine, other = moved[t - 1], moved[steps + t - 1]
+            up = lax.rem(here + count - t, count)
+            down = lax.rem(here + t, count)
+            rows_ref[pl.ds(2 * lax.select(core == 0, up, down), 2)] = mine[...]
+            rows_ref[pl.ds(2 * lax.select(core == 0, down, up), 2)] = other[...]
         put_rows(log_scale, rows_ref, 1 - core, away_right_ref)
         put_rows(log_scale, rows_ref, core, home_right_ref)
 
     return body
+
+
+def pair_body(mine_ref, other_ref, out_ref):
+    core = lax.axis_index("core")
+    out_ref[core] = mine_ref[...]
+    out_ref[1 - core] = other_ref[...]
 
 
 def join_body(mine_ref, other_ref, out_ref):
@@ -364,8 +382,21 @@
         out_specs=(hbm_space, pl.BlockSpec(memory_space=pltpu.VMEM)),
     )
     cols = exchange(cols, "row")
-    rows = lax.all_gather(rows, ("z", "core"))
-    away_right, home_right = call(rows_body(log_scale), (right_shape, right_shape), rows)
+    other = swap(rows)
+    pair = call(pair_body, pltpu.VMEM((2, 80, LANES), BF16), rows, other)
+    ways = [(2 * z, 2 * ((z + 1) % half)) for z in range(half)]
+    ways += [(2 * z + 1, 2 * ((z - 1) % half) + 1) for z in range(half)]
+    mine, others = [pair], []
+    for _ in range(half // 2):
+        mine.append(lax.ppermute(mine[-1], ("z", "core"), ways))
+        others.append(swap(mine[-1]))
+    away_right, home_right = call(
+        rows_body(log_scale),
+        (right_shape, right_shape),
+        *mine,
+        *others,
+        scratch=(pltpu.VMEM((col, 80, LANES), BF16),),
+    )
     aff_shape = pltpu.VMEM((row * group, lanes), BF16)
     send_shape = shape((half, 48, LANES), F32)
     away_aff, away_send, left, vec = call(

time: 110 us -> 118 us (1.073)
  starting transfers between devices: 11.3 us -> 32.4 us
  blocking collectives: 84.2 us -> 65 us
  waiting for transfers between devices: 0.01 us -> 5.61 us
    all_gather x1 -> x0, blocking collectives: 21.7 us -> none  [shards(): rows = lax.all_gather(rows, ('z', 'core'))]
    ppermute x0 -> x4, starting transfers between devices: none -> 15.3 us  [shards(): mine.append(lax.ppermute(mine[-1], ('z', 'core'), ways))]
    ppermute x2 -> x7, starting transfers between devices: 3.7 us -> 9.42 us  [swap(): return lax.ppermute(x, 'core', [(0, 1), (1, 0)])]
    ppermute x0 -> x4, waiting for transfers between devices: none -> 3.89 us  [shards(): mine.append(lax.ppermute(mine[-1], ('z', 'core'), ways))]
    all_to_all x5, blocking collectives: 62.6 us -> 65 us  [exchange(): return lax.all_to_all(x, axis, 0, 0, tiled=True)]
    ppermute x2 -> x7, waiting for transfers between devices: 0.01 us -> 1.72 us  [swap(): return lax.ppermute(x, 'core', [(0, 1), (1, 0)])]
    pallas_call x12 -> x13, Pallas kernels: 14.2 us -> 14.2 us  [call(): pl.pallas_call(body, out_shape=out_shape, scratch_shapes=scratch, compile...]
  transfers between devices with their start and end apart: 3 -> 12, of which waited for: 0 -> 6; matrix products, arithmetic and copies ran while one was open for 0% -> 0% of each run, Pallas kernels for 4% -> 4%
where the time goes in v8:
time: 118 us; the launch traced here: 117 us
  blocking collectives  65 us (55%)
  starting transfers between devices  32.4 us (27%)
  Pallas kernels  14.2 us (12%)
  waiting for transfers between devices  5.61 us (5%)
    all_to_all x5, blocking collectives, exchange(): return lax.all_to_all(x, axis, 0, 0, tiled=True)  65 us
    ppermute x4, starting transfers between devices, shards(): mine.append(lax.ppermute(mine[-1], ('z', 'core'), ways))  15.3 us
    pallas_call x13, Pallas kernels, call(): pl.pallas_call(body, out_shape=out_shape, scratch_shapes=scratch, compile...  14.2 us
    ppermute x7, starting transfers between devices, swap(): return lax.ppermute(x, 'core', [(0, 1), (1, 0)])  9.42 us
    all_to_all x1, starting transfers between devices, exchange(): return lax.all_to_all(x, axis, 0, 0, tiled=True)  7.58 us
    ppermute x4, waiting for transfers between devices, shards(): mine.append(lax.ppermute(mine[-1], ('z', 'core'), ways))  3.89 us
  transfers between devices with their start and end apart: 12, of which 6 were waited for; matrix products, arithmetic and copies ran while one was open for 0% of the time, Pallas kernels for 4%

profile of v8, /device:TPU:1, one launch (start us, length us, event | category | flops | bytes accessed | tf_op | source)
XLA Modules:
  0.0 117.2 jit_solution(15874973868312421303)
XLA Ops:
  0.0 2.0 %shard_map.28 = (bf16[16,200,128]{2,1,0:T(8,128)(2,1)}, bf16[80,128]{1,0:T(8,128)(2,1)S(1)}) custom-call(bf16[64,160]{1,0:T(8,128)(2,1)} %bitcast.3, bf16[32,160]{1,0:T(8,128)(2,1)} %bitcast.4), custom_call_target="tpu_custom_call" | custom-call | tf_op jit(solution)/shard_map/pallas_call | solution.py:365
  2.0 7.6 %all-to-all-start = ((bf16[16,200,128]{2,1,0:T(8,128)(2,1)}), bf16[16,200,128]{2,1,0:T(8,128)(2,1)S(1)}, u32[]{:S(2)}, u32[]{:S(2)}) async-start(bf16[16,200,128]{2,1,0:T(8,128)(2,1)} %get-tuple-element.24), calls=%async_computation | async-start | bytes 1638400 | tf_op jit(solution)/shard_map/all_to_all | solution.py:359
  9.6 1.0 collective-permute-start
  11.5 5.6 %collective-permute-start.1 = (bf16[2,80,128]{2,1,0:T(8,128)(2,1)S(1)}, bf16[2,80,128]{2,1,0:T(8,128)(2,1)S(1)}, u32[]{:S(2)}, u32[]{:S(2)}) collective-permute-start(bf16[2,80,128]{2,1,0:T(8,128)(2,1)S(1)} %shard_map.29.pair_ref), channel_id=1, source_target_pairs={{0,2},{2,4},{4,6},{6,8},{8,10},{10,12},{12,14},{14,0},{1,15},{3,1}... | collective-permute-start | bytes 122888 | tf_op jit(solution)/shard_map/ppermute | solution.py:391
  17.1 1.1 collective-permute-done.1.refs_0_
  18.2 3.3 %collective-permute-start.2 = (bf16[2,80,128]{2,1,0:T(8,128)(2,1)S(1)}, bf16[2,80,128]{2,1,0:T(8,128)(2,1)S(1)}, u32[]{:S(2)}, u32[]{:S(2)}) collective-permute-start(bf16[2,80,128]{2,1,0:T(8,128)(2,1)S(1)} %collective-permute-done.1.refs_0_), channel_id=1, source_target_pairs={{0,2},{2,4},{4,6},{6,8},{8,10},{10,12},{12,14},{14,0},{1,15},{3,1}... | collective-permute-start | bytes 122888 | tf_op jit(solution)/shard_map/ppermute | solution.py:391
  21.4 1.1 collective-permute-done.2.refs_1_
  22.5 3.3 %collective-permute-start.3 = (bf16[2,80,128]{2,1,0:T(8,128)(2,1)S(1)}, bf16[2,80,128]{2,1,0:T(8,128)(2,1)S(1)}, u32[]{:S(2)}, u32[]{:S(2)}) collective-permute-start(bf16[2,80,128]{2,1,0:T(8,128)(2,1)S(1)} %collective-permute-done.2.refs_1_), channel_id=1, source_target_pairs={{0,2},{2,4},{4,6},{6,8},{8,10},{10,12},{12,14},{14,0},{1,15},{3,1}... | collective-permute-start | bytes 122888 | tf_op jit(solution)/shard_map/ppermute | solution.py:391
  25.8 1.1 collective-permute-done.3.refs_2_
  26.9 3.3 %collective-permute-start.4 = (bf16[2,80,128]{2,1,0:T(8,128)(2,1)S(1)}, bf16[2,80,128]{2,1,0:T(8,128)(2,1)S(1)}, u32[]{:S(2)}, u32[]{:S(2)}) collective-permute-start(bf16[2,80,128]{2,1,0:T(8,128)(2,1)S(1)} %collective-permute-done.3.refs_2_), channel_id=1, source_target_pairs={{0,2},{2,4},{4,6},{6,8},{8,10},{10,12},{12,14},{14,0},{1,15},{3,1}... | collective-permute-start | bytes 122888 | tf_op jit(solution)/shard_map/ppermute | solution.py:391
  31.3 4.1 %collective-permute-start.8 = (bf16[2,80,128]{2,1,0:T(8,128)(2,1)S(1)}, bf16[2,80,128]{2,1,0:T(8,128)(2,1)S(1)}, u32[]{:S(2)}, u32[]{:S(2)}) collective-permute-start(bf16[2,80,128]{2,1,0:T(8,128)(2,1)S(1)} %collective-permute-done.4.refs_3_), channel_id=1, source_target_pairs={{0,1},{1,0},{2,3},{3,2},{4,5},{5,4},{6,7},{7,6},{8,9},{9,8},{10,11... | collective-permute-start | bytes 122888 | tf_op jit(solution)/shard_map/ppermute | solution.py:362
  35.3 0.9 collective-permute-done.8.refs_7_
  36.6 3.1 %shard_map.31 = (bf16[2560,1280]{1,0:T(8,128)(2,1)S(1)}, f32[8,48,128]{2,1,0:T(8,128)S(1)}, bf16[2560,128]{1,0:T(8,128)(2,1)S(1)}, bf16[48,2560]{1,0:T(8,128)(2,1)S(1)}) custom-call(bf16[256,1280]{1,0:T(8,128)(2,1)S(1)} %get-tuple-element.23.right_ref, bf16[16,200,128]{2,1,0:T(8,128)(2,1)S(1)} %all-to-all-done.cols_ref), custom_call_target="tpu_custom_call" | custom-call | tf_op jit(solution)/shard_map/pallas_call | solution.py:365
  40.4 3.1 %shard_map.32 = (bf16[2560,1280]{1,0:T(8,128)(2,1)S(1)}, f32[8,48,128]{2,1,0:T(8,128)S(1)}) custom-call(bf16[2560,128]{1,0:T(8,128)(2,1)S(1)} %get-tuple-element.25.left_ref, bf16[256,1280]{1,0:T(8,128)(2,1)S(1)} %get-tuple-element.26.right_ref, bf16[48,2560]{1,0:T(8,128)(2,1)S(1)} %get-tuple-element.27.vec_ref), custom_call_target="tpu_custom_call" | custom-call | tf_op jit(solution)/shard_map/pallas_call | solution.py:365
  43.5 15.2 %all_to_all.30.recv_ref = f32[8,48,128]{2,1,0:T(8,128)S(1)} all-to-all(f32[8,48,128]{2,1,0:T(8,128)S(1)} %shard_map.33), channel_id=1, replica_groups=mesh['row'=16,'z'=8,'core'=2] {'z'}, dimensions={0} | all-to-all | bytes 393216 | tf_op jit(solution)/shard_map/all_to_all | solution.py:359
  59.0 14.6 %all_to_all.31.spread_ref = f32[16,48,128]{2,1,0:T(8,128)S(1)} all-to-all(f32[16,48,128]{2,1,0:T(8,128)S(1)} %get-tuple-element.32), channel_id=1, replica_groups=mesh['row'=16,'z'=8,'core'=2] {'row'}, dimensions={0} | all-to-all | bytes 786432 | tf_op jit(solution)/shard_map/all_to_all | solution.py:359
  73.6 1.3 %shard_map.35 = (f32[8,48,128]{2,1,0:T(8,128)S(1)}, bf16[64,2560]{1,0:T(8,128)(2,1)S(1)}, f32[8,128]{1,0:T(8,128)S(1)}) custom-call(bf16[2560,1280]{1,0:T(8,128)(2,1)S(1)} %get-tuple-element.29.aff_ref, f32[16,48,128]{2,1,0:T(8,128)S(1)} %all_to_all.31.spread_ref), custom_call_target="tpu_custom_call" | custom-call | tf_op jit(solution)/shard_map/pallas_call | solution.py:365
  75.0 3.2 %collective-permute-start.10 = (f32[8,48,128]{2,1,0:T(8,128)S(1)}, f32[8,48,128]{2,1,0:T(8,128)S(1)}, u32[]{:S(2)}, u32[]{:S(2)}) collective-permute-start(f32[8,48,128]{2,1,0:T(8,128)S(1)} %get-tuple-element.35), channel_id=1, source_target_pairs={{0,1},{1,0},{2,3},{3,2},{4,5},{5,4},{6,7},{7,6},{8,9},{9,8},{10,11... | collective-permute-start | bytes 589832 | tf_op jit(solution)/shard_map/ppermute | solution.py:362
  78.2 1.3 %shard_map.36.mine_ref = f32[8,48,128]{2,1,0:T(8,128)S(1)} custom-call(bf16[2560,1280]{1,0:T(8,128)(2,1)S(1)} %get-tuple-element.28.aff_ref, bf16[64,2560]{1,0:T(8,128)(2,1)S(1)} %get-tuple-element.33.vec_ref, f32[8,128]{1,0:T(8,128)S(1)} %get-tuple-element.34.gram_ref), custom_call_target="tpu_custom_call" | custom-call | tf_op jit(solution)/shard_map/pallas_call | solution.py:365
  79.5 13.4 %all_to_all.32.recv_ref = f32[8,48,128]{2,1,0:T(8,128)S(1)} all-to-all(f32[8,48,128]{2,1,0:T(8,128)S(1)} %shard_map.37), channel_id=1, replica_groups=mesh['row'=16,'z'=8,'core'=2] {'z'}, dimensions={0} | all-to-all | bytes 393216 | tf_op jit(solution)/shard_map/all_to_all | solution.py:359
  92.9 1.0 shard_map.38
  93.9 9.8 %all_to_all.33.recv_ref = f32[16,8,128]{2,1,0:T(8,128)S(1)} all-to-all(f32[16,8,128]{2,1,0:T(8,128)S(1)} %get-tuple-element.37), channel_id=1, replica_groups=mesh['row'=16,'z'=8,'core'=2] {'row'}, dimensions={0} | all-to-all | bytes 131072 | tf_op jit(solution)/shard_map/all_to_all | solution.py:359
  103.7 12.1 %all_to_all.34.recv_ref = f32[16,8,128]{2,1,0:T(8,128)S(1)} all-to-all(f32[16,8,128]{2,1,0:T(8,128)S(1)} %shard_map.39), channel_id=1, replica_groups=mesh['row'=16,'z'=8,'core'=2] {'z','core'}, dimensions={0} | all-to-all | bytes 131072 | tf_op jit(solution)/shard_map/all_to_all | solution.py:359
  115.8 1.4 %shard_map.40 = f32[32,160]{1,0:T(8,128)} custom-call(f32[16,8,128]{2,1,0:T(8,128)S(1)} %all_to_all.34.recv_ref, f32[32,256]{1,0:T(8,128)S(1)} %get-tuple-element.38.scaled_ref), custom_call_target="tpu_custom_call" | custom-call | tf_op jit(solution)/shard_map/pallas_call | solution.py:365
  (18 shorter events, 3.4 us)
Async XLA Ops:
  2.0 34.6 %all-to-all-start = ((bf16[16,200,128]{2,1,0:T(8,128)(2,1)}), bf16[16,200,128]{2,1,0:T(8,128)(2,1)S(1)}, u32[]{:S(2)}, u32[]{:S(2)}) async-start(bf16[16,200,128]{2,1,0:T(8,128)(2,1)} %get-tuple-element.24), calls=%async_computation | async-start | bytes 1638400 | tf_op jit(solution)/shard_map/all_to_all | solution.py:359
  9.6 1.9 %collective-permute-start = (bf16[80,128]{1,0:T(8,128)(2,1)S(1)}, bf16[80,128]{1,0:T(8,128)(2,1)S(1)}, u32[]{:S(2)}, u32[]{:S(2)}) collective-permute-start(bf16[80,128]{1,0:T(8,128)(2,1)S(1)} %get-tuple-element.22.mine_ref), channel_id=1, source_target_pairs={{0,1},{1,0},{2,3},{3,2},{4,5},{5,4},{6,7},{7,6},{8,9},{9,8},{10,11... | collective-permute-start | bytes 61448 | tf_op jit(solution)/shard_map/ppermute | solution.py:362
  11.5 6.7 %collective-permute-start.1 = (bf16[2,80,128]{2,1,0:T(8,128)(2,1)S(1)}, bf16[2,80,128]{2,1,0:T(8,128)(2,1)S(1)}, u32[]{:S(2)}, u32[]{:S(2)}) collective-permute-start(bf16[2,80,128]{2,1,0:T(8,128)(2,1)S(1)} %shard_map.29.pair_ref), channel_id=1, source_target_pairs={{0,2},{2,4},{4,6},{6,8},{8,10},{10,12},{12,14},{14,0},{1,15},{3,1}... | collective-permute-start | bytes 122888 | tf_op jit(solution)/shard_map/ppermute | solution.py:391
  18.2 4.4 %collective-permute-start.2 = (bf16[2,80,128]{2,1,0:T(8,128)(2,1)S(1)}, bf16[2,80,128]{2,1,0:T(8,128)(2,1)S(1)}, u32[]{:S(2)}, u32[]{:S(2)}) collective-permute-start(bf16[2,80,128]{2,1,0:T(8,128)(2,1)S(1)} %collective-permute-done.1.refs_0_), channel_id=1, source_target_pairs={{0,2},{2,4},{4,6},{6,8},{8,10},{10,12},{12,14},{14,0},{1,15},{3,1}... | collective-permute-start | bytes 122888 | tf_op jit(solution)/shard_map/ppermute | solution.py:391
  22.5 4.4 %collective-permute-start.3 = (bf16[2,80,128]{2,1,0:T(8,128)(2,1)S(1)}, bf16[2,80,128]{2,1,0:T(8,128)(2,1)S(1)}, u32[]{:S(2)}, u32[]{:S(2)}) collective-permute-start(bf16[2,80,128]{2,1,0:T(8,128)(2,1)S(1)} %collective-permute-done.2.refs_1_), channel_id=1, source_target_pairs={{0,2},{2,4},{4,6},{6,8},{8,10},{10,12},{12,14},{14,0},{1,15},{3,1}... | collective-permute-start | bytes 122888 | tf_op jit(solution)/shard_map/ppermute | solution.py:391
  26.9 4.4 %collective-permute-start.4 = (bf16[2,80,128]{2,1,0:T(8,128)(2,1)S(1)}, bf16[2,80,128]{2,1,0:T(8,128)(2,1)S(1)}, u32[]{:S(2)}, u32[]{:S(2)}) collective-permute-start(bf16[2,80,128]{2,1,0:T(8,128)(2,1)S(1)} %collective-permute-done.3.refs_2_), channel_id=1, source_target_pairs={{0,2},{2,4},{4,6},{6,8},{8,10},{10,12},{12,14},{14,0},{1,15},{3,1}... | collective-permute-start | bytes 122888 | tf_op jit(solution)/shard_map/ppermute | solution.py:391
  30.2 5.2 %collective-permute-start.5 = (bf16[2,80,128]{2,1,0:T(8,128)(2,1)S(1)}, bf16[2,80,128]{2,1,0:T(8,128)(2,1)S(1)}, u32[]{:S(2)}, u32[]{:S(2)}) collective-permute-start(bf16[2,80,128]{2,1,0:T(8,128)(2,1)S(1)} %collective-permute-done.1.refs_0_), channel_id=1, source_target_pairs={{0,1},{1,0},{2,3},{3,2},{4,5},{5,4},{6,7},{7,6},{8,9},{9,8},{10,11... | collective-permute-start | bytes 122888 | tf_op jit(solution)/shard_map/ppermute | solution.py:362
  30.2 5.2 %collective-permute-start.6 = (bf16[2,80,128]{2,1,0:T(8,128)(2,1)S(1)}, bf16[2,80,128]{2,1,0:T(8,128)(2,1)S(1)}, u32[]{:S(2)}, u32[]{:S(2)}) collective-permute-start(bf16[2,80,128]{2,1,0:T(8,128)(2,1)S(1)} %collective-permute-done.2.refs_1_), channel_id=1, source_target_pairs={{0,1},{1,0},{2,3},{3,2},{4,5},{5,4},{6,7},{7,6},{8,9},{9,8},{10,11... | collective-permute-start | bytes 122888 | tf_op jit(solution)/shard_map/ppermute | solution.py:362
  30.7 4.7 %collective-permute-start.7 = (bf16[2,80,128]{2,1,0:T(8,128)(2,1)S(1)}, bf16[2,80,128]{2,1,0:T(8,128)(2,1)S(1)}, u32[]{:S(2)}, u32[]{:S(2)}) collective-permute-start(bf16[2,80,128]{2,1,0:T(8,128)(2,1)S(1)} %collective-permute-done.3.refs_2_), channel_id=1, source_target_pairs={{0,1},{1,0},{2,3},{3,2},{4,5},{5,4},{6,7},{7,6},{8,9},{9,8},{10,11... | collective-permute-start | bytes 122888 | tf_op jit(solution)/shard_map/ppermute | solution.py:362
  31.3 4.9 %collective-permute-start.8 = (bf16[2,80,128]{2,1,0:T(8,128)(2,1)S(1)}, bf16[2,80,128]{2,1,0:T(8,128)(2,1)S(1)}, u32[]{:S(2)}, u32[]{:S(2)}) collective-permute-start(bf16[2,80,128]{2,1,0:T(8,128)(2,1)S(1)} %collective-permute-done.4.refs_3_), channel_id=1, source_target_pairs={{0,1},{1,0},{2,3},{3,2},{4,5},{5,4},{6,7},{7,6},{8,9},{9,8},{10,11... | collective-permute-start | bytes 122888 | tf_op jit(solution)/shard_map/ppermute | solution.py:362
  39.7 3.7 %collective-permute-start.9 = (f32[8,48,128]{2,1,0:T(8,128)S(1)}, f32[8,48,128]{2,1,0:T(8,128)S(1)}, u32[]{:S(2)}, u32[]{:S(2)}) collective-permute-start(f32[8,48,128]{2,1,0:T(8,128)S(1)} %get-tuple-element.31), channel_id=1, source_target_pairs={{0,1},{1,0},{2,3},{3,2},{4,5},{5,4},{6,7},{7,6},{8,9},{9,8},{10,11... | collective-permute-start | bytes 589832 | tf_op jit(solution)/shard_map/ppermute | solution.py:362
  75.0 4.5 %collective-permute-start.10 = (f32[8,48,128]{2,1,0:T(8,128)S(1)}, f32[8,48,128]{2,1,0:T(8,128)S(1)}, u32[]{:S(2)}, u32[]{:S(2)}) collective-permute-start(f32[8,48,128]{2,1,0:T(8,128)S(1)} %get-tuple-element.35), channel_id=1, source_target_pairs={{0,1},{1,0},{2,3},{3,2},{4,5},{5,4},{6,7},{7,6},{8,9},{9,8},{10,11... | collective-permute-start | bytes 589832 | tf_op jit(solution)/shard_map/ppermute | solution.py:362

commit v9 on v7

--- a/solution.py
+++ b/solution.py
@@ -85,12 +85,13 @@
         main, rest = main_and_rest(pts)
         rows_ref[...] = jnp.concatenate([main, rest], axis=0).astype(BF16)
         flat = jnp.concatenate([main, widen(pts[:, LANES:])], axis=1)
-        flat = jnp.concatenate([flat, jnp.zeros_like(flat)], axis=0).T[0:group]
-        norm = jnp.sum(flat * flat, axis=1, keepdims=True) * (-0.5 * log_scale)
-        lane = lane_of(flat.shape)
+        norm = jnp.sum(flat * flat, axis=0, keepdims=True) * (-0.5 * log_scale)
+        row = row_of((8, flat.shape[1]))
+        extra = jnp.where((row >= ONES - NORM) & (row < END - NORM), 1.0, 0.0)
         for k, piece in enumerate(split(norm)):
-            flat = jnp.where(lane == NORM + k, piece, flat)
-        flat = jnp.where((lane >= ONES) & (lane < END), 1.0, flat)
+            extra = jnp.where(row == k, piece, extra)
+        blank = jnp.zeros((LANES - NORM - 8, flat.shape[1]), F32)
+        flat = jnp.concatenate([flat, extra, blank], axis=0).T[0:group]
         loads[1].wait()
         main, rest = main_and_rest(vectors_ref[...].astype(F32))
         block_ref[...] = jnp.concatenate([flat, main, rest], axis=0).astype(BF16)
@@ -158,7 +159,7 @@
     main, rest = blocks_of(send_ref.shape[0])
     chunk = 512
 
-    def product(at, width):
+    def weights(at, width):
         right = right_ref[:, at : at + width]
         for start in range(0, total, chunk):
             left = left_ref[start : start + chunk, :]
@@ -166,22 +167,36 @@
                 jnp.concatenate([left, left], axis=1), right, preferred_element_type=F32
             )
             aff_ref[start : start + chunk, at : at + width] = jnp.exp2(power).astype(BF16)
+
+    def product(at, width):
         return jnp.dot(
             vec_ref[...], aff_ref[:, at : at + width], preferred_element_type=F32
         )
 
-    for at, width in main:
+    def send_main(at, width):
         out = product(at, width)
         for k in range(width // LANES):
             tile = out[:, k * LANES : (k + 1) * LANES]
             send_ref[at // LANES + k, 0:32, :] = tile[0:32]
-            send_ref[at // LANES + k, 40:48, :] = tile[32:40]
-    out = product(*rest)
-    for m in range(rest[1] // LANES):
-        tile = out[:, m * LANES : (m + 1) * LANES]
-        for q in range(4):
-            send_ref[4 * m + q, 32:40, :] = fold(tile[0:32], q)
-            send_ref[4 * m + q, 41:42, :] = roll(tile[32:40], -REST * q)[0:1]
+            send_ref[at // LANES + k, 40:41, :] = tile[32:33]
+
+    def send_rest(at, width):
+        out = product(at, width)
+        row = row_of((8, LANES))
+        for m in range(width // LANES):
+            tile = out[:, m * LANES : (m + 1) * LANES]
+            for q in range(4):
+                send_ref[4 * m + q, 32:40, :] = fold(tile[0:32], q)
+                degree = jnp.broadcast_to(roll(tile[32:40], -REST * q)[0:1], (8, LANES))
+                send_ref[4 * m + q, 40:48, :] = jnp.where(row == 1, degree, 0.0)
+
+    weights(*main[0])
+    weights(*rest)
+    send_rest(*rest)
+    send_main(*main[0])
+    for block in main[1:]:
+        weights(*block)
+        send_main(*block)
 
 
 def away_body(right_ref, cols_ref, aff_ref, send_ref, left_ref, vec_ref):
@@ -224,8 +239,7 @@
     degree_ref[0:8, :] = jnp.broadcast_to(total[40:41], (8, LANES))
     degree_ref[8:16, :] = rest
     main, rest = total[0:32] / total[40:41], total[32:40] / rest
-    gram = fold(widen(gram_of(whole(main, rest))))
-    copies(spread_ref, jnp.concatenate([main, rest, gram], axis=0))
+    copies(spread_ref, jnp.concatenate([main, rest], axis=0))
 
 
 def put_vectors(spread_ref, vec_ref):
@@ -243,33 +257,42 @@
         put(count + m, unfold([spread_ref[4 * m + q, 32:40, :] for q in range(4)]))
 
 
-def second_product(aff_ref, vec_ref, gram, send_ref):
+def second_product(aff_ref, vec_ref, send_ref):
     main, rest = blocks_of(send_ref.shape[0])
 
     def product(at, width):
         out = jnp.dot(vec_ref[...], aff_ref[:, at : at + width], preferred_element_type=F32)
         return out[0:32] + out[32:64]
 
+    out = product(*rest)
+    for m in range(rest[1] // LANES):
+        for q in range(4):
+            send_ref[4 * m + q, 32:40, :] = fold(out[:, m * LANES : (m + 1) * LANES], q)
     for at, width in main:
         out = product(at, width)
         for k in range(width // LANES):
             send_ref[at // LANES + k, 0:32, :] = out[:, k * LANES : (k + 1) * LANES]
-            send_ref[at // LANES + k, 40:48, :] = gram
-    out = product(*rest)
-    for m in range(rest[1] // LANES):
-        for q in range(4):
-            send_ref[4 * m + q, 32:40, :] = fold(out[:, m * LANES : (m + 1) * LANES], q)
+
+
+def put_gram(gram, send_ref):
+    for i in range(send_ref.shape[0]):
+        send_ref[i, 40:48, :] = gram
 
 
 def away_again_body(aff_ref, spread_ref, send_ref, vec_ref, gram_ref):
-    gram = jnp.sum(spread_ref[:, 40:48, :], axis=0)
+    put_vectors(spread_ref, vec_ref)
+    vec = vec_ref[...]
+    gram = lax.dot_general(vec, vec, (((1,), (1,)), ((), ())), preferred_element_type=F32)
+    gram = gram[0:32] + gram[32:64]
+    gram = fold(widen(gram[:, 0:32] + gram[:, 32:64]))
     gram_ref[...] = gram
-    put_vectors(spread_ref, vec_ref)
-    second_product(aff_ref, vec_ref, gram, send_ref)
+    second_product(aff_ref, vec_ref, send_ref)
+    put_gram(gram, send_ref)
 
 
 def home_again_body(aff_ref, vec_ref, gram_ref, send_ref):
-    second_product(aff_ref, vec_ref, gram_ref[...], send_ref)
+    second_product(aff_ref, vec_ref, send_ref)
+    put_gram(gram_ref[...], send_ref)
 
 
 def solved(gram, right):
@@ -383,7 +406,7 @@
     home_aff, home_send = call(affinity_product, (aff_shape, send_shape), left, home_right, vec)
     send = call(join_body, send_shape, home_send, other)
     spread, degree = call(
-        scale_body, (shape((row, 48, LANES), F32), shape((16, LANES), F32)), exchange(send, "z")
+        scale_body, (shape((row, 40, LANES), F32), shape((16, LANES), F32)), exchange(send, "z")
     )
     away_send, vec, gram = call(
         away_again_body,

time: 110 us -> 109 us (level)
  no operation moved by 1% of the time
where the time goes in v9:
time: 109 us
  blocking collectives  83.8 us (77%)
  Pallas kernels  13.3 us (12%)
  starting transfers between devices  11.3 us (10%)
    all_to_all x5, blocking collectives, exchange(): return lax.all_to_all(x, axis, 0, 0, tiled=True)  62.2 us
    all_gather x1, blocking collectives, shards(): rows = lax.all_gather(rows, ('z', 'core'))  21.7 us
    pallas_call x12, Pallas kernels, call(): pl.pallas_call(body, out_shape=out_shape, scratch_shapes=scratch, compile...  13.3 us
    all_to_all x1, starting transfers between devices, exchange(): return lax.all_to_all(x, axis, 0, 0, tiled=True)  7.58 us
    ppermute x2, starting transfers between devices, swap(): return lax.ppermute(x, 'core', [(0, 1), (1, 0)])  3.74 us
  transfers between devices with their start and end apart: 3, of which 0 were waited for; matrix products, arithmetic and copies ran while one was open for 0% of the time, Pallas kernels for 4%

profile of v9, /device:TPU:1, one launch (start us, length us, event | category | flops | bytes accessed | tf_op | source)
XLA Modules:
  0.0 108.6 jit_solution(6533548057077996381)
XLA Ops:
  0.0 2.0 %shard_map.28 = (bf16[16,200,128]{2,1,0:T(8,128)(2,1)}, bf16[80,128]{1,0:T(8,128)(2,1)S(1)}) custom-call(bf16[64,160]{1,0:T(8,128)(2,1)} %bitcast.5, bf16[32,160]{1,0:T(8,128)(2,1)} %bitcast.6), custom_call_target="tpu_custom_call" | custom-call | tf_op jit(solution)/shard_map/pallas_call | solution.py:370
  2.0 7.6 %all-to-all-start = ((bf16[16,200,128]{2,1,0:T(8,128)(2,1)}), bf16[16,200,128]{2,1,0:T(8,128)(2,1)S(1)}, u32[]{:S(2)}, u32[]{:S(2)}) async-start(bf16[16,200,128]{2,1,0:T(8,128)(2,1)} %get-tuple-element.24), calls=%async_computation | async-start | bytes 1638400 | tf_op jit(solution)/shard_map/all_to_all | solution.py:364
  9.6 21.7 %all-gather = bf16[1280,128]{1,0:T(8,128)(2,1)S(1)} all-gather(bf16[80,128]{1,0:T(8,128)(2,1)S(1)} %get-tuple-element.22), channel_id=2, replica_groups=mesh['row'=16,'z'=8,'core'=2] {'z','core'}, dimensions={0}, use_global_device_ids=true | all-gather | bytes 348160 | tf_op jit(solution)/shard_map/all_gather | solution.py:390
  31.3 0.3 shard_map.29
  31.6 0.0 all-to-all-done.cols_ref
  31.6 2.9 %shard_map.30 = (bf16[2560,1280]{1,0:T(8,128)(2,1)S(1)}, f32[8,48,128]{2,1,0:T(8,128)S(1)}, bf16[2560,128]{1,0:T(8,128)(2,1)S(1)}, bf16[48,2560]{1,0:T(8,128)(2,1)S(1)}) custom-call(bf16[256,1280]{1,0:T(8,128)(2,1)S(1)} %get-tuple-element.23.right_ref, bf16[16,200,128]{2,1,0:T(8,128)(2,1)S(1)} %all-to-all-done.cols_ref), custom_call_target="tpu_custom_call" | custom-call | tf_op jit(solution)/shard_map/pallas_call | solution.py:370
  34.6 0.3 collective-permute-start
  34.8 2.9 %shard_map.31 = (bf16[2560,1280]{1,0:T(8,128)(2,1)S(1)}, f32[8,48,128]{2,1,0:T(8,128)S(1)}) custom-call(bf16[2560,128]{1,0:T(8,128)(2,1)S(1)} %get-tuple-element.25.left_ref, bf16[256,1280]{1,0:T(8,128)(2,1)S(1)} %get-tuple-element.26.right_ref, bf16[48,2560]{1,0:T(8,128)(2,1)S(1)} %get-tuple-element.27.vec_ref), custom_call_target="tpu_custom_call" | custom-call | tf_op jit(solution)/shard_map/pallas_call | solution.py:370
  37.7 0.0 collective-permute-done.other_ref
  37.8 12.6 %all_to_all.30.recv_ref = f32[8,48,128]{2,1,0:T(8,128)S(1)} all-to-all(f32[8,48,128]{2,1,0:T(8,128)S(1)} %shard_map.32), channel_id=1, replica_groups=mesh['row'=16,'z'=8,'core'=2] {'z'}, dimensions={0} | all-to-all | bytes 393216 | tf_op jit(solution)/shard_map/all_to_all | solution.py:364
  50.4 0.1 shard_map.33
  50.5 14.4 %all_to_all.31.spread_ref = f32[16,40,128]{2,1,0:T(8,128)S(1)} all-to-all(f32[16,40,128]{2,1,0:T(8,128)S(1)} %get-tuple-element.32), channel_id=1, replica_groups=mesh['row'=16,'z'=8,'core'=2] {'row'}, dimensions={0} | all-to-all | bytes 655360 | tf_op jit(solution)/shard_map/all_to_all | solution.py:364
  64.9 1.3 %shard_map.34 = (f32[8,48,128]{2,1,0:T(8,128)S(1)}, bf16[64,2560]{1,0:T(8,128)(2,1)S(1)}, f32[8,128]{1,0:T(8,128)S(1)}) custom-call(bf16[2560,1280]{1,0:T(8,128)(2,1)S(1)} %get-tuple-element.29.aff_ref, f32[16,40,128]{2,1,0:T(8,128)S(1)} %all_to_all.31.spread_ref), custom_call_target="tpu_custom_call" | custom-call | tf_op jit(solution)/shard_map/pallas_call | solution.py:370
  66.2 3.5 %collective-permute-start.1 = (f32[8,48,128]{2,1,0:T(8,128)S(1)}, f32[8,48,128]{2,1,0:T(8,128)S(1)}, u32[]{:S(2)}, u32[]{:S(2)}) collective-permute-start(f32[8,48,128]{2,1,0:T(8,128)S(1)} %get-tuple-element.35), channel_id=1, source_target_pairs={{0,1},{1,0},{2,3},{3,2},{4,5},{5,4},{6,7},{7,6},{8,9},{9,8},{10,11... | collective-permute-start | bytes 589832 | tf_op jit(solution)/shard_map/ppermute | solution.py:367
  69.6 1.2 %shard_map.35.mine_ref = f32[8,48,128]{2,1,0:T(8,128)S(1)} custom-call(bf16[2560,1280]{1,0:T(8,128)(2,1)S(1)} %get-tuple-element.28.aff_ref, bf16[64,2560]{1,0:T(8,128)(2,1)S(1)} %get-tuple-element.33.vec_ref, f32[8,128]{1,0:T(8,128)S(1)} %get-tuple-element.34.gram_ref), custom_call_target="tpu_custom_call" | custom-call | tf_op jit(solution)/shard_map/pallas_call | solution.py:370
  70.9 0.0 collective-permute-done.1.other_ref
  70.9 13.3 %all_to_all.32.recv_ref = f32[8,48,128]{2,1,0:T(8,128)S(1)} all-to-all(f32[8,48,128]{2,1,0:T(8,128)S(1)} %shard_map.36), channel_id=1, replica_groups=mesh['row'=16,'z'=8,'core'=2] {'z'}, dimensions={0} | all-to-all | bytes 393216 | tf_op jit(solution)/shard_map/all_to_all | solution.py:364
  84.3 1.0 shard_map.37
  85.3 9.7 %all_to_all.33.recv_ref = f32[16,8,128]{2,1,0:T(8,128)S(1)} all-to-all(f32[16,8,128]{2,1,0:T(8,128)S(1)} %get-tuple-element.37), channel_id=1, replica_groups=mesh['row'=16,'z'=8,'core'=2] {'row'}, dimensions={0} | all-to-all | bytes 131072 | tf_op jit(solution)/shard_map/all_to_all | solution.py:364
  95.0 12.1 %all_to_all.34.recv_ref = f32[16,8,128]{2,1,0:T(8,128)S(1)} all-to-all(f32[16,8,128]{2,1,0:T(8,128)S(1)} %shard_map.38), channel_id=1, replica_groups=mesh['row'=16,'z'=8,'core'=2] {'z','core'}, dimensions={0} | all-to-all | bytes 131072 | tf_op jit(solution)/shard_map/all_to_all | solution.py:364
  107.1 1.4 %shard_map.39 = f32[32,160]{1,0:T(8,128)} custom-call(f32[16,8,128]{2,1,0:T(8,128)S(1)} %all_to_all.34.recv_ref, f32[32,256]{1,0:T(8,128)S(1)} %get-tuple-element.38.scaled_ref), custom_call_target="tpu_custom_call" | custom-call | tf_op jit(solution)/shard_map/pallas_call | solution.py:370
  (3 shorter events, 0.1 us)
Async XLA Ops:
  2.0 29.6 %all-to-all-start = ((bf16[16,200,128]{2,1,0:T(8,128)(2,1)}), bf16[16,200,128]{2,1,0:T(8,128)(2,1)S(1)}, u32[]{:S(2)}, u32[]{:S(2)}) async-start(bf16[16,200,128]{2,1,0:T(8,128)(2,1)} %get-tuple-element.24), calls=%async_computation | async-start | bytes 1638400 | tf_op jit(solution)/shard_map/all_to_all | solution.py:364
  34.6 3.2 %collective-permute-start = (f32[8,48,128]{2,1,0:T(8,128)S(1)}, f32[8,48,128]{2,1,0:T(8,128)S(1)}, u32[]{:S(2)}, u32[]{:S(2)}) collective-permute-start(f32[8,48,128]{2,1,0:T(8,128)S(1)} %get-tuple-element.31), channel_id=1, source_target_pairs={{0,1},{1,0},{2,3},{3,2},{4,5},{5,4},{6,7},{7,6},{8,9},{9,8},{10,11... | collective-permute-start | bytes 589832 | tf_op jit(solution)/shard_map/ppermute | solution.py:367
  66.2 4.7 %collective-permute-start.1 = (f32[8,48,128]{2,1,0:T(8,128)S(1)}, f32[8,48,128]{2,1,0:T(8,128)S(1)}, u32[]{:S(2)}, u32[]{:S(2)}) collective-permute-start(f32[8,48,128]{2,1,0:T(8,128)S(1)} %get-tuple-element.35), channel_id=1, source_target_pairs={{0,1},{1,0},{2,3},{3,2},{4,5},{5,4},{6,7},{7,6},{8,9},{9,8},{10,11... | collective-permute-start | bytes 589832 | tf_op jit(solution)/shard_map/ppermute | solution.py:367

commit v10 on v9

--- a/solution.py
+++ b/solution.py
@@ -296,10 +296,16 @@
 
 
 def solved(gram, right):
-    size = gram.shape[0]
+    size = 4 * gram.shape[0]
     wide = right.shape[1] // LANES
     columns = [
-        jnp.broadcast_to(gram[8 * (k // 8) :, k : k + 1], (size - 8 * (k // 8), LANES))
+        jnp.concatenate(
+            [
+                jnp.broadcast_to(gram[:, REST * g + k : REST * g + k + 1], (8, LANES))
+                for g in range(k // 8, 4)
+            ],
+            axis=0,
+        )
         for k in range(size)
     ]
     rows = [right[8 * g : 8 * g + 8] for g in range(size // 8)]
@@ -331,7 +337,7 @@
         total = jnp.sum(recv_ref[...], axis=0)
         main = total[0:32] / degree_ref[0:1, :]
         rest = total[32:40] / degree_ref[8:16, :]
-        scaled = solved(unfold([total[40:48]]) / points, whole(main, rest))
+        scaled = solved(total[40:48] / points, whole(main, rest))
         scaled_ref[...] = scaled
         copies(gram_ref, fold(widen(gram_of(scaled))))
 
@@ -344,7 +350,7 @@
 
 def last_body(points):
     def body(recv_ref, scaled_ref, out_ref):
-        gram = unfold([jnp.sum(recv_ref[...], axis=0)]) / points
+        gram = jnp.sum(recv_ref[...], axis=0) / points
         out_ref[...] = solved(gram, scaled_ref[...])[:, 0 : out_ref.shape[1]]
 
     return body
@@ -419,12 +425,13 @@
     send = call(join_body, send_shape, home_send, other)
     scaled, gram = call(
         middle_body(total),
-        (shape((32, 2 * LANES), F32), shape((row, 8, LANES), F32)),
+        (shape((32, 2 * LANES), F32), shape((col, 8, LANES), F32)),
         exchange(send, "z"),
         degree,
     )
-    gram = call(again_body, shape((col, 8, LANES), F32), exchange(gram, "row"))
-    out = call(last_body(total), shape((32, group), F32), exchange(gram, ("z", "core")), scaled)
+    gram = exchange(gram, ("z", "core"))
+    gram = call(again_body, shape((row, 8, LANES), F32), gram)
+    out = call(last_body(total), shape((32, group), F32), exchange(gram, "row"), scaled)
     return out.T
 
 

time: 109 us -> 107 us (0.982)
  blocking collectives: 83.8 us -> 82.4 us
    all_to_all x5, blocking collectives: 62.2 us -> 60.7 us  [exchange(): return lax.all_to_all(x, axis, 0, 0, tiled=True)]
where the time goes in v10:
time: 107 us
  blocking collectives  82.4 us (77%)
  Pallas kernels  13.1 us (12%)
  starting transfers between devices  11.3 us (11%)
    all_to_all x5, blocking collectives, exchange(): return lax.all_to_all(x, axis, 0, 0, tiled=True)  60.7 us
    all_gather x1, blocking collectives, shards(): rows = lax.all_gather(rows, ('z', 'core'))  21.7 us
    pallas_call x12, Pallas kernels, call(): pl.pallas_call(body, out_shape=out_shape, scratch_shapes=scratch, compile...  13.1 us
    all_to_all x1, starting transfers between devices, exchange(): return lax.all_to_all(x, axis, 0, 0, tiled=True)  7.58 us
    ppermute x2, starting transfers between devices, swap(): return lax.ppermute(x, 'core', [(0, 1), (1, 0)])  3.74 us
  transfers between devices with their start and end apart: 3, of which 0 were waited for; matrix products, arithmetic and copies ran while one was open for 0% of the time, Pallas kernels for 4%

profile of v10, /device:TPU:1, one launch (start us, length us, event | category | flops | bytes accessed | tf_op | source)
XLA Modules:
  0.0 106.9 jit_solution(18137792079432249759)
XLA Ops:
  0.0 2.0 %shard_map.28 = (bf16[16,200,128]{2,1,0:T(8,128)(2,1)}, bf16[80,128]{1,0:T(8,128)(2,1)S(1)}) custom-call(bf16[64,160]{1,0:T(8,128)(2,1)} %bitcast.5, bf16[32,160]{1,0:T(8,128)(2,1)} %bitcast.6), custom_call_target="tpu_custom_call" | custom-call | tf_op jit(solution)/shard_map/pallas_call | solution.py:376
  2.0 7.6 %all-to-all-start = ((bf16[16,200,128]{2,1,0:T(8,128)(2,1)}), bf16[16,200,128]{2,1,0:T(8,128)(2,1)S(1)}, u32[]{:S(2)}, u32[]{:S(2)}) async-start(bf16[16,200,128]{2,1,0:T(8,128)(2,1)} %get-tuple-element.24), calls=%async_computation | async-start | bytes 1638400 | tf_op jit(solution)/shard_map/all_to_all | solution.py:370
  9.6 21.7 %all-gather = bf16[1280,128]{1,0:T(8,128)(2,1)S(1)} all-gather(bf16[80,128]{1,0:T(8,128)(2,1)S(1)} %get-tuple-element.22), channel_id=2, replica_groups=mesh['row'=16,'z'=8,'core'=2] {'z','core'}, dimensions={0}, use_global_device_ids=true | all-gather | bytes 348160 | tf_op jit(solution)/shard_map/all_gather | solution.py:396
  31.3 0.3 shard_map.29
  31.6 0.0 all-to-all-done.cols_ref
  31.6 2.9 %shard_map.30 = (bf16[2560,1280]{1,0:T(8,128)(2,1)S(1)}, f32[8,48,128]{2,1,0:T(8,128)S(1)}, bf16[2560,128]{1,0:T(8,128)(2,1)S(1)}, bf16[48,2560]{1,0:T(8,128)(2,1)S(1)}) custom-call(bf16[256,1280]{1,0:T(8,128)(2,1)S(1)} %get-tuple-element.23.right_ref, bf16[16,200,128]{2,1,0:T(8,128)(2,1)S(1)} %all-to-all-done.cols_ref), custom_call_target="tpu_custom_call" | custom-call | tf_op jit(solution)/shard_map/pallas_call | solution.py:376
  34.6 0.3 collective-permute-start
  34.8 2.9 %shard_map.31 = (bf16[2560,1280]{1,0:T(8,128)(2,1)S(1)}, f32[8,48,128]{2,1,0:T(8,128)S(1)}) custom-call(bf16[2560,128]{1,0:T(8,128)(2,1)S(1)} %get-tuple-element.25.left_ref, bf16[256,1280]{1,0:T(8,128)(2,1)S(1)} %get-tuple-element.26.right_ref, bf16[48,2560]{1,0:T(8,128)(2,1)S(1)} %get-tuple-element.27.vec_ref), custom_call_target="tpu_custom_call" | custom-call | tf_op jit(solution)/shard_map/pallas_call | solution.py:376
  37.7 0.0 collective-permute-done.other_ref
  37.8 12.6 %all_to_all.30.recv_ref = f32[8,48,128]{2,1,0:T(8,128)S(1)} all-to-all(f32[8,48,128]{2,1,0:T(8,128)S(1)} %shard_map.32), channel_id=1, replica_groups=mesh['row'=16,'z'=8,'core'=2] {'z'}, dimensions={0} | all-to-all | bytes 393216 | tf_op jit(solution)/shard_map/all_to_all | solution.py:370
  50.4 0.1 shard_map.33
  50.5 14.4 %all_to_all.31.spread_ref = f32[16,40,128]{2,1,0:T(8,128)S(1)} all-to-all(f32[16,40,128]{2,1,0:T(8,128)S(1)} %get-tuple-element.32), channel_id=1, replica_groups=mesh['row'=16,'z'=8,'core'=2] {'row'}, dimensions={0} | all-to-all | bytes 655360 | tf_op jit(solution)/shard_map/all_to_all | solution.py:370
  64.9 1.3 %shard_map.34 = (f32[8,48,128]{2,1,0:T(8,128)S(1)}, bf16[64,2560]{1,0:T(8,128)(2,1)S(1)}, f32[8,128]{1,0:T(8,128)S(1)}) custom-call(bf16[2560,1280]{1,0:T(8,128)(2,1)S(1)} %get-tuple-element.29.aff_ref, f32[16,40,128]{2,1,0:T(8,128)S(1)} %all_to_all.31.spread_ref), custom_call_target="tpu_custom_call" | custom-call | tf_op jit(solution)/shard_map/pallas_call | solution.py:376
  66.2 3.5 %collective-permute-start.1 = (f32[8,48,128]{2,1,0:T(8,128)S(1)}, f32[8,48,128]{2,1,0:T(8,128)S(1)}, u32[]{:S(2)}, u32[]{:S(2)}) collective-permute-start(f32[8,48,128]{2,1,0:T(8,128)S(1)} %get-tuple-element.35), channel_id=1, source_target_pairs={{0,1},{1,0},{2,3},{3,2},{4,5},{5,4},{6,7},{7,6},{8,9},{9,8},{10,11... | collective-permute-start | bytes 589832 | tf_op jit(solution)/shard_map/ppermute | solution.py:373
  69.6 1.2 %shard_map.35.mine_ref = f32[8,48,128]{2,1,0:T(8,128)S(1)} custom-call(bf16[2560,1280]{1,0:T(8,128)(2,1)S(1)} %get-tuple-element.28.aff_ref, bf16[64,2560]{1,0:T(8,128)(2,1)S(1)} %get-tuple-element.33.vec_ref, f32[8,128]{1,0:T(8,128)S(1)} %get-tuple-element.34.gram_ref), custom_call_target="tpu_custom_call" | custom-call | tf_op jit(solution)/shard_map/pallas_call | solution.py:376
  70.9 0.0 collective-permute-done.1.other_ref
  70.9 13.3 %all_to_all.32.recv_ref = f32[8,48,128]{2,1,0:T(8,128)S(1)} all-to-all(f32[8,48,128]{2,1,0:T(8,128)S(1)} %shard_map.36), channel_id=1, replica_groups=mesh['row'=16,'z'=8,'core'=2] {'z'}, dimensions={0} | all-to-all | bytes 393216 | tf_op jit(solution)/shard_map/all_to_all | solution.py:370
  84.3 0.9 shard_map.37
  85.1 10.7 %all_to_all.33.recv_ref = f32[16,8,128]{2,1,0:T(8,128)S(1)} all-to-all(f32[16,8,128]{2,1,0:T(8,128)S(1)} %get-tuple-element.37), channel_id=1, replica_groups=mesh['row'=16,'z'=8,'core'=2] {'z','core'}, dimensions={0} | all-to-all | bytes 131072 | tf_op jit(solution)/shard_map/all_to_all | solution.py:370
  95.9 9.7 %all_to_all.34.recv_ref = f32[16,8,128]{2,1,0:T(8,128)S(1)} all-to-all(f32[16,8,128]{2,1,0:T(8,128)S(1)} %shard_map.38), channel_id=1, replica_groups=mesh['row'=16,'z'=8,'core'=2] {'row'}, dimensions={0} | all-to-all | bytes 131072 | tf_op jit(solution)/shard_map/all_to_all | solution.py:370
  105.6 1.3 %shard_map.39 = f32[32,160]{1,0:T(8,128)} custom-call(f32[16,8,128]{2,1,0:T(8,128)S(1)} %all_to_all.34.recv_ref, f32[32,256]{1,0:T(8,128)S(1)} %get-tuple-element.38.scaled_ref), custom_call_target="tpu_custom_call" | custom-call | tf_op jit(solution)/shard_map/pallas_call | solution.py:376
  (3 shorter events, 0.1 us)
Async XLA Ops:
  2.0 29.6 %all-to-all-start = ((bf16[16,200,128]{2,1,0:T(8,128)(2,1)}), bf16[16,200,128]{2,1,0:T(8,128)(2,1)S(1)}, u32[]{:S(2)}, u32[]{:S(2)}) async-start(bf16[16,200,128]{2,1,0:T(8,128)(2,1)} %get-tuple-element.24), calls=%async_computation | async-start | bytes 1638400 | tf_op jit(solution)/shard_map/all_to_all | solution.py:370
  34.6 3.2 %collective-permute-start = (f32[8,48,128]{2,1,0:T(8,128)S(1)}, f32[8,48,128]{2,1,0:T(8,128)S(1)}, u32[]{:S(2)}, u32[]{:S(2)}) collective-permute-start(f32[8,48,128]{2,1,0:T(8,128)S(1)} %get-tuple-element.31), channel_id=1, source_target_pairs={{0,1},{1,0},{2,3},{3,2},{4,5},{5,4},{6,7},{7,6},{8,9},{9,8},{10,11... | collective-permute-start | bytes 589832 | tf_op jit(solution)/shard_map/ppermute | solution.py:373
  66.2 4.7 %collective-permute-start.1 = (f32[8,48,128]{2,1,0:T(8,128)S(1)}, f32[8,48,128]{2,1,0:T(8,128)S(1)}, u32[]{:S(2)}, u32[]{:S(2)}) collective-permute-start(f32[8,48,128]{2,1,0:T(8,128)S(1)} %get-tuple-element.35), channel_id=1, source_target_pairs={{0,1},{1,0},{2,3},{3,2},{4,5},{5,4},{6,7},{7,6},{8,9},{9,8},{10,11... | collective-permute-start | bytes 589832 | tf_op jit(solution)/shard_map/ppermute | solution.py:373

commit v11 on v10

--- a/solution.py
+++ b/solution.py
@@ -199,16 +199,19 @@
         send_main(*block)
 
 
-def away_body(right_ref, cols_ref, aff_ref, send_ref, left_ref, vec_ref):
-    put_columns(cols_ref, left_ref, vec_ref)
-    affinity_product(left_ref, right_ref, vec_ref, aff_ref, send_ref)
-
-
-def rows_body(log_scale):
-    def body(rows_ref, away_right_ref, home_right_ref):
-        core = lax.axis_index("core")
-        put_rows(log_scale, rows_ref, 1 - core, away_right_ref)
-        put_rows(log_scale, rows_ref, core, home_right_ref)
+def away_body(log_scale):
+    def body(rows_ref, cols_ref, aff_ref, send_ref, left_ref, vec_ref, right_ref):
+        put_rows(log_scale, rows_ref, 1 - lax.axis_index("core"), right_ref)
+        put_columns(cols_ref, left_ref, vec_ref)
+        affinity_product(left_ref, right_ref, vec_ref, aff_ref, send_ref)
+
+    return body
+
+
+def home_body(log_scale):
+    def body(rows_ref, left_ref, vec_ref, aff_ref, send_ref, right_ref):
+        put_rows(log_scale, rows_ref, lax.axis_index("core"), right_ref)
+        affinity_product(left_ref, right_ref, vec_ref, aff_ref, send_ref)
 
     return body
 
@@ -394,22 +397,24 @@
     )
     cols = exchange(cols, "row")
     rows = lax.all_gather(rows, ("z", "core"))
-    away_right, home_right = call(rows_body(log_scale), (right_shape, right_shape), rows)
     aff_shape = pltpu.VMEM((row * group, lanes), BF16)
     send_shape = shape((half, 48, LANES), F32)
     away_aff, away_send, left, vec = call(
-        away_body,
+        away_body(log_scale),
         (
             aff_shape,
             send_shape,
             pltpu.VMEM((row * group, LANES), BF16),
             pltpu.VMEM((48, row * group), BF16),
         ),
-        away_right,
+        rows,
         cols,
+        scratch=(right_shape,),
     )
     other = swap(away_send)
-    home_aff, home_send = call(affinity_product, (aff_shape, send_shape), left, home_right, vec)
+    home_aff, home_send = call(
+        home_body(log_scale), (aff_shape, send_shape), rows, left, vec, scratch=(right_shape,)
+    )
     send = call(join_body, send_shape, home_send, other)
     spread, degree = call(
         scale_body, (shape((row, 40, LANES), F32), shape((16, LANES), F32)), exchange(send, "z")

time: 107 us -> 107 us (level)
    pallas_call x12 -> x11, Pallas kernels: 13.1 us -> 13 us  [call(): pl.pallas_call(body, out_shape=out_shape, scratch_shapes=scratch, compile...]
where the time goes in v11:
time: 107 us
  blocking collectives  82.4 us (77%)
  Pallas kernels  13 us (12%)
  starting transfers between devices  11.3 us (11%)
    all_to_all x5, blocking collectives, exchange(): return lax.all_to_all(x, axis, 0, 0, tiled=True)  60.8 us
    all_gather x1, blocking collectives, shards(): rows = lax.all_gather(rows, ('z', 'core'))  21.7 us
    pallas_call x11, Pallas kernels, call(): pl.pallas_call(body, out_shape=out_shape, scratch_shapes=scratch, compile...  13 us
    all_to_all x1, starting transfers between devices, exchange(): return lax.all_to_all(x, axis, 0, 0, tiled=True)  7.58 us
    ppermute x2, starting transfers between devices, swap(): return lax.ppermute(x, 'core', [(0, 1), (1, 0)])  3.7 us
  transfers between devices with their start and end apart: 3, of which 0 were waited for; matrix products, arithmetic and copies ran while one was open for 0% of the time, Pallas kernels for 4%

profile of v11, /device:TPU:1, one launch (start us, length us, event | category | flops | bytes accessed | tf_op | source)
XLA Modules:
  0.0 106.7 jit_solution(7953607446727022834)
XLA Ops:
  0.0 2.0 %shard_map.28 = (bf16[16,200,128]{2,1,0:T(8,128)(2,1)}, bf16[80,128]{1,0:T(8,128)(2,1)S(1)}) custom-call(bf16[64,160]{1,0:T(8,128)(2,1)} %bitcast.6, bf16[32,160]{1,0:T(8,128)(2,1)} %bitcast.7), custom_call_target="tpu_custom_call" | custom-call | tf_op jit(solution)/shard_map/pallas_call | solution.py:379
  2.0 7.6 %all-to-all-start = ((bf16[16,200,128]{2,1,0:T(8,128)(2,1)}), bf16[16,200,128]{2,1,0:T(8,128)(2,1)S(1)}, u32[]{:S(2)}, u32[]{:S(2)}) async-start(bf16[16,200,128]{2,1,0:T(8,128)(2,1)} %get-tuple-element.21), calls=%async_computation | async-start | bytes 1638400 | tf_op jit(solution)/shard_map/all_to_all | solution.py:373
  9.6 21.7 %all-gather = bf16[1280,128]{1,0:T(8,128)(2,1)S(1)} all-gather(bf16[80,128]{1,0:T(8,128)(2,1)S(1)} %get-tuple-element.20), channel_id=2, replica_groups=mesh['row'=16,'z'=8,'core'=2] {'z','core'}, dimensions={0}, use_global_device_ids=true | all-gather | bytes 348160 | tf_op jit(solution)/shard_map/all_gather | solution.py:399
  31.3 0.0 all-to-all-done.cols_ref
  31.3 3.0 %shard_map.29 = (bf16[2560,1280]{1,0:T(8,128)(2,1)S(1)}, f32[8,48,128]{2,1,0:T(8,128)S(1)}, bf16[2560,128]{1,0:T(8,128)(2,1)S(1)}, bf16[48,2560]{1,0:T(8,128)(2,1)S(1)}) custom-call(bf16[16,80,128]{2,1,0:T(8,128)(2,1)S(1)} %bitcast.4, bf16[16,200,128]{2,1,0:T(8,128)(2,1)S(1)} %all-to-all-done.cols_ref), custom_call_target="tpu_custom_call" | custom-call | tf_op jit(solution)/shard_map/pallas_call | solution.py:379
  34.3 0.2 collective-permute-start
  34.5 3.0 %shard_map.30 = (bf16[2560,1280]{1,0:T(8,128)(2,1)S(1)}, f32[8,48,128]{2,1,0:T(8,128)S(1)}) custom-call(bf16[16,80,128]{2,1,0:T(8,128)(2,1)S(1)} %bitcast.5, bf16[2560,128]{1,0:T(8,128)(2,1)S(1)} %get-tuple-element.22.left_ref, bf16[48,2560]{1,0:T(8,128)(2,1)S(1)} %get-tuple-element.23.vec_ref), custom_call_target="tpu_custom_call" | custom-call | tf_op jit(solution)/shard_map/pallas_call | solution.py:379
  37.5 0.0 collective-permute-done.other_ref
  37.6 12.6 %all_to_all.30.recv_ref = f32[8,48,128]{2,1,0:T(8,128)S(1)} all-to-all(f32[8,48,128]{2,1,0:T(8,128)S(1)} %shard_map.31), channel_id=1, replica_groups=mesh['row'=16,'z'=8,'core'=2] {'z'}, dimensions={0} | all-to-all | bytes 393216 | tf_op jit(solution)/shard_map/all_to_all | solution.py:373
  50.2 0.1 shard_map.32
  50.3 14.4 %all_to_all.31.spread_ref = f32[16,40,128]{2,1,0:T(8,128)S(1)} all-to-all(f32[16,40,128]{2,1,0:T(8,128)S(1)} %get-tuple-element.28), channel_id=1, replica_groups=mesh['row'=16,'z'=8,'core'=2] {'row'}, dimensions={0} | all-to-all | bytes 655360 | tf_op jit(solution)/shard_map/all_to_all | solution.py:373
  64.7 1.3 %shard_map.33 = (f32[8,48,128]{2,1,0:T(8,128)S(1)}, bf16[64,2560]{1,0:T(8,128)(2,1)S(1)}, f32[8,128]{1,0:T(8,128)S(1)}) custom-call(bf16[2560,1280]{1,0:T(8,128)(2,1)S(1)} %get-tuple-element.25.aff_ref, f32[16,40,128]{2,1,0:T(8,128)S(1)} %all_to_all.31.spread_ref), custom_call_target="tpu_custom_call" | custom-call | tf_op jit(solution)/shard_map/pallas_call | solution.py:379
  66.0 3.5 %collective-permute-start.1 = (f32[8,48,128]{2,1,0:T(8,128)S(1)}, f32[8,48,128]{2,1,0:T(8,128)S(1)}, u32[]{:S(2)}, u32[]{:S(2)}) collective-permute-start(f32[8,48,128]{2,1,0:T(8,128)S(1)} %get-tuple-element.31), channel_id=1, source_target_pairs={{0,1},{1,0},{2,3},{3,2},{4,5},{5,4},{6,7},{7,6},{8,9},{9,8},{10,11... | collective-permute-start | bytes 589832 | tf_op jit(solution)/shard_map/ppermute | solution.py:376
  69.4 1.2 %shard_map.34.mine_ref = f32[8,48,128]{2,1,0:T(8,128)S(1)} custom-call(bf16[2560,1280]{1,0:T(8,128)(2,1)S(1)} %get-tuple-element.24.aff_ref, bf16[64,2560]{1,0:T(8,128)(2,1)S(1)} %get-tuple-element.29.vec_ref, f32[8,128]{1,0:T(8,128)S(1)} %get-tuple-element.30.gram_ref), custom_call_target="tpu_custom_call" | custom-call | tf_op jit(solution)/shard_map/pallas_call | solution.py:379
  70.7 0.0 collective-permute-done.1.other_ref
  70.7 13.3 %all_to_all.32.recv_ref = f32[8,48,128]{2,1,0:T(8,128)S(1)} all-to-all(f32[8,48,128]{2,1,0:T(8,128)S(1)} %shard_map.35), channel_id=1, replica_groups=mesh['row'=16,'z'=8,'core'=2] {'z'}, dimensions={0} | all-to-all | bytes 393216 | tf_op jit(solution)/shard_map/all_to_all | solution.py:373
  84.0 0.9 shard_map.36
  84.9 10.7 %all_to_all.33.recv_ref = f32[16,8,128]{2,1,0:T(8,128)S(1)} all-to-all(f32[16,8,128]{2,1,0:T(8,128)S(1)} %get-tuple-element.33), channel_id=1, replica_groups=mesh['row'=16,'z'=8,'core'=2] {'z','core'}, dimensions={0} | all-to-all | bytes 131072 | tf_op jit(solution)/shard_map/all_to_all | solution.py:373
  95.7 9.7 %all_to_all.34.recv_ref = f32[16,8,128]{2,1,0:T(8,128)S(1)} all-to-all(f32[16,8,128]{2,1,0:T(8,128)S(1)} %shard_map.37), channel_id=1, replica_groups=mesh['row'=16,'z'=8,'core'=2] {'row'}, dimensions={0} | all-to-all | bytes 131072 | tf_op jit(solution)/shard_map/all_to_all | solution.py:373
  105.4 1.3 %shard_map.38 = f32[32,160]{1,0:T(8,128)} custom-call(f32[16,8,128]{2,1,0:T(8,128)S(1)} %all_to_all.34.recv_ref, f32[32,256]{1,0:T(8,128)S(1)} %get-tuple-element.34.scaled_ref), custom_call_target="tpu_custom_call" | custom-call | tf_op jit(solution)/shard_map/pallas_call | solution.py:379
  (3 shorter events, 0.1 us)
Async XLA Ops:
  2.0 29.3 %all-to-all-start = ((bf16[16,200,128]{2,1,0:T(8,128)(2,1)}), bf16[16,200,128]{2,1,0:T(8,128)(2,1)S(1)}, u32[]{:S(2)}, u32[]{:S(2)}) async-start(bf16[16,200,128]{2,1,0:T(8,128)(2,1)} %get-tuple-element.21), calls=%async_computation | async-start | bytes 1638400 | tf_op jit(solution)/shard_map/all_to_all | solution.py:373
  34.3 3.3 %collective-permute-start = (f32[8,48,128]{2,1,0:T(8,128)S(1)}, f32[8,48,128]{2,1,0:T(8,128)S(1)}, u32[]{:S(2)}, u32[]{:S(2)}) collective-permute-start(f32[8,48,128]{2,1,0:T(8,128)S(1)} %get-tuple-element.27), channel_id=1, source_target_pairs={{0,1},{1,0},{2,3},{3,2},{4,5},{5,4},{6,7},{7,6},{8,9},{9,8},{10,11... | collective-permute-start | bytes 589832 | tf_op jit(solution)/shard_map/ppermute | solution.py:376
  66.0 4.7 %collective-permute-start.1 = (f32[8,48,128]{2,1,0:T(8,128)S(1)}, f32[8,48,128]{2,1,0:T(8,128)S(1)}, u32[]{:S(2)}, u32[]{:S(2)}) collective-permute-start(f32[8,48,128]{2,1,0:T(8,128)S(1)} %get-tuple-element.31), channel_id=1, source_target_pairs={{0,1},{1,0},{2,3},{3,2},{4,5},{5,4},{6,7},{7,6},{8,9},{9,8},{10,11... | collective-permute-start | bytes 589832 | tf_op jit(solution)/shard_map/ppermute | solution.py:376

commit v12 on v10

--- a/solution.py
+++ b/solution.py
@@ -257,42 +257,45 @@
         put(count + m, unfold([spread_ref[4 * m + q, 32:40, :] for q in range(4)]))
 
 
-def second_product(aff_ref, vec_ref, send_ref):
-    main, rest = blocks_of(send_ref.shape[0])
-
-    def product(at, width):
-        out = jnp.dot(vec_ref[...], aff_ref[:, at : at + width], preferred_element_type=F32)
-        return out[0:32] + out[32:64]
-
-    out = product(*rest)
-    for m in range(rest[1] // LANES):
-        for q in range(4):
-            send_ref[4 * m + q, 32:40, :] = fold(out[:, m * LANES : (m + 1) * LANES], q)
-    for at, width in main:
-        out = product(at, width)
-        for k in range(width // LANES):
-            send_ref[at // LANES + k, 0:32, :] = out[:, k * LANES : (k + 1) * LANES]
-
-
-def put_gram(gram, send_ref):
-    for i in range(send_ref.shape[0]):
-        send_ref[i, 40:48, :] = gram
-
-
-def away_again_body(aff_ref, spread_ref, send_ref, vec_ref, gram_ref):
-    put_vectors(spread_ref, vec_ref)
+def second_product(vec_ref, aff_ref, at, width):
+    out = lax.dot_general(
+        vec_ref[...],
+        aff_ref[at : at + width, :],
+        (((1,), (1,)), ((), ())),
+        preferred_element_type=F32,
+    )
+    return out[0:32] + out[32:64]
+
+
+def gram_folded(vec_ref):
     vec = vec_ref[...]
     gram = lax.dot_general(vec, vec, (((1,), (1,)), ((), ())), preferred_element_type=F32)
     gram = gram[0:32] + gram[32:64]
-    gram = fold(widen(gram[:, 0:32] + gram[:, 32:64]))
-    gram_ref[...] = gram
-    second_product(aff_ref, vec_ref, send_ref)
-    put_gram(gram, send_ref)
-
-
-def home_again_body(aff_ref, vec_ref, gram_ref, send_ref):
-    second_product(aff_ref, vec_ref, send_ref)
-    put_gram(gram_ref[...], send_ref)
+    return fold(widen(gram[:, 0:32] + gram[:, 32:64]))
+
+
+def home_again_body(aff_ref, spread_ref, part_ref, gram_ref, vec_ref):
+    put_vectors(spread_ref, vec_ref)
+    gram_ref[...] = gram_folded(vec_ref)
+    for at in range(0, part_ref.shape[1], WIDTH):
+        part_ref[:, at : at + WIDTH] = second_product(vec_ref, aff_ref, at, WIDTH)
+
+
+def away_again_body(aff_ref, spread_ref, part_ref, gram_ref, send_ref, vec_ref):
+    put_vectors(spread_ref, vec_ref)
+    gram = gram_folded(vec_ref) + gram_ref[...]
+    main, rest = blocks_of(send_ref.shape[0])
+    for at, width in [rest] + main:
+        out = part_ref[:, at : at + width] + second_product(vec_ref, aff_ref, at, width)
+        for k in range(width // LANES):
+            tile = out[:, k * LANES : (k + 1) * LANES]
+            if at == rest[0]:
+                for q in range(4):
+                    send_ref[4 * k + q, 32:40, :] = fold(tile, q)
+            else:
+                send_ref[at // LANES + k, 0:32, :] = tile
+    for i in range(send_ref.shape[0]):
+        send_ref[i, 40:48, :] = gram
 
 
 def solved(gram, right):
@@ -374,7 +377,11 @@
 
     def call(body, out_shape, *args, scratch=(), **kwargs):
         return pl.pallas_call(
-            body, out_shape=out_shape, scratch_shapes=scratch, compiler_params=PARAMS, **kwargs
+            body,
+            out_shape=out_shape,
+            scratch_shapes=scratch,
+            compiler_params=PARAMS,
+            **kwargs,
         )(*args)
 
     hbm_space = pl.BlockSpec(memory_space=pltpu.HBM)
@@ -394,7 +401,9 @@
     )
     cols = exchange(cols, "row")
     rows = lax.all_gather(rows, ("z", "core"))
-    away_right, home_right = call(rows_body(log_scale), (right_shape, right_shape), rows)
+    away_right, home_right = call(
+        rows_body(log_scale), (right_shape, right_shape), rows
+    )
     aff_shape = pltpu.VMEM((row * group, lanes), BF16)
     send_shape = shape((half, 48, LANES), F32)
     away_aff, away_send, left, vec = call(
@@ -409,29 +418,45 @@
         cols,
     )
     other = swap(away_send)
-    home_aff, home_send = call(affinity_product, (aff_shape, send_shape), left, home_right, vec)
+    home_aff, home_send = call(
+        affinity_product, (aff_shape, send_shape), left, home_right, vec
+    )
     send = call(join_body, send_shape, home_send, other)
     spread, degree = call(
-        scale_body, (shape((row, 40, LANES), F32), shape((16, LANES), F32)), exchange(send, "z")
-    )
-    away_send, vec, gram = call(
+        scale_body,
+        (shape((half, 40, LANES), F32), shape((16, LANES), F32)),
+        exchange(send, "z"),
+    )
+    home_spread = exchange(spread, "z")
+    away_spread = swap(home_spread)
+    vec_shape = pltpu.VMEM((64, lanes), BF16)
+    part, gram = call(
+        home_again_body,
+        (pltpu.VMEM((32, row * group), F32), pltpu.VMEM((8, LANES), F32)),
+        home_aff,
+        home_spread,
+        scratch=(vec_shape,),
+    )
+    send = call(
         away_again_body,
-        (send_shape, pltpu.VMEM((64, row * group), BF16), pltpu.VMEM((8, LANES), F32)),
+        shape((row, 48, LANES), F32),
         away_aff,
-        exchange(spread, "row"),
-    )
-    other = swap(away_send)
-    home_send = call(home_again_body, send_shape, home_aff, vec, gram)
-    send = call(join_body, send_shape, home_send, other)
+        away_spread,
+        part,
+        gram,
+        scratch=(vec_shape,),
+    )
     scaled, gram = call(
         middle_body(total),
-        (shape((32, 2 * LANES), F32), shape((col, 8, LANES), F32)),
-        exchange(send, "z"),
+        (shape((32, 2 * LANES), F32), shape((row, 8, LANES), F32)),
+        exchange(send, "row"),
         degree,
     )
-    gram = exchange(gram, ("z", "core"))
-    gram = call(again_body, shape((row, 8, LANES), F32), gram)
-    out = call(last_body(total), shape((32, group), F32), exchange(gram, "row"), scaled)
+    gram = exchange(gram, "row")
+    gram = call(again_body, shape((col, 8, LANES), F32), gram)
+    out = call(
+        last_body(total), shape((32, group), F32), exchange(gram, ("z", "core")), scaled
+    )
     return out.T
 
 

time: 107 us -> 110 us (1.028)
  Pallas kernels: 13.1 us -> 15 us
  blocking collectives: 82.4 us -> 84.3 us
    pallas_call x12 -> x11, Pallas kernels: 13.1 us -> 15 us  [call(): pl.pallas_call(body, out_shape=out_shape, scratch_shapes=scratch, compile...]
    all_to_all x5, blocking collectives: 60.7 us -> 62.6 us  [exchange(): return lax.all_to_all(x, axis, 0, 0, tiled=True)]
  transfers between devices with their start and end apart: 3 -> 3, of which waited for: 0 -> 0; matrix products, arithmetic and copies ran while one was open for 0% -> 0% of each run, Pallas kernels for 4% -> 5%
where the time goes in v12:
time: 110 us
  blocking collectives  84.3 us (77%)
  Pallas kernels  15 us (14%)
  starting transfers between devices  10.6 us (10%)
    all_to_all x5, blocking collectives, exchange(): return lax.all_to_all(x, axis, 0, 0, tiled=True)  62.6 us
    all_gather x1, blocking collectives, shards(): rows = lax.all_gather(rows, ('z', 'core'))  21.7 us
    pallas_call x11, Pallas kernels, call(): pl.pallas_call(body, out_shape=out_shape, scratch_shapes=scratch, compile...  15 us
    all_to_all x1, starting transfers between devices, exchange(): return lax.all_to_all(x, axis, 0, 0, tiled=True)  7.58 us
    ppermute x2, starting transfers between devices, swap(): return lax.ppermute(x, 'core', [(0, 1), (1, 0)])  2.97 us
  transfers between devices with their start and end apart: 3, of which 0 were waited for; matrix products, arithmetic and copies ran while one was open for 0% of the time, Pallas kernels for 5%

profile of v12, /device:TPU:1, one launch (start us, length us, event | category | flops | bytes accessed | tf_op | source)
XLA Modules:
  0.0 109.9 jit_solution(18241639764947942259)
XLA Ops:
  0.0 2.0 %shard_map.28 = (bf16[16,200,128]{2,1,0:T(8,128)(2,1)}, bf16[80,128]{1,0:T(8,128)(2,1)S(1)}) custom-call(bf16[64,160]{1,0:T(8,128)(2,1)} %bitcast.5, bf16[32,160]{1,0:T(8,128)(2,1)} %bitcast.6), custom_call_target="tpu_custom_call" | custom-call | tf_op jit(solution)/shard_map/pallas_call | solution.py:379
  2.0 7.6 %all-to-all-start = ((bf16[16,200,128]{2,1,0:T(8,128)(2,1)}), bf16[16,200,128]{2,1,0:T(8,128)(2,1)S(1)}, u32[]{:S(2)}, u32[]{:S(2)}) async-start(bf16[16,200,128]{2,1,0:T(8,128)(2,1)} %get-tuple-element.23), calls=%async_computation | async-start | bytes 1638400 | tf_op jit(solution)/shard_map/all_to_all | solution.py:373
  9.6 21.7 %all-gather = bf16[1280,128]{1,0:T(8,128)(2,1)S(1)} all-gather(bf16[80,128]{1,0:T(8,128)(2,1)S(1)} %get-tuple-element.21), channel_id=2, replica_groups=mesh['row'=16,'z'=8,'core'=2] {'z','core'}, dimensions={0}, use_global_device_ids=true | all-gather | bytes 348160 | tf_op jit(solution)/shard_map/all_gather | solution.py:403
  31.3 0.3 shard_map.29
  31.6 0.0 all-to-all-done.cols_ref
  31.6 2.9 %shard_map.30 = (bf16[2560,1280]{1,0:T(8,128)(2,1)S(1)}, f32[8,48,128]{2,1,0:T(8,128)S(1)}, bf16[2560,128]{1,0:T(8,128)(2,1)S(1)}, bf16[48,2560]{1,0:T(8,128)(2,1)S(1)}) custom-call(bf16[256,1280]{1,0:T(8,128)(2,1)S(1)} %get-tuple-element.22.right_ref, bf16[16,200,128]{2,1,0:T(8,128)(2,1)S(1)} %all-to-all-done.cols_ref), custom_call_target="tpu_custom_call" | custom-call | tf_op jit(solution)/shard_map/pallas_call | solution.py:379
  34.6 0.3 collective-permute-start
  34.8 2.9 %shard_map.31 = (bf16[2560,1280]{1,0:T(8,128)(2,1)S(1)}, f32[8,48,128]{2,1,0:T(8,128)S(1)}) custom-call(bf16[2560,128]{1,0:T(8,128)(2,1)S(1)} %get-tuple-element.25.left_ref, bf16[256,1280]{1,0:T(8,128)(2,1)S(1)} %get-tuple-element.26.right_ref, bf16[48,2560]{1,0:T(8,128)(2,1)S(1)} %get-tuple-element.27.vec_ref), custom_call_target="tpu_custom_call" | custom-call | tf_op jit(solution)/shard_map/pallas_call | solution.py:379
  37.7 0.0 collective-permute-done.other_ref
  37.8 12.6 %all_to_all.30.recv_ref = f32[8,48,128]{2,1,0:T(8,128)S(1)} all-to-all(f32[8,48,128]{2,1,0:T(8,128)S(1)} %shard_map.32), channel_id=1, replica_groups=mesh['row'=16,'z'=8,'core'=2] {'z'}, dimensions={0} | all-to-all | bytes 393216 | tf_op jit(solution)/shard_map/all_to_all | solution.py:373
  50.4 0.1 shard_map.33
  50.5 11.1 %all_to_all.31.spread_ref = f32[8,40,128]{2,1,0:T(8,128)S(1)} all-to-all(f32[8,40,128]{2,1,0:T(8,128)S(1)} %get-tuple-element.30), channel_id=1, replica_groups=mesh['row'=16,'z'=8,'core'=2] {'z'}, dimensions={0} | all-to-all | bytes 327680 | tf_op jit(solution)/shard_map/all_to_all | solution.py:373
  61.5 2.7 %collective-permute-start.1 = (f32[8,40,128]{2,1,0:T(8,128)S(1)}, f32[8,40,128]{2,1,0:T(8,128)S(1)}, u32[]{:S(2)}, u32[]{:S(2)}) collective-permute-start(f32[8,40,128]{2,1,0:T(8,128)S(1)} %all_to_all.31.spread_ref), channel_id=1, source_target_pairs={{0,1},{1,0},{2,3},{3,2},{4,5},{5,4},{6,7},{7,6},{8,9},{9,8},{10,11... | collective-permute-start | bytes 491528 | tf_op jit(solution)/shard_map/ppermute | solution.py:376
  64.2 2.2 %shard_map.34 = (f32[32,2560]{1,0:T(8,128)S(1)}, f32[8,128]{1,0:T(8,128)S(1)}) custom-call(bf16[2560,1280]{1,0:T(8,128)(2,1)S(1)} %get-tuple-element.31.aff_ref, f32[8,40,128]{2,1,0:T(8,128)S(1)} %all_to_all.31.spread_ref), custom_call_target="tpu_custom_call" | custom-call | tf_op jit(solution)/shard_map/pallas_call | solution.py:379
  66.4 0.0 collective-permute-done.1.spread_ref
  66.4 2.2 %shard_map.35 = f32[16,48,128]{2,1,0:T(8,128)S(1)} custom-call(bf16[2560,1280]{1,0:T(8,128)(2,1)S(1)} %get-tuple-element.24.aff_ref, f32[8,40,128]{2,1,0:T(8,128)S(1)} %collective-permute-done.1.spread_ref, f32[32,2560]{1,0:T(8,128)S(1)} %get-tuple-element.32.part_ref, f32[8,128]{1,0:T(8,128)S(1)} %get-tuple-element.33.gram_ref), custom_call_target="tpu_custom_call" | custom-call | tf_op jit(solution)/shard_map/pallas_call | solution.py:379
  68.7 15.8 %all_to_all.32.recv_ref = f32[16,48,128]{2,1,0:T(8,128)S(1)} all-to-all(f32[16,48,128]{2,1,0:T(8,128)S(1)} %shard_map.35), channel_id=1, replica_groups=mesh['row'=16,'z'=8,'core'=2] {'row'}, dimensions={0} | all-to-all | bytes 786432 | tf_op jit(solution)/shard_map/all_to_all | solution.py:373
  84.4 0.9 shard_map.36
  85.3 10.4 %all_to_all.33.recv_ref = f32[16,8,128]{2,1,0:T(8,128)S(1)} all-to-all(f32[16,8,128]{2,1,0:T(8,128)S(1)} %get-tuple-element.35), channel_id=1, replica_groups=mesh['row'=16,'z'=8,'core'=2] {'row'}, dimensions={0} | all-to-all | bytes 131072 | tf_op jit(solution)/shard_map/all_to_all | solution.py:373
  95.7 12.8 %all_to_all.34.recv_ref = f32[16,8,128]{2,1,0:T(8,128)S(1)} all-to-all(f32[16,8,128]{2,1,0:T(8,128)S(1)} %shard_map.37), channel_id=1, replica_groups=mesh['row'=16,'z'=8,'core'=2] {'z','core'}, dimensions={0} | all-to-all | bytes 131072 | tf_op jit(solution)/shard_map/all_to_all | solution.py:373
  108.5 1.3 %shard_map.38 = f32[32,160]{1,0:T(8,128)} custom-call(f32[16,8,128]{2,1,0:T(8,128)S(1)} %all_to_all.34.recv_ref, f32[32,256]{1,0:T(8,128)S(1)} %get-tuple-element.36.scaled_ref), custom_call_target="tpu_custom_call" | custom-call | tf_op jit(solution)/shard_map/pallas_call | solution.py:379
  (2 shorter events, 0.0 us)
Async XLA Ops:
  2.0 29.6 %all-to-all-start = ((bf16[16,200,128]{2,1,0:T(8,128)(2,1)}), bf16[16,200,128]{2,1,0:T(8,128)(2,1)S(1)}, u32[]{:S(2)}, u32[]{:S(2)}) async-start(bf16[16,200,128]{2,1,0:T(8,128)(2,1)} %get-tuple-element.23), calls=%async_computation | async-start | bytes 1638400 | tf_op jit(solution)/shard_map/all_to_all | solution.py:373
  34.6 3.2 %collective-permute-start = (f32[8,48,128]{2,1,0:T(8,128)S(1)}, f32[8,48,128]{2,1,0:T(8,128)S(1)}, u32[]{:S(2)}, u32[]{:S(2)}) collective-permute-start(f32[8,48,128]{2,1,0:T(8,128)S(1)} %get-tuple-element.29), channel_id=1, source_target_pairs={{0,1},{1,0},{2,3},{3,2},{4,5},{5,4},{6,7},{7,6},{8,9},{9,8},{10,11... | collective-permute-start | bytes 589832 | tf_op jit(solution)/shard_map/ppermute | solution.py:376
  61.5 4.9 %collective-permute-start.1 = (f32[8,40,128]{2,1,0:T(8,128)S(1)}, f32[8,40,128]{2,1,0:T(8,128)S(1)}, u32[]{:S(2)}, u32[]{:S(2)}) collective-permute-start(f32[8,40,128]{2,1,0:T(8,128)S(1)} %all_to_all.31.spread_ref), channel_id=1, source_target_pairs={{0,1},{1,0},{2,3},{3,2},{4,5},{5,4},{6,7},{7,6},{8,9},{9,8},{10,11... | collective-permute-start | bytes 491528 | tf_op jit(solution)/shard_map/ppermute | solution.py:376
